TPU v7x, 512 devices: a whole 4x4x16 slice. The times are simulated.
512 devices in a mesh: ep: 64 (over x, z), rep: 8 (over y, core).
Axes of the slice: x: 4, y: 4, z: 16, core: 2. Of those that a mesh axis runs over, the one named last changes fastest.
Arguments:
- tokens: bfloat16 [65536, 1024], P(('ep', 'rep')), may hold values from -6 to 6
- expert_ids: int32 [65536, 6], P(('ep', 'rep')), may hold values from 0 to 63, all different within a row; in each aligned block of 128 rows (0 to 127, 128 to 255, ...) at most 13 rows name the same one
- gate_weights: float32 [65536, 6], P(('ep', 'rep')), may hold values from 0.1 to 0.5
- cotangent: bfloat16 [65536, 1024], P(('ep', 'rep')), may hold values from -6 to 6
- w_gate: bfloat16 [64, 1024, 704], P('ep', 'rep'), may hold values from -0.1875 to 0.1875
- w_up: bfloat16 [64, 1024, 704], P('ep', 'rep'), may hold values from -0.1875 to 0.1875
- w_down: bfloat16 [64, 704, 1024], P('ep', None, 'rep'), may hold values from -0.21875 to 0.21875
Outputs:
- mixed_out: bfloat16 [65536, 1024], P(('ep', 'rep'))
- grad_up: float32 [64, 1024, 704], P('ep', 'rep')
- grad_down: float32 [64, 704, 1024], P('ep', None, 'rep')
Inputs may be any that keep to these rules, and one draw needn't show every extreme that they name: `expert_ids`: each token names 6 different experts. Of the tokens of one device, at most 13 name any one expert, and in every draw some expert is named by exactly 13 of some device's tokens.
All inputs are finite; a program needn't handle non-finite values.
Results may differ from a plain program's by a relative error of at most 0.012.
Values may be sent and summed in bfloat16 or wider, within the bound.
No kernel may reach another device: no remote copies, remote signals or barrier semaphores. Data moves between devices by JAX's collectives and lax.ppermute only.
A program may use at most 128 MiB of HBM per device.

v0:
```python
import jax
import jax.numpy as jnp
from jax import lax
from jax.sharding import PartitionSpec as P


def sent_together(arrays, axis, dim, along):
    ends, at = ([], 0)
    for a in arrays[:-1]:
        at += a.shape[along]
        ends.append(at)
    both = jnp.concatenate(arrays, axis=along)
    return tuple(jnp.split(lax.all_gather(both, axis, axis=dim, tiled=True), ends, axis=along))


def local(tokens, expert_ids, gate_weights, cotangent, w_gate, w_up, w_down):
    ep_count = lax.axis_size("ep")
    tok_rows, feature_width = tokens.shape
    top_count = expert_ids.shape[1]
    slot_count = tok_rows * top_count // ep_count + 1
    pair_count = tok_rows * top_count
    flat_ids = expert_ids.reshape(pair_count)
    one_hot = (flat_ids[:, None] == jnp.arange(ep_count, dtype=jnp.int32)[None, :]).astype(
        jnp.int32
    )
    position = jnp.sum(one_hot * jnp.cumsum(one_hot, axis=0), axis=1) - 1
    target = flat_ids * slot_count + position
    owner_pair = (
        jnp.zeros((ep_count * slot_count,), jnp.int32)
        .at[target]
        .set(jnp.arange(pair_count, dtype=jnp.int32))
    )
    filled = jnp.zeros((ep_count * slot_count,), jnp.float32).at[target].set(1.0)
    source_row = owner_pair // top_count
    gate_flat = gate_weights.reshape(pair_count)
    send_rows = (tokens[source_row] * filled.astype(jnp.bfloat16)[:, None]).reshape(
        ep_count, slot_count, feature_width
    )
    pair_scale = gate_flat[owner_pair] * filled
    send_back = (pair_scale[:, None] * cotangent[source_row].astype(jnp.float32)).astype(
        jnp.bfloat16
    )
    send_back = send_back.reshape(ep_count, slot_count, feature_width)
    arrived, arrived_grad = (
        lax.all_to_all(send_rows, "ep", split_axis=0, concat_axis=0, tiled=True),
        lax.all_to_all(send_back, "ep", split_axis=0, concat_axis=0, tiled=True),
    )
    arrived_grad = arrived_grad.reshape(-1, feature_width)
    arrived = arrived.reshape(-1, feature_width)
    gate_shard = w_gate[0]
    up_shard = w_up[0]
    down_shard = w_down[0]
    pieces = sent_together((gate_shard, up_shard), "rep", 0, 1)
    columns = arrived
    gate_pre = jnp.dot(columns, pieces[0], preferred_element_type=jnp.float32)
    up_pre = jnp.dot(columns, pieces[1], preferred_element_type=jnp.float32)
    gate_silu = jax.nn.silu(gate_pre)
    hidden = (gate_silu * up_pre).astype(jnp.bfloat16)
    expert_out = jnp.dot(
        hidden,
        lax.all_gather(down_shard, "rep", axis=1, tiled=True),
        preferred_element_type=jnp.float32,
    ).astype(jnp.bfloat16)
    returned = lax.all_to_all(
        expert_out.reshape(ep_count, slot_count, feature_width),
        "ep",
        split_axis=0,
        concat_axis=0,
        tiled=True,
    )
    returned = returned.reshape(ep_count * slot_count, feature_width)
    weighted = returned[target].astype(jnp.float32) * gate_flat[:, None]
    mixed_out = jnp.sum(weighted.reshape(tok_rows, top_count, feature_width), axis=1).astype(
        jnp.bfloat16
    )
    columns = arrived_grad
    hidden_grad = lax.dot_general(
        columns,
        lax.all_gather(down_shard, "rep", axis=1, tiled=True),
        (((1,), (1,)), ((), ())),
        preferred_element_type=jnp.float32,
    )
    up_grad = (hidden_grad * gate_silu).astype(jnp.bfloat16)
    part_up = lax.dot_general(
        arrived, up_grad, (((0,), (0,)), ((), ())), preferred_element_type=jnp.float32
    )
    part_down = lax.dot_general(
        hidden, arrived_grad, (((0,), (0,)), ((), ())), preferred_element_type=jnp.float32
    )
    grad_up, grad_down = (
        lax.psum_scatter(
            part_up.astype(jnp.bfloat16), "rep", scatter_dimension=0, tiled=True
        ).astype(jnp.float32),
        lax.psum_scatter(
            part_down.astype(jnp.bfloat16), "rep", scatter_dimension=1, tiled=True
        ).astype(jnp.float32),
    )
    return (mixed_out, grad_up[None], grad_down[None])


def solution(mesh):
    in_specs = (
        P(("ep", "rep"), None),
        P(("ep", "rep"), None),
        P(("ep", "rep"), None),
        P(("ep", "rep"), None),
        P("ep", "rep", None),
        P("ep", "rep", None),
        P("ep", None, "rep"),
    )
    out_specs = (P(("ep", "rep"), None), P("ep", "rep", None), P("ep", None, "rep"))
    return jax.shard_map(local, mesh=mesh, in_specs=in_specs, out_specs=out_specs, check_vma=False)
```

profile of v0, /device:TPU:1, one launch (start us, length us, event | category | flops | bytes accessed | tf_op | source)
XLA Modules:
  0.0 377.3 jit_solution(16683254621904494720)
XLA Ops:
  7.2 0.7 broadcast_multiply_fusion.1
  7.9 0.8 copy.18
  9.1 0.1 mul.65
  9.2 0.8 copy.21
  10.2 0.5 copy-done.3
  10.7 1.8 reduce-window.6
  12.5 0.3 slice_reduce_fusion
  13.0 3.4 scatter_custom_fusion
  16.4 3.4 scatter_custom_fusion.1
  19.8 3.5 gather_fusion.2
  23.3 0.1 mul.67
  23.4 4.1 %gather_fusion = bf16[832,1024]{1,0:T(8,128)(2,1)} fusion(bf16[128,1024]{1,0:T(8,128)(2,1)S(1)} %copy-done, s32[1024]{0:T(1024)S(1)} %get-tuple-element.8), kind=kCustom, calls=%fused_computation | custom fusion | bytes 3411200 | tf_op jit(solution)/shard_map/gather | solution.py:36
  27.6 2.5 gather.15
  30.1 1.5 broadcast_multiply_fusion
  31.6 19.2 %all-to-all-start = ((bf16[64,13,1024]{2,1,0:T(8,128)(2,1)}), bf16[64,13,1024]{2,1,0:T(8,128)(2,1)S(1)}, u32[]{:S(2)}, u32[]{:S(2)}) async-start(bf16[64,13,1024]{2,1,0:T(8,128)(2,1)} %broadcast_multiply_fusion), calls=%async_computation | async-start | bytes 4194304 | tf_op jit(solution)/shard_map/all_to_all | solution.py:45
  50.9 0.8 pad_maximum_fusion
  51.8 4.2 %gather_fusion.3 = bf16[832,1024]{1,0:T(8,128)(2,1)} fusion(bf16[128,1024]{1,0:T(8,128)(2,1)S(1)} %copy-done.1, s32[1024]{0:T(1024)S(1)} %get-tuple-element.8), kind=kCustom, calls=%fused_computation.3 | custom fusion | bytes 3411200 | tf_op jit(solution)/shard_map/gather | solution.py:40
  56.0 3.7 reshape.107
  59.7 3.8 %multiply_convert_fusion = bf16[64,13,1024]{2,1,0:T(8,128)(2,1)} fusion(f32[64,13,1024]{2,1,0:T(8,128)} %reshape.107, f32[64,13]{1,0:T(8,128)S(1)} %mul.75), kind=kLoop, calls=%fused_computation.6 | loop fusion | flops 1703936 | bytes 5115136 | tf_op jit(solution)/shard_map/convert_element_type | solution.py:40
  63.5 82.0 %all-to-all-done = bf16[64,13,1024]{2,1,0:T(8,128)(2,1)S(1)} async-done(((bf16[64,13,1024]{2,1,0:T(8,128)(2,1)}), bf16[64,13,1024]{2,1,0:T(8,128)(2,1)S(1)}, u32[]{:S(2)}, u32[]{:S(2)}) %all-to-all-start) | async-done | bytes 1703968 | tf_op jit(solution)/shard_map/all_to_all | solution.py:45
  145.5 11.3 %all-to-all-start.2 = ((bf16[64,13,1024]{2,1,0:T(8,128)(2,1)}), bf16[64,13,1024]{2,1,0:T(8,128)(2,1)}, u32[]{:S(2)}, u32[]{:S(2)}) async-start(bf16[64,13,1024]{2,1,0:T(8,128)(2,1)} %multiply_convert_fusion), calls=%async_computation.2 | async-start | bytes 4194304 | tf_op jit(solution)/shard_map/all_to_all | solution.py:46
  156.8 0.2 all-gather.6.cloned.1.call-start
  157.0 0.5 all-gather.6.cloned.1.call-update
  157.5 1.5 reshape.101
  159.1 3.9 %divide_multiply_fusion = f32[832,704]{0,1:T(8,128)S(1)} fusion(bf16[832,1024]{1,0:T(8,128)(2,1)} %reshape.101, bf16[1024,1408]{0,1:T(8,128)(2,1)} %all-gather.4.cloned.1.call-done), kind=kOutput, calls=%fused_computation.10 | convolution fusion | flops 1201913856 | bytes 5488640 | tf_op jit(solution)/shard_map/dot_general | solution.py:55
  163.0 1.4 copy-done.8
  164.5 1.7 multiply_convert_fusion.2
  166.2 27.3 %all-gather.6.cloned.1.call-done = bf16[1,704,1024]{2,1,0:T(8,128)(2,1)} async-done(((bf16[1,704,128]{2,1,0:T(8,128)(2,1)}), bf16[1,704,1024]{2,1,0:T(8,128)(2,1)}) %all-gather.6.cloned.1.call-update) | async-done | bytes 1441808 | tf_op jit(solution)/shard_map/all_gather | solution.py:61
  193.5 4.1 %convolution_convert_fusion = bf16[832,1024]{1,0:T(8,128)(2,1)} fusion(bf16[832,704]{0,1:T(8,128)(2,1)S(1)} %multiply_convert_fusion.2, bf16[1,704,1024]{2,1,0:T(8,128)(2,1)} %all-gather.6.cloned.1.call-done), kind=kOutput, calls=%fused_computation.11 | convolution fusion | flops 1200422912 | bytes 4317184 | tf_op jit(solution)/shard_map/dot_general | solution.py:59
  197.6 3.6 reshape.102
  201.2 50.3 %all-to-all-done.2 = bf16[64,13,1024]{2,1,0:T(8,128)(2,1)} async-done(((bf16[64,13,1024]{2,1,0:T(8,128)(2,1)}), bf16[64,13,1024]{2,1,0:T(8,128)(2,1)}, u32[]{:S(2)}, u32[]{:S(2)}) %all-to-all-start.2) | async-done | bytes 1703968 | tf_op jit(solution)/shard_map/all_to_all | solution.py:46
  251.6 11.0 %all-to-all-start.1 = ((bf16[64,13,1024]{2,1,0:T(8,128)(2,1)}), bf16[64,13,1024]{2,1,0:T(8,128)(2,1)}, u32[]{:S(2)}, u32[]{:S(2)}) async-start(bf16[64,13,1024]{2,1,0:T(8,128)(2,1)} %reshape.102), calls=%async_computation.1 | async-start | bytes 4194304 | tf_op jit(solution)/shard_map/all_to_all | solution.py:64
  262.6 3.7 reshape.105
  266.4 3.5 convolution_convert_fusion.2
  269.9 1.6 copy.25
  271.5 0.3 reduce-scatter.7.cloned.1.call-start
  271.8 5.8 %convolution_convert_fusion.1 = bf16[1024,704]{0,1:T(8,128)(2,1)S(1)} fusion(bf16[832,1024]{1,0:T(8,128)(2,1)S(1)} %copy-done.2, f32[832,704]{0,1:T(8,128)} %copy-done.8, bf16[832,1024]{1,0:T(8,128)(2,1)} %reshape.105, bf16[1,704,1024]{2,1,0:T(8,128)(2,1)} %all-gather.6.cloned.1.call-done), kind=kOutput, calls=%fused_computation.12 | convolution fusion | flops 2401034240 | bytes 8634368 | tf_op jit(solution)/shard_map/dot_general | solution.py:84
  277.7 1.6 copy.23
  279.3 33.5 %reduce-scatter.9.cloned.1.call-done = bf16[128,704]{1,0:T(8,128)(2,1)} async-done(((bf16[1024,704]{1,0:T(8,128)(2,1)}), bf16[128,704]{1,0:T(8,128)(2,1)}) %reduce-scatter.9.cloned.1.call-update) | async-done | bytes 180240
  312.8 1.1 copy.26
  313.9 42.4 %reduce-scatter.7.cloned.1.call-done = bf16[128,704]{1,0:T(8,128)(2,1)} async-done(((bf16[1024,704]{1,0:T(8,128)(2,1)}), bf16[128,704]{1,0:T(8,128)(2,1)}) %reduce-scatter.7.cloned.1.call-update) | async-done | bytes 180240
  356.3 1.1 copy.24
  357.4 0.8 bitcast_convert_fusion.1
  358.1 0.8 bitcast_convert_fusion
  358.9 2.6 reshape.103
  361.5 2.8 gather_fusion.1
  364.3 2.2 reshape.106
  366.5 4.3 %multiply_reduce_fusion = bf16[128,1024]{1,0:T(8,128)(2,1)} fusion(f32[128,6,1024]{2,1,0:T(8,128)} %reshape.106, f32[128,6]{1,0:T(8,128)S(1)} %copy-done.4), kind=kLoop, calls=%fused_computation.7 | loop fusion | flops 1441792 | bytes 3410944 | tf_op jit(solution)/shard_map/reduce_sum | solution.py:73
  (41 shorter events, 1.0 us)
Async XLA Ops:
  7.2 16.3 %copy-start = (bf16[128,1024]{1,0:T(8,128)(2,1)S(1)}, bf16[128,1024]{1,0:T(8,128)(2,1)}, u32[]{:S(2)}) copy-start(bf16[128,1024]{1,0:T(8,128)(2,1)} %param.7) | copy-start | bytes 786436
  10.0 0.6 copy-start.3
  31.6 19.3 %copy-start.5 = (bf16[1,128,704]{1,2,0:T(8,128)(2,1)S(1)}, bf16[1,128,704]{1,2,0:T(8,128)(2,1)}, u32[]{:S(2)}) copy-start(bf16[1,128,704]{1,2,0:T(8,128)(2,1)} %param.12) | copy-start | bytes 540676
  31.6 19.3 %copy-start.6 = (bf16[1,128,704]{1,2,0:T(8,128)(2,1)S(1)}, bf16[1,128,704]{1,2,0:T(8,128)(2,1)}, u32[]{:S(2)}) copy-start(bf16[1,128,704]{1,2,0:T(8,128)(2,1)} %param.11) | copy-start | bytes 540676
  31.6 20.2 %copy-start.1 = (bf16[128,1024]{1,0:T(8,128)(2,1)S(1)}, bf16[128,1024]{1,0:T(8,128)(2,1)}, u32[]{:S(2)}) copy-start(bf16[128,1024]{1,0:T(8,128)(2,1)} %param.10) | copy-start | bytes 786436
  31.6 113.9 %all-to-all-start = ((bf16[64,13,1024]{2,1,0:T(8,128)(2,1)}), bf16[64,13,1024]{2,1,0:T(8,128)(2,1)S(1)}, u32[]{:S(2)}, u32[]{:S(2)}) async-start(bf16[64,13,1024]{2,1,0:T(8,128)(2,1)} %broadcast_multiply_fusion), calls=%async_computation | async-start | bytes 4194304 | tf_op jit(solution)/shard_map/all_to_all | solution.py:45
  50.9 108.2 %all-gather.4.cloned.1.call-start = ((), (), s32[]{:S(2)}) async-start(), calls=%async_computation.5 | async-start | bytes 3244032 | tf_op jit(solution)/shard_map/all_gather | solution.py:13
  145.5 106.0 %all-to-all-start.2 = ((bf16[64,13,1024]{2,1,0:T(8,128)(2,1)}), bf16[64,13,1024]{2,1,0:T(8,128)(2,1)}, u32[]{:S(2)}, u32[]{:S(2)}) async-start(bf16[64,13,1024]{2,1,0:T(8,128)(2,1)} %multiply_convert_fusion), calls=%async_computation.2 | async-start | bytes 4194304 | tf_op jit(solution)/shard_map/all_to_all | solution.py:46
  156.8 36.7 %all-gather.6.cloned.1.call-start = ((), (), s32[]{:S(2)}) async-start(), calls=%async_computation.6 | async-start | bytes 1622016 | tf_op jit(solution)/shard_map/all_gather | solution.py:61
  159.1 5.4 %copy-start.2 = (bf16[832,1024]{1,0:T(8,128)(2,1)S(1)}, bf16[832,1024]{1,0:T(8,128)(2,1)}, u32[]{:S(2)}) copy-start(bf16[832,1024]{1,0:T(8,128)(2,1)} %reshape.101) | copy-start | bytes 5111812
  159.1 5.4 %copy-start.7 = (bf16[1024,1408]{0,1:T(8,128)(2,1)S(1)}, bf16[1024,1408]{0,1:T(8,128)(2,1)}, u32[]{:S(2)}) copy-start(bf16[1024,1408]{0,1:T(8,128)(2,1)} %all-gather.4.cloned.1.call-done) | copy-start | bytes 8650756
  163.0 1.4 copy-start.8
  166.2 31.4 %copy-start.9 = (bf16[832,704]{0,1:T(8,128)(2,1)}, bf16[832,704]{0,1:T(8,128)(2,1)S(1)}, u32[]{:S(2)}) copy-start(bf16[832,704]{0,1:T(8,128)(2,1)S(1)} %multiply_convert_fusion.2) | copy-start | bytes 3514372
  251.6 107.3 %all-to-all-start.1 = ((bf16[64,13,1024]{2,1,0:T(8,128)(2,1)}), bf16[64,13,1024]{2,1,0:T(8,128)(2,1)}, u32[]{:S(2)}, u32[]{:S(2)}) async-start(bf16[64,13,1024]{2,1,0:T(8,128)(2,1)} %reshape.102), calls=%async_computation.1 | async-start | bytes 4194304 | tf_op jit(solution)/shard_map/all_to_all | solution.py:64
  262.6 50.2 %reduce-scatter.9.cloned.1.call-start = ((), (), s32[]{:S(2)}) async-start(), calls=%async_computation.8 | async-start | bytes 1769472
  271.5 84.7 %reduce-scatter.7.cloned.1.call-start = ((), (), s32[]{:S(2)}) async-start(), calls=%async_computation.7 | async-start | bytes 1769472
  364.3 2.2 copy-start.4
Sparse Core Ops, SparseCore 0:
  54.4 39.5 all-gather.3
  159.7 33.7 all-gather.5
  271.6 41.0 reduce-scatter.8
  315.5 40.7 reduce-scatter.6
where the time goes:
time: 379 us; the launch traced here: 377 us
  waiting for transfers between devices  236 us (62%)
  local copies, waits for them, and re-layouts  51.3 us (14%)
  starting transfers between devices  42.1 us (11%)
  matrix products  19.1 us (5%)
  other arithmetic  14.7 us (4%)
  between operations  14 us (4%)
    all_to_all x1, waiting for transfers between devices, local(): lax.all_to_all(send_rows, 'ep', split_axis=0, concat_axis=0, tiled=True)  82 us
    unnamed x6, waiting for transfers between devices  76.5 us
    all_to_all x1, waiting for transfers between devices, local(): lax.all_to_all(send_back, 'ep', split_axis=0, concat_axis=0, tiled=True)  50.3 us
    all_gather x1, waiting for transfers between devices, local(): lax.all_gather(down_shard, 'rep', axis=1, tiled=True)  27.3 us
    all_to_all x1, starting transfers between devices, local(): lax.all_to_all(send_rows, 'ep', split_axis=0, concat_axis=0, tiled=True)  19.2 us
    all_to_all x1, starting transfers between devices, local(): lax.all_to_all(send_back, 'ep', split_axis=0, concat_axis=0, tiled=True)  11.3 us
    all_to_all x1, starting transfers between devices, local(): lax.all_to_all(expert_out.reshape(ep_count, slot_count, feature_width), '...  11 us
    unnamed x26, local copies, waits for them, and re-layouts  8.96 us
  transfers between devices with their start and end apart: 7, of which 5 were waited for; matrix products, arithmetic and copies ran while one was open for 13% of the time, Pallas kernels for 0%

commit v1 on v0

v1 whole, which is shorter than its diff:
```python
import functools

import jax
import jax.numpy as jnp
from jax import lax
from jax.experimental import pallas as pl
from jax.experimental.pallas import tpu as pltpu
from jax.sharding import PartitionSpec as P

NX, NZ = 4, 16
CAP = 13
TOP = 6
TOK = 128
EXTRA = 8
NEAR = (0, 1, 2, 3, 4, -1, -2, -3)
FAR = (5, 6, 7, -4, -5, -6, -7, 8)
COUNT = len(NEAR)
ROWS = CAP * COUNT
PAD = 128
ZG = [[x * NZ + z for z in range(NZ)] for x in range(NX)]
XG = [[x * NZ + z for x in range(NX)] for z in range(NZ)]


def zperm(d):
    return [(x * NZ + z, x * NZ + (z + d) % NZ) for x in range(NX) for z in range(NZ)]


def pack_body(tokens_ref, ids_ref, gates_ref, out_ref):
    out_ref[:TOK, :] = tokens_ref[...]
    gates = gates_ref[...]
    high = gates.astype(jnp.bfloat16).astype(jnp.float32)
    mid = (gates - high).astype(jnp.bfloat16).astype(jnp.float32)
    low = gates - high - mid
    ids = ids_ref[...].astype(jnp.float32)
    blank = jnp.zeros((EXTRA - 4, TOK), jnp.float32)
    for k in range(TOP):
        at = slice(k, k + 1)
        rows = jnp.concatenate([ids[at], high[at], mid[at], low[at], blank], axis=0)
        out_ref[TOK:, k * TOK : (k + 1) * TOK] = rows.astype(jnp.bfloat16)
    rest = out_ref.shape[1] - TOP * TOK
    out_ref[TOK:, TOP * TOK :] = jnp.zeros((EXTRA, rest), jnp.bfloat16)


def pack(tokens, ids, gates):
    return pl.pallas_call(
        pack_body,
        out_shape=jax.ShapeDtypeStruct((TOK + EXTRA, tokens.shape[1]), jnp.bfloat16),
        cost_estimate=pl.CostEstimate(flops=0, bytes_accessed=4 * TOK * tokens.shape[1], transcendentals=0),
        name="pack",
    )(tokens, ids.T, gates.T)


def ring(a):
    held = {0: (a,)}
    fwd = back = a
    half = NZ // 2
    for i in range(1, half):
        fwd = lax.ppermute(fwd, "ep", zperm(1))
        back = lax.ppermute(back, "ep", zperm(-1))
        held[i], held[-i] = (fwd,), (back,)
    mid = TOK // 2
    held[half] = (
        lax.ppermute(fwd[:mid], "ep", zperm(1)),
        lax.ppermute(back[mid:], "ep", zperm(-1)),
    )
    return held


def pick_rows(code, gate, all_rows, out_ref, weighted):
    slot = lax.broadcasted_iota(jnp.int32, (ROWS, all_rows.shape[0]), 0)
    for j in range(NX):
        hit = slot == code[j : j + 1, :]
        got = jnp.dot(
            jnp.where(hit, 1.0, 0.0).astype(jnp.bfloat16), all_rows, preferred_element_type=jnp.float32
        )
        if weighted:
            got = got * jnp.sum(jnp.where(hit, gate[j : j + 1, :], 0.0), axis=1, keepdims=True)
        out_ref[j] = got.astype(jnp.bfloat16)


def pick_body(place_ref, *refs, spots):
    chunks, (out_ref, code_ref, gate_ref, code_t_ref, gate_t_ref, stage, extra) = refs[:-7], refs[-7:]
    for c, (n, row) in zip(chunks, spots):
        end = row + c.shape[0]
        if end <= TOK:
            stage[n * TOK + row : n * TOK + end, :] = c[...]
        else:
            stage[n * TOK + row : (n + 1) * TOK, :] = c[: TOK - row, :]
            extra[n * EXTRA : (n + 1) * EXTRA, :] = c[TOK - row :, :].astype(jnp.float32)
    mine = place_ref[0] + NZ * lax.broadcasted_iota(jnp.int32, (NX, TOK), 0)
    mine = mine.astype(jnp.float32)
    hits, weights = [], []
    for n in range(COUNT):
        hit = jnp.zeros((NX, TOK), jnp.float32)
        weight = jnp.zeros((NX, TOK), jnp.float32)
        for k in range(TOP):
            part = extra[n * EXTRA : n * EXTRA + 4, k * TOK : (k + 1) * TOK]
            same = part[0:1] == mine
            hit = jnp.where(same, 1.0, hit)
            weight = jnp.where(same, part[1:2] + part[2:3] + part[3:4], weight)
        hits.append(hit)
        weights.append(weight)
    hits, weights = jnp.concatenate(hits, axis=0), jnp.concatenate(weights, axis=0)
    shape = (TOK, TOK)
    earlier = lax.broadcasted_iota(jnp.int32, shape, 0) < lax.broadcasted_iota(jnp.int32, shape, 1)
    position = jnp.dot(
        hits.astype(jnp.bfloat16),
        jnp.where(earlier, 1.0, 0.0).astype(jnp.bfloat16),
        preferred_element_type=jnp.float32,
    )
    first = CAP * (lax.broadcasted_iota(jnp.int32, (NX * COUNT, TOK), 0) // NX)
    codes = jnp.where(hits > 0, position.astype(jnp.int32) + first, -1)
    codes_f = codes.astype(jnp.float32)
    fill = jnp.zeros((TOK - NX * COUNT, TOK), jnp.float32)
    code_t = jnp.concatenate([codes_f, fill], axis=0).T
    gate_t = jnp.concatenate([weights, fill], axis=0).T
    for n in range(COUNT):
        at = slice(n * NX, (n + 1) * NX)
        code_ref[:, n * TOK : (n + 1) * TOK] = codes[at]
        gate_ref[:, n * TOK : (n + 1) * TOK] = weights[at]
        code_t_ref[n] = code_t[:, at]
        gate_t_ref[n] = gate_t[:, at]
    pick_rows(code_ref[...], None, stage[...], out_ref, False)


def pick_cost(rows, width):
    return pl.CostEstimate(
        flops=2 * NX * ROWS * rows * width, bytes_accessed=2 * (rows + NX * ROWS) * width, transcendentals=0
    )


def pick(place, groups):
    pieces, spots = [], []
    for n, group in enumerate(groups):
        row = 0
        for piece in group:
            pieces.append(piece)
            spots.append((n, row))
            row += piece.shape[0]
    width = pieces[0].shape[1]
    rows = COUNT * TOK
    shapes = [((NX, ROWS, width), jnp.bfloat16), ((NX, rows), jnp.int32), ((NX, rows), jnp.float32)]
    shapes += [((COUNT, TOK, NX), jnp.float32)] * 2
    return pl.pallas_call(
        functools.partial(pick_body, spots=spots),
        out_shape=[jax.ShapeDtypeStruct(s, t) for s, t in shapes],
        in_specs=[pl.BlockSpec(memory_space=pltpu.SMEM)] + [pl.BlockSpec(memory_space=pltpu.VMEM)] * len(pieces),
        scratch_shapes=[pltpu.VMEM((rows, width), jnp.bfloat16), pltpu.VMEM((COUNT * EXTRA, width), jnp.float32)],
        cost_estimate=pick_cost(rows, width),
        name="pick",
    )(place, *pieces)


def pick_from_body(source_ref, code_ref, gate_ref, *refs):
    chunks, out_ref, stage = refs[:-2], refs[-2], refs[-1]
    for n, c in enumerate(chunks):
        stage[n * TOK : (n + 1) * TOK, :] = c[...]
    pick_rows(code_ref[...], gate_ref[...], stage[...], out_ref, True)


def pick_from(source, code, gate, gathered):
    width = gathered.shape[1]
    rows = COUNT * TOK
    small = pl.BlockSpec((NX, rows), lambda i, source: (0, 0))
    chunk = [pl.BlockSpec((TOK, width), lambda i, source, n=n: (source[n], 0)) for n in range(COUNT)]
    return pl.pallas_call(
        pick_from_body,
        out_shape=jax.ShapeDtypeStruct((NX, ROWS, width), jnp.bfloat16),
        grid_spec=pltpu.PrefetchScalarGridSpec(
            num_scalar_prefetch=1,
            grid=(1,),
            in_specs=[small, small] + chunk,
            out_specs=pl.BlockSpec((NX, ROWS, width), lambda i, source: (0, 0, 0)),
            scratch_shapes=[pltpu.VMEM((rows, width), jnp.bfloat16)],
        ),
        cost_estimate=pick_cost(rows, width),
        name="pick_weighted",
    )(source, code, gate, *([gathered] * COUNT))


def mix_body(dest_ref, code_ref, gate_ref, rows_ref, *refs):
    out_ref, stage = refs[-2], refs[-1]
    width = out_ref.shape[1]

    @pl.when(pl.program_id(0) == 0)
    def _():
        for j in range(NX):
            stage[j * PAD : j * PAD + ROWS, :] = rows_ref[j]
            stage[j * PAD + ROWS : (j + 1) * PAD, :] = jnp.zeros((PAD - ROWS, width), jnp.bfloat16)

    slot = lax.broadcasted_iota(jnp.int32, (TOK, PAD), 1).astype(jnp.float32)
    code, gate = code_ref[0], gate_ref[0]
    full = jnp.concatenate(
        [jnp.where(slot == code[:, j : j + 1], gate[:, j : j + 1], 0.0) for j in range(NX)], axis=1
    )
    high = full.astype(jnp.bfloat16)
    low = (full - high.astype(jnp.float32)).astype(jnp.bfloat16)
    both = jnp.dot(jnp.concatenate([high, low], axis=0), stage[...], preferred_element_type=jnp.float32)
    out_ref[...] = (both[:TOK] + both[TOK:]).astype(jnp.bfloat16)


def mix(dest, code_t, gate_t, rows, before):
    width = rows.shape[2]
    small = pl.BlockSpec((1, TOK, NX), lambda i, dest: (i, 0, 0))
    chained = before is not None
    return pl.pallas_call(
        mix_body,
        out_shape=jax.ShapeDtypeStruct((NZ * TOK, width), jnp.bfloat16),
        grid_spec=pltpu.PrefetchScalarGridSpec(
            num_scalar_prefetch=1,
            grid=(COUNT,),
            in_specs=[small, small, pl.BlockSpec((NX, ROWS, width), lambda i, dest: (0, 0, 0))]
            + ([pl.BlockSpec(memory_space=pl.ANY)] if chained else []),
            out_specs=pl.BlockSpec((TOK, width), lambda i, dest: (dest[i], 0)),
            scratch_shapes=[pltpu.VMEM((NX * PAD, width), jnp.bfloat16)],
        ),
        input_output_aliases={4: 0} if chained else {},
        cost_estimate=pl.CostEstimate(
            flops=4 * NX * PAD * COUNT * TOK * width,
            bytes_accessed=2 * (NX * ROWS + COUNT * TOK) * width,
            transcendentals=0,
        ),
        name="mix",
    )(dest, code_t, gate_t, rows, *((before,) if chained else ()))


def across_x(blocks):
    return lax.all_to_all(blocks, "ep", split_axis=0, concat_axis=0, axis_index_groups=XG, tiled=True)


def local(tokens, expert_ids, gate_weights, cotangent, w_gate, w_up, w_down):
    width = tokens.shape[1]
    z = lax.axis_index("ep") % NZ
    n_rep = lax.axis_size("rep")
    all_cot = lax.all_gather(cotangent, "ep", axis_index_groups=ZG, axis=0, tiled=True)
    held = ring(pack(tokens, expert_ids, gate_weights))
    source = (z - jnp.array(NEAR + FAR, jnp.int32)) % NZ
    place = z.reshape(1)

    hidden_width = w_gate.shape[2]
    share = w_gate.shape[1]
    shards = jnp.concatenate([w_gate[0].T, w_up[0].T, w_down[0]], axis=1)
    shards, _, _ = lax.optimization_barrier((shards, held[1][0], held[-1][0]))
    shards = jnp.broadcast_to(shards[None], (n_rep,) + shards.shape)
    shards = lax.all_to_all(shards, "rep", split_axis=0, concat_axis=0, tiled=True)
    full_gate, full_up, full_down = (
        shards[:, :, n * share : (n + 1) * share].transpose(1, 0, 2).reshape(hidden_width, width)
        for n in range(3)
    )
    last = (((1,), (1,)), ((), ()))
    first = (((0,), (0,)), ((), ()))

    mixed = None
    kept = []
    for b, group in enumerate((NEAR, FAR)):
        sources = source[b * COUNT : (b + 1) * COUNT]
        rows, code, gate, code_t, gate_t = pick(place, [held[d] for d in group])
        rows = across_x(rows).reshape(NX * ROWS, width)
        gate_pre = lax.dot_general(rows, full_gate, last, preferred_element_type=jnp.float32)
        up_pre = lax.dot_general(rows, full_up, last, preferred_element_type=jnp.float32)
        silu = jax.nn.silu(gate_pre)
        hidden = (silu * up_pre).astype(jnp.bfloat16)
        out = jnp.dot(hidden, full_down, preferred_element_type=jnp.float32).astype(jnp.bfloat16)
        mixed = mix(sources, code_t, gate_t, across_x(out.reshape(NX, ROWS, width)), mixed)
        kept.append((sources, code, gate, rows, silu, hidden))
    mixed_out = lax.psum_scatter(mixed, "ep", axis_index_groups=ZG, scatter_dimension=0, tiled=True)

    part_up = part_down = None
    for sources, code, gate, rows, silu, hidden in kept:
        grad_rows = across_x(pick_from(sources, code, gate, all_cot)).reshape(NX * ROWS, width)
        hidden_grad = lax.dot_general(grad_rows, full_down, last, preferred_element_type=jnp.float32)
        up_grad = (hidden_grad * silu).astype(jnp.bfloat16)
        down = lax.dot_general(grad_rows, hidden, first, preferred_element_type=jnp.float32)
        up = lax.dot_general(rows, up_grad, first, preferred_element_type=jnp.float32)
        part_down = down if part_down is None else part_down + down
        part_up = up if part_up is None else part_up + up

    def summed(part):
        part = part.astype(jnp.bfloat16).reshape(n_rep, width // n_rep, hidden_width)
        part = lax.all_to_all(part, "rep", split_axis=0, concat_axis=0, tiled=True)
        return jnp.sum(part.astype(jnp.float32), axis=0)

    grad_down = summed(part_down).T
    grad_up = summed(part_up)
    return mixed_out, grad_up[None], grad_down[None]


def solution(mesh):
    in_specs = (
        P(("ep", "rep"), None),
        P(("ep", "rep"), None),
        P(("ep", "rep"), None),
        P(("ep", "rep"), None),
        P("ep", "rep", None),
        P("ep", "rep", None),
        P("ep", None, "rep"),
    )
    out_specs = (P(("ep", "rep"), None), P("ep", "rep", None), P("ep", None, "rep"))
    return jax.shard_map(local, mesh=mesh, in_specs=in_specs, out_specs=out_specs, check_vma=False)
```

time: 379 us -> 304 us (0.80)
  waiting for transfers between devices: 236 us -> 93.5 us
  starting transfers between devices: 42.1 us -> 113 us
  local copies, waits for them, and re-layouts: 51.3 us -> 13.4 us
  Pallas kernels: 0 us -> 35.7 us
  other arithmetic: 14.7 us -> 4.44 us
  matrix products: 19.1 us -> 27.3 us
    all_to_all x3 -> x9, waiting for transfers between devices: 132 us -> 44.2 us  [the longest x2 33 us: summed(): part = lax.all_to_all(part, 'rep', split_axis=0, concat_axis=0, tiled=True)]
    unnamed x6 -> x2, waiting for transfers between devices: 76.5 us -> 0.7 us
    ppermute x0 -> x16, starting transfers between devices: none -> 61.2 us  [the longest x7 39.7 us: ring(): back = lax.ppermute(back, 'ep', zperm(-1))]
    ppermute x0 -> x16, waiting for transfers between devices: none -> 48.6 us  [the longest x7 37.5 us: ring(): back = lax.ppermute(back, 'ep', zperm(-1))]
    pallas_call x0 -> x7, Pallas kernels: none -> 35.7 us  [the longest x2 17.1 us: mix(): pl.pallas_call(mix_body, out_shape=jax.ShapeDtypeStruct((NZ * TOK, width)...]
    all_gather x2 -> x1, waiting for transfers between devices: 27.3 us -> 0.02 us  [local(): lax.all_gather(cotangent, 'ep', axis_index_groups=ZG, axis=0, tiled=True)]
    gather x5 -> x0, local copies, waits for them, and re-layouts: 17.1 us -> none  [the longest x2 6.62 us: local(): tokens[source_row] * filled.astype(jnp.bfloat16)[:, None]]
    all_to_all x3 -> x9, starting transfers between devices: 41.5 us -> 51.2 us  [the longest x6 23.6 us: across_x(): lax.all_to_all(blocks, 'ep', split_axis=0, concat_axis=0, axis_index_grou...]
  transfers between devices with their start and end apart: 7 -> 27, of which waited for: 5 -> 15; matrix products, arithmetic and copies ran while one was open for 13% -> 14% of each run, Pallas kernels for 0% -> 12%
where the time goes in v1:
time: 304 us; the launch traced here: 302 us
  starting transfers between devices  113 us (37%)
  waiting for transfers between devices  93.5 us (31%)
  Pallas kernels  35.7 us (12%)
  matrix products  27.3 us (9%)
  between operations  14.6 us (5%)
  local copies, waits for them, and re-layouts  13.4 us (4%)
  other arithmetic  4.44 us (1%)
    ppermute x7, starting transfers between devices, ring(): back = lax.ppermute(back, 'ep', zperm(-1))  39.7 us
    ppermute x7, waiting for transfers between devices, ring(): back = lax.ppermute(back, 'ep', zperm(-1))  37.5 us
    all_to_all x2, waiting for transfers between devices, summed(): part = lax.all_to_all(part, 'rep', split_axis=0, concat_axis=0, tiled=True)  33 us
    all_to_all x6, starting transfers between devices, across_x(): lax.all_to_all(blocks, 'ep', split_axis=0, concat_axis=0, axis_index_grou...  23.6 us
    all_to_all x2, starting transfers between devices, summed(): part = lax.all_to_all(part, 'rep', split_axis=0, concat_axis=0, tiled=True)  21.3 us
    pallas_call x2, Pallas kernels, mix(): pl.pallas_call(mix_body, out_shape=jax.ShapeDtypeStruct((NZ * TOK, width)...  17.1 us
    ppermute x7, starting transfers between devices, ring(): fwd = lax.ppermute(fwd, 'ep', zperm(1))  15.1 us
    all_to_all x6, waiting for transfers between devices, across_x(): lax.all_to_all(blocks, 'ep', split_axis=0, concat_axis=0, axis_index_grou...  11.2 us
  transfers between devices with their start and end apart: 27, of which 15 were waited for; matrix products, arithmetic and copies ran while one was open for 14% of the time, Pallas kernels for 12%

profile of v1, /device:TPU:1, one launch (start us, length us, event | category | flops | bytes accessed | tf_op | source)
XLA Modules:
  0.0 301.6 jit_solution(894860247858918290)
XLA Ops:
  9.6 11.9 %collective-permute-start.7 = (bf16[136,1024]{1,0:T(8,128)(2,1)}, bf16[136,1024]{1,0:T(8,128)(2,1)S(1)}, u32[]{:S(2)}, u32[]{:S(2)}) collective-permute-start(bf16[136,1024]{1,0:T(8,128)(2,1)} %pack.1.refs_0_), channel_id=1, source_target_pairs={{0,120},{8,0},{16,8},{24,16},{32,24},{40,32},{48,40},{56,48},{64,5... | collective-permute-start | bytes 835592 | tf_op jit(solution)/shard_map/ppermute | solution.py:59
  24.6 2.5 collective-permute-done.7.refs_5_
  27.2 4.9 %collective-permute-done.refs_1_ = bf16[136,1024]{1,0:T(8,128)(2,1)S(1)} collective-permute-done((bf16[136,1024]{1,0:T(8,128)(2,1)}, bf16[136,1024]{1,0:T(8,128)(2,1)S(1)}, u32[]{:S(2)}, u32[]{:S(2)}) %collective-permute-start) | collective-permute-done | bytes 278560 | tf_op jit(solution)/shard_map/ppermute | solution.py:58
  32.1 2.3 broadcast_in_dim.12
  34.5 6.3 %all-to-all-start.1 = ((bf16[8,704,384]{2,1,0:T(8,128)(2,1)}), bf16[8,704,384]{2,1,0:T(8,128)(2,1)}, u32[]{:S(2)}, u32[]{:S(2)}) async-start(bf16[8,704,384]{2,1,0:T(8,128)(2,1)} %broadcast_in_dim.12), calls=%async_computation.1 | async-start | bytes 8650752 | tf_op jit(solution)/shard_map/all_to_all | solution.py:245
  42.7 3.4 %collective-permute-start.1 = (bf16[136,1024]{1,0:T(8,128)(2,1)S(1)}, bf16[136,1024]{1,0:T(8,128)(2,1)S(1)}, u32[]{:S(2)}, u32[]{:S(2)}) collective-permute-start(bf16[136,1024]{1,0:T(8,128)(2,1)S(1)} %collective-permute-done.refs_1_), channel_id=1, source_target_pairs={{0,8},{8,16},{16,24},{24,32},{32,40},{40,48},{48,56},{56,64},{64,7... | collective-permute-start | bytes 835592 | tf_op jit(solution)/shard_map/ppermute | solution.py:58
  46.0 9.6 %collective-permute-done.8.refs_6_ = bf16[136,1024]{1,0:T(8,128)(2,1)S(1)} collective-permute-done((bf16[136,1024]{1,0:T(8,128)(2,1)S(1)}, bf16[136,1024]{1,0:T(8,128)(2,1)S(1)}, u32[]{:S(2)}, u32[]{:S(2)}) %collective-permute-start.8) | collective-permute-done | bytes 278560 | tf_op jit(solution)/shard_map/ppermute | solution.py:59
  55.6 4.6 %collective-permute-start.9 = (bf16[136,1024]{1,0:T(8,128)(2,1)S(1)}, bf16[136,1024]{1,0:T(8,128)(2,1)S(1)}, u32[]{:S(2)}, u32[]{:S(2)}) collective-permute-start(bf16[136,1024]{1,0:T(8,128)(2,1)S(1)} %collective-permute-done.8.refs_6_), channel_id=1, source_target_pairs={{0,120},{8,0},{16,8},{24,16},{32,24},{40,32},{48,40},{56,48},{64,5... | collective-permute-start | bytes 835592 | tf_op jit(solution)/shard_map/ppermute | solution.py:59
  60.2 2.1 collective-permute-start.2
  62.3 9.6 %collective-permute-done.9.refs_7_ = bf16[136,1024]{1,0:T(8,128)(2,1)S(1)} collective-permute-done((bf16[136,1024]{1,0:T(8,128)(2,1)S(1)}, bf16[136,1024]{1,0:T(8,128)(2,1)S(1)}, u32[]{:S(2)}, u32[]{:S(2)}) %collective-permute-start.9) | collective-permute-done | bytes 278560 | tf_op jit(solution)/shard_map/ppermute | solution.py:59
  72.0 5.4 %collective-permute-start.10 = (bf16[136,1024]{1,0:T(8,128)(2,1)S(1)}, bf16[136,1024]{1,0:T(8,128)(2,1)S(1)}, u32[]{:S(2)}, u32[]{:S(2)}) collective-permute-start(bf16[136,1024]{1,0:T(8,128)(2,1)S(1)} %collective-permute-done.9.refs_7_), channel_id=1, source_target_pairs={{0,120},{8,0},{16,8},{24,16},{32,24},{40,32},{48,40},{56,48},{64,5... | collective-permute-start | bytes 835592 | tf_op jit(solution)/shard_map/ppermute | solution.py:59
  77.4 1.9 collective-permute-start.3
  79.3 8.5 %collective-permute-done.10.refs_3_ = bf16[136,1024]{1,0:T(8,128)(2,1)S(1)} collective-permute-done((bf16[136,1024]{1,0:T(8,128)(2,1)S(1)}, bf16[136,1024]{1,0:T(8,128)(2,1)S(1)}, u32[]{:S(2)}, u32[]{:S(2)}) %collective-permute-start.10) | collective-permute-done | bytes 278560 | tf_op jit(solution)/shard_map/ppermute | solution.py:59
  87.9 5.4 %collective-permute-start.11 = (bf16[136,1024]{1,0:T(8,128)(2,1)S(1)}, bf16[136,1024]{1,0:T(8,128)(2,1)S(1)}, u32[]{:S(2)}, u32[]{:S(2)}) collective-permute-start(bf16[136,1024]{1,0:T(8,128)(2,1)S(1)} %collective-permute-done.10.refs_3_), channel_id=1, source_target_pairs={{0,120},{8,0},{16,8},{24,16},{32,24},{40,32},{48,40},{56,48},{64,5... | collective-permute-start | bytes 835592 | tf_op jit(solution)/shard_map/ppermute | solution.py:59
  95.9 5.7 %collective-permute-done.11.refs_4_ = bf16[136,1024]{1,0:T(8,128)(2,1)S(1)} collective-permute-done((bf16[136,1024]{1,0:T(8,128)(2,1)S(1)}, bf16[136,1024]{1,0:T(8,128)(2,1)S(1)}, u32[]{:S(2)}, u32[]{:S(2)}) %collective-permute-start.11) | collective-permute-done | bytes 278560 | tf_op jit(solution)/shard_map/ppermute | solution.py:59
  101.7 5.4 %collective-permute-start.12 = (bf16[136,1024]{1,0:T(8,128)(2,1)S(1)}, bf16[136,1024]{1,0:T(8,128)(2,1)S(1)}, u32[]{:S(2)}, u32[]{:S(2)}) collective-permute-start(bf16[136,1024]{1,0:T(8,128)(2,1)S(1)} %collective-permute-done.11.refs_4_), channel_id=1, source_target_pairs={{0,120},{8,0},{16,8},{24,16},{32,24},{40,32},{48,40},{56,48},{64,5... | collective-permute-start | bytes 835592 | tf_op jit(solution)/shard_map/ppermute | solution.py:59
  107.1 1.9 collective-permute-start.5
  110.5 5.0 %collective-permute-start.13 = (bf16[136,1024]{1,0:T(8,128)(2,1)S(1)}, bf16[136,1024]{1,0:T(8,128)(2,1)S(1)}, u32[]{:S(2)}, u32[]{:S(2)}) collective-permute-start(bf16[136,1024]{1,0:T(8,128)(2,1)S(1)} %collective-permute-done.12.refs_5_), channel_id=1, source_target_pairs={{0,120},{8,0},{16,8},{24,16},{32,24},{40,32},{48,40},{56,48},{64,5... | collective-permute-start | bytes 835592 | tf_op jit(solution)/shard_map/ppermute | solution.py:59
  117.6 3.9 %pick.3 = (bf16[4,104,1024]{2,1,0:T(8,128)(2,1)}, s32[4,1024]{1,0:T(4,128)}, f32[4,1024]{1,0:T(4,128)}, f32[8,128,4]{2,1,0:T(8,128)}, f32[8,128,4]{2,1,0:T(8,128)}) custom-call(s32[1]{0:T(128)} %bitcast.place_ref, bf16[136,1024]{1,0:T(8,128)(2,1)} %pack.1.refs_0_, bf16[136,1024]{1,0:T(8,128)(2,1)} %copy-done.9, bf16[136,1024]{1,0:T(8,128)(2,1)} %copy-done.13, ...), custom_call_target="tpu_custom_call" | custom-call | flops 872415232 | bytes 2949120 | tf_op jit(solution)/shard_map/pick/pallas_call | solution.py:144
  121.6 4.2 %all-to-all-start.3 = ((bf16[4,104,1024]{2,1,0:T(8,128)(2,1)}), bf16[4,104,1024]{2,1,0:T(8,128)(2,1)}, u32[]{:S(2)}, u32[]{:S(2)}) async-start(bf16[4,104,1024]{2,1,0:T(8,128)(2,1)} %get-tuple-element.20), calls=%async_computation.3 | async-start | bytes 1703936 | tf_op jit(solution)/shard_map/all_to_all | solution.py:228
  125.8 4.6 %collective-permute-start.15 = (bf16[72,1024]{1,0:T(8,128)(2,1)S(1)}, bf16[72,1024]{1,0:T(8,128)(2,1)S(1)}, u32[]{:S(2)}, u32[]{:S(2)}) collective-permute-start(bf16[72,1024]{1,0:T(8,128)(2,1)S(1)} %slice.29), channel_id=1, source_target_pairs={{0,120},{8,0},{16,8},{24,16},{32,24},{40,32},{48,40},{56,48},{64,5... | collective-permute-start | bytes 442376 | tf_op jit(solution)/shard_map/ppermute | solution.py:64
  130.5 1.9 collective-permute-start.14
  132.4 5.4 %collective-permute-done.14.refs_7_ = bf16[64,1024]{1,0:T(8,128)(2,1)S(1)} collective-permute-done((bf16[64,1024]{1,0:T(8,128)(2,1)S(1)}, bf16[64,1024]{1,0:T(8,128)(2,1)S(1)}, u32[]{:S(2)}, u32[]{:S(2)}) %collective-permute-start.14) | collective-permute-done | bytes 131104 | tf_op jit(solution)/shard_map/ppermute | solution.py:63
  139.1 3.9 %pick.2 = (bf16[4,104,1024]{2,1,0:T(8,128)(2,1)}, s32[4,1024]{1,0:T(4,128)}, f32[4,1024]{1,0:T(4,128)}, f32[8,128,4]{2,1,0:T(8,128)}, f32[8,128,4]{2,1,0:T(8,128)}) custom-call(s32[1]{0:T(128)} %bitcast.place_ref, bf16[136,1024]{1,0:T(8,128)(2,1)} %copy-done.11, bf16[136,1024]{1,0:T(8,128)(2,1)} %copy-done.16, bf16[136,1024]{1,0:T(8,128)(2,1)} %copy-done.6, ...), custom_call_target="tpu_custom_call" | custom-call | flops 872415232 | bytes 2949120 | tf_op jit(solution)/shard_map/pick/pallas_call | solution.py:144
  143.0 3.7 %slice_bitcast_fusion = (bf16[8,88,8,128]{3,2,1,0:T(8,128)(2,1)S(1)}, bf16[8,88,8,128]{3,2,1,0:T(8,128)(2,1)S(1)}, bf16[8,88,8,128]{3,2,1,0:T(8,128)(2,1)}) fusion(bf16[8,704,384]{2,1,0:T(8,128)(2,1)} %all-to-all-done.1), kind=kLoop, calls=%fused_computation.24 | loop fusion | bytes 8650752
  146.7 4.2 %all-to-all-start = ((bf16[4,104,1024]{2,1,0:T(8,128)(2,1)}), bf16[4,104,1024]{2,1,0:T(8,128)(2,1)}, u32[]{:S(2)}, u32[]{:S(2)}) async-start(bf16[4,104,1024]{2,1,0:T(8,128)(2,1)} %get-tuple-element.16), calls=%async_computation | async-start | bytes 1703936 | tf_op jit(solution)/shard_map/all_to_all | solution.py:228
  150.9 2.6 divide_multiply_fusion
  153.5 2.5 fusion.42
  159.6 4.2 %all-to-all-start.4 = ((bf16[4,104,1024]{2,1,0:T(8,128)(2,1)}), bf16[4,104,1024]{2,1,0:T(8,128)(2,1)}, u32[]{:S(2)}, u32[]{:S(2)}) async-start(bf16[4,104,1024]{2,1,0:T(8,128)(2,1)} %bitcast.106), calls=%async_computation.4 | async-start | bytes 1703936 | tf_op jit(solution)/shard_map/all_to_all | solution.py:228
  163.9 2.6 divide_multiply_fusion.1
  166.5 2.5 fusion.45
  172.6 3.5 %all-to-all-start.2 = ((bf16[4,104,1024]{2,1,0:T(8,128)(2,1)}), bf16[4,104,1024]{2,1,0:T(8,128)(2,1)S(1)}, u32[]{:S(2)}, u32[]{:S(2)}) async-start(bf16[4,104,1024]{2,1,0:T(8,128)(2,1)} %bitcast.12), calls=%async_computation.2 | async-start | bytes 1703936 | tf_op jit(solution)/shard_map/all_to_all | solution.py:228
  176.9 8.6 %mix.2.refs_0_ = bf16[2048,1024]{1,0:T(8,128)(2,1)} custom-call(s32[8]{0:T(128)} %get-tuple-element.28.dest_ref.source_ref, f32[8,128,4]{2,1,0:T(8,128)} %get-tuple-element.18.code_ref, f32[8,128,4]{2,1,0:T(8,128)} %get-tuple-element.19.gate_ref, bf16[4,104,1024]{2,1,0:T(8,128)(2,1)} %all-to-all-done.4.rows_ref), custom_call_target="tpu_custom_call" | custom-call | flops 2147483648 | bytes 2949120 | tf_op jit(solution)/shard_map/mix/pallas_call | solution.py:206
  186.4 8.5 %mix.3 = bf16[2048,1024]{1,0:T(8,128)(2,1)} custom-call(s32[8]{0:T(128)} %get-tuple-element.29.dest_ref.source_ref, f32[8,128,4]{2,1,0:T(8,128)} %get-tuple-element.14.code_ref, f32[8,128,4]{2,1,0:T(8,128)} %get-tuple-element.15.gate_ref, bf16[4,104,1024]{2,1,0:T(8,128)(2,1)} %copy-done, bf16[2048,1024]{1,0:T(8,128)(2,1)} %mix.2.refs_0_), custom_call_target="tpu_custom_call", output_to_operand_aliasing={{}: (4, {})} | custom-call | flops 2147483648 | bytes 2949120 | tf_op jit(solution)/shard_map/mix/pallas_call | solution.py:206
  195.0 4.5 %pick_weighted.2 = bf16[4,104,1024]{2,1,0:T(8,128)(2,1)} custom-call(s32[8]{0:T(128)} %get-tuple-element.28.dest_ref.source_ref, s32[4,1024]{1,0:T(4,128)} %get-tuple-element.21.code_ref, f32[4,1024]{1,0:T(4,128)} %get-tuple-element.22.gate_ref, ...), custom_call_target="tpu_custom_call" | custom-call | flops 872415232 | bytes 2949120 | tf_op jit(solution)/shard_map/pick_weighted/pallas_call | solution.py:166
  199.5 4.0 %all-to-all-start.5 = ((bf16[4,104,1024]{2,1,0:T(8,128)(2,1)}), bf16[4,104,1024]{2,1,0:T(8,128)(2,1)S(1)}, u32[]{:S(2)}, u32[]{:S(2)}) async-start(bf16[4,104,1024]{2,1,0:T(8,128)(2,1)} %pick_weighted.2), calls=%async_computation.6 | async-start | bytes 1703936 | tf_op jit(solution)/shard_map/all_to_all | solution.py:228
  203.5 4.5 %pick_weighted.3 = bf16[4,104,1024]{2,1,0:T(8,128)(2,1)} custom-call(s32[8]{0:T(128)} %get-tuple-element.29.dest_ref.source_ref, s32[4,1024]{1,0:T(4,128)} %get-tuple-element.23.code_ref, f32[4,1024]{1,0:T(4,128)} %get-tuple-element.24.gate_ref, ...), custom_call_target="tpu_custom_call" | custom-call | flops 872415232 | bytes 2949120 | tf_op jit(solution)/shard_map/pick_weighted/pallas_call | solution.py:166
  208.1 4.2 %all-to-all-done.5 = bf16[4,104,1024]{2,1,0:T(8,128)(2,1)S(1)} async-done(((bf16[4,104,1024]{2,1,0:T(8,128)(2,1)}), bf16[4,104,1024]{2,1,0:T(8,128)(2,1)S(1)}, u32[]{:S(2)}, u32[]{:S(2)}) %all-to-all-start.5) | async-done | bytes 852000 | tf_op jit(solution)/shard_map/all_to_all | solution.py:228
  212.2 3.5 %all-to-all-start.6 = ((bf16[4,104,1024]{2,1,0:T(8,128)(2,1)}), bf16[4,104,1024]{2,1,0:T(8,128)(2,1)S(1)}, u32[]{:S(2)}, u32[]{:S(2)}) async-start(bf16[4,104,1024]{2,1,0:T(8,128)(2,1)} %pick_weighted.3), calls=%async_computation.7 | async-start | bytes 1703936 | tf_op jit(solution)/shard_map/all_to_all | solution.py:228
  215.7 5.3 %fusion.53 = f32[1024,704]{0,1:T(8,128)} fusion(bf16[416,1024]{1,0:T(8,128)(2,1)} %bitcast.13, f32[416,704]{1,0:T(8,128)} %copy-done.22, bf16[416,1024]{1,0:T(8,128)(2,1)S(1)} %bitcast.100, bf16[8,88,8,128]{3,2,1,0:T(8,128)(2,1)S(1)} %get-tuple-element.25), kind=kOutput, calls=%fused_computation.43 | convolution fusion | flops 1200156672 | bytes 7200768 | tf_op jit(solution)/shard_map/dot_general | solution.py:274
  221.1 5.0 %all-to-all-done.6 = bf16[4,104,1024]{2,1,0:T(8,128)(2,1)S(1)} async-done(((bf16[4,104,1024]{2,1,0:T(8,128)(2,1)}), bf16[4,104,1024]{2,1,0:T(8,128)(2,1)S(1)}, u32[]{:S(2)}, u32[]{:S(2)}) %all-to-all-start.6) | async-done | bytes 852000 | tf_op jit(solution)/shard_map/all_to_all | solution.py:228
  226.0 5.1 %fusion = bf16[88,8,8,128]{3,2,1,0:T(8,128)(2,1)S(1)} fusion(f32[1024,704]{0,1:T(8,128)} %fusion.53, bf16[416,1024]{1,0:T(8,128)(2,1)} %bitcast.3, f32[416,704]{1,0:T(8,128)} %copy-done.23, bf16[416,1024]{1,0:T(8,128)(2,1)S(1)} %bitcast.104, bf16[8,88,8,128]{3,2,1,0:T(8,128)(2,1)} %copy-done.1), kind=kOutput, calls=%fused_computation.4 | convolution fusion | flops 1201598464 | bytes 8642560 | tf_op jit(solution)/shard_map/dot_general | solution.py:274
  232.6 16.2 %all-to-all-start.7 = ((bf16[8,128,704]{1,2,0:T(8,128)(2,1)}), bf16[8,128,704]{1,2,0:T(8,128)(2,1)S(1)}, u32[]{:S(2)}, u32[]{:S(2)}) async-start(bf16[8,128,704]{1,2,0:T(8,128)(2,1)} %bitcast.102), calls=%async_computation.8 | async-start | bytes 2883584 | tf_op jit(solution)/shard_map/all_to_all | solution.py:280
  248.8 2.1 fusion.68
  253.4 14.6 %all-to-all-done.7 = bf16[8,128,704]{1,2,0:T(8,128)(2,1)S(1)} async-done(((bf16[8,128,704]{1,2,0:T(8,128)(2,1)}), bf16[8,128,704]{1,2,0:T(8,128)(2,1)S(1)}, u32[]{:S(2)}, u32[]{:S(2)}) %all-to-all-start.7) | async-done | bytes 1441824 | tf_op jit(solution)/shard_map/all_to_all | solution.py:280
  268.0 5.1 %all-to-all-start.8 = ((bf16[8,128,704]{1,2,0:T(8,128)(2,1)}), bf16[8,128,704]{1,2,0:T(8,128)(2,1)}, u32[]{:S(2)}, u32[]{:S(2)}) async-start(bf16[8,128,704]{1,2,0:T(8,128)(2,1)} %bitcast.103), calls=%async_computation.9 | async-start | bytes 2883584 | tf_op jit(solution)/shard_map/all_to_all | solution.py:280
  274.1 18.4 %all-to-all-done.8 = bf16[8,128,704]{1,2,0:T(8,128)(2,1)} async-done(((bf16[8,128,704]{1,2,0:T(8,128)(2,1)}), bf16[8,128,704]{1,2,0:T(8,128)(2,1)}, u32[]{:S(2)}, u32[]{:S(2)}) %all-to-all-start.8) | async-done | bytes 1441824 | tf_op jit(solution)/shard_map/all_to_all | solution.py:280
  292.4 2.3 convert_reduce_fusion
  (84 shorter events, 28.7 us)
Async XLA Ops:
  7.2 187.9 %all-gather.2.cloned.1.call-start = ((), (), s32[]{:S(2)}) async-start(), calls=%async_computation.11 | async-start | bytes 4456448 | tf_op jit(solution)/shard_map/all_gather | solution.py:235
  9.6 17.6 %collective-permute-start.7 = (bf16[136,1024]{1,0:T(8,128)(2,1)}, bf16[136,1024]{1,0:T(8,128)(2,1)S(1)}, u32[]{:S(2)}, u32[]{:S(2)}) collective-permute-start(bf16[136,1024]{1,0:T(8,128)(2,1)} %pack.1.refs_0_), channel_id=1, source_target_pairs={{0,120},{8,0},{16,8},{24,16},{32,24},{40,32},{48,40},{56,48},{64,5... | collective-permute-start | bytes 835592 | tf_op jit(solution)/shard_map/ppermute | solution.py:59
  21.5 10.6 %collective-permute-start = (bf16[136,1024]{1,0:T(8,128)(2,1)}, bf16[136,1024]{1,0:T(8,128)(2,1)S(1)}, u32[]{:S(2)}, u32[]{:S(2)}) collective-permute-start(bf16[136,1024]{1,0:T(8,128)(2,1)} %pack.1.refs_0_), channel_id=1, source_target_pairs={{0,8},{8,16},{16,24},{24,32},{32,40},{40,48},{48,56},{56,64},{64,7... | collective-permute-start | bytes 835592 | tf_op jit(solution)/shard_map/ppermute | solution.py:58
  27.2 13.6 %copy-start.7 = (bf16[136,1024]{1,0:T(8,128)(2,1)}, bf16[136,1024]{1,0:T(8,128)(2,1)S(1)}, u32[]{:S(2)}) copy-start(bf16[136,1024]{1,0:T(8,128)(2,1)S(1)} %collective-permute-done.7.refs_5_) | copy-start | bytes 835588
  32.1 10.5 %copy-start.9 = (bf16[136,1024]{1,0:T(8,128)(2,1)}, bf16[136,1024]{1,0:T(8,128)(2,1)S(1)}, u32[]{:S(2)}) copy-start(bf16[136,1024]{1,0:T(8,128)(2,1)S(1)} %collective-permute-done.refs_1_) | copy-start | bytes 835588
  34.5 87.1 %all-to-all-start.1 = ((bf16[8,704,384]{2,1,0:T(8,128)(2,1)}), bf16[8,704,384]{2,1,0:T(8,128)(2,1)}, u32[]{:S(2)}, u32[]{:S(2)}) async-start(bf16[8,704,384]{2,1,0:T(8,128)(2,1)} %broadcast_in_dim.12), calls=%async_computation.1 | async-start | bytes 8650752 | tf_op jit(solution)/shard_map/all_to_all | solution.py:245
  40.7 14.9 %collective-permute-start.8 = (bf16[136,1024]{1,0:T(8,128)(2,1)S(1)}, bf16[136,1024]{1,0:T(8,128)(2,1)S(1)}, u32[]{:S(2)}, u32[]{:S(2)}) collective-permute-start(bf16[136,1024]{1,0:T(8,128)(2,1)S(1)} %collective-permute-done.7.refs_5_), channel_id=1, source_target_pairs={{0,120},{8,0},{16,8},{24,16},{32,24},{40,32},{48,40},{56,48},{64,5... | collective-permute-start | bytes 835592 | tf_op jit(solution)/shard_map/ppermute | solution.py:59
  42.7 17.5 %collective-permute-start.1 = (bf16[136,1024]{1,0:T(8,128)(2,1)S(1)}, bf16[136,1024]{1,0:T(8,128)(2,1)S(1)}, u32[]{:S(2)}, u32[]{:S(2)}) collective-permute-start(bf16[136,1024]{1,0:T(8,128)(2,1)S(1)} %collective-permute-done.refs_1_), channel_id=1, source_target_pairs={{0,8},{8,16},{16,24},{24,32},{32,40},{40,48},{48,56},{56,64},{64,7... | collective-permute-start | bytes 835592 | tf_op jit(solution)/shard_map/ppermute | solution.py:58
  55.6 61.9 %copy-start.12 = (bf16[136,1024]{1,0:T(8,128)(2,1)}, bf16[136,1024]{1,0:T(8,128)(2,1)S(1)}, u32[]{:S(2)}) copy-start(bf16[136,1024]{1,0:T(8,128)(2,1)S(1)} %collective-permute-done.8.refs_6_) | copy-start | bytes 835588
  55.6 16.4 %collective-permute-start.9 = (bf16[136,1024]{1,0:T(8,128)(2,1)S(1)}, bf16[136,1024]{1,0:T(8,128)(2,1)S(1)}, u32[]{:S(2)}, u32[]{:S(2)}) collective-permute-start(bf16[136,1024]{1,0:T(8,128)(2,1)S(1)} %collective-permute-done.8.refs_6_), channel_id=1, source_target_pairs={{0,120},{8,0},{16,8},{24,16},{32,24},{40,32},{48,40},{56,48},{64,5... | collective-permute-start | bytes 835592 | tf_op jit(solution)/shard_map/ppermute | solution.py:59
  60.2 57.4 %copy-start.13 = (bf16[136,1024]{1,0:T(8,128)(2,1)}, bf16[136,1024]{1,0:T(8,128)(2,1)S(1)}, u32[]{:S(2)}) copy-start(bf16[136,1024]{1,0:T(8,128)(2,1)S(1)} %collective-permute-done.1.refs_2_) | copy-start | bytes 835588
  60.2 17.2 %collective-permute-start.2 = (bf16[136,1024]{1,0:T(8,128)(2,1)S(1)}, bf16[136,1024]{1,0:T(8,128)(2,1)S(1)}, u32[]{:S(2)}, u32[]{:S(2)}) collective-permute-start(bf16[136,1024]{1,0:T(8,128)(2,1)S(1)} %collective-permute-done.1.refs_2_), channel_id=1, source_target_pairs={{0,8},{8,16},{16,24},{24,32},{32,40},{40,48},{48,56},{56,64},{64,7... | collective-permute-start | bytes 835592 | tf_op jit(solution)/shard_map/ppermute | solution.py:58
  72.0 45.6 %copy-start.15 = (bf16[136,1024]{1,0:T(8,128)(2,1)}, bf16[136,1024]{1,0:T(8,128)(2,1)S(1)}, u32[]{:S(2)}) copy-start(bf16[136,1024]{1,0:T(8,128)(2,1)S(1)} %collective-permute-done.9.refs_7_) | copy-start | bytes 835588
  72.0 15.9 %collective-permute-start.10 = (bf16[136,1024]{1,0:T(8,128)(2,1)S(1)}, bf16[136,1024]{1,0:T(8,128)(2,1)S(1)}, u32[]{:S(2)}, u32[]{:S(2)}) collective-permute-start(bf16[136,1024]{1,0:T(8,128)(2,1)S(1)} %collective-permute-done.9.refs_7_), channel_id=1, source_target_pairs={{0,120},{8,0},{16,8},{24,16},{32,24},{40,32},{48,40},{56,48},{64,5... | collective-permute-start | bytes 835592 | tf_op jit(solution)/shard_map/ppermute | solution.py:59
  77.4 40.2 %copy-start.17 = (bf16[136,1024]{1,0:T(8,128)(2,1)}, bf16[136,1024]{1,0:T(8,128)(2,1)S(1)}, u32[]{:S(2)}) copy-start(bf16[136,1024]{1,0:T(8,128)(2,1)S(1)} %collective-permute-done.2.refs_3_) | copy-start | bytes 835588
  77.4 16.6 %collective-permute-start.3 = (bf16[136,1024]{1,0:T(8,128)(2,1)S(1)}, bf16[136,1024]{1,0:T(8,128)(2,1)S(1)}, u32[]{:S(2)}, u32[]{:S(2)}) collective-permute-start(bf16[136,1024]{1,0:T(8,128)(2,1)S(1)} %collective-permute-done.2.refs_3_), channel_id=1, source_target_pairs={{0,8},{8,16},{16,24},{24,32},{32,40},{40,48},{48,56},{56,64},{64,7... | collective-permute-start | bytes 835592 | tf_op jit(solution)/shard_map/ppermute | solution.py:58
  87.8 33.7 %copy-start.8 = (bf16[136,1024]{1,0:T(8,128)(2,1)}, bf16[136,1024]{1,0:T(8,128)(2,1)S(1)}, u32[]{:S(2)}) copy-start(bf16[136,1024]{1,0:T(8,128)(2,1)S(1)} %collective-permute-done.10.refs_3_) | copy-start | bytes 835588
  87.9 13.8 %collective-permute-start.11 = (bf16[136,1024]{1,0:T(8,128)(2,1)S(1)}, bf16[136,1024]{1,0:T(8,128)(2,1)S(1)}, u32[]{:S(2)}, u32[]{:S(2)}) collective-permute-start(bf16[136,1024]{1,0:T(8,128)(2,1)S(1)} %collective-permute-done.10.refs_3_), channel_id=1, source_target_pairs={{0,120},{8,0},{16,8},{24,16},{32,24},{40,32},{48,40},{56,48},{64,5... | collective-permute-start | bytes 835592 | tf_op jit(solution)/shard_map/ppermute | solution.py:59
  94.0 23.6 %copy-start.18 = (bf16[136,1024]{1,0:T(8,128)(2,1)}, bf16[136,1024]{1,0:T(8,128)(2,1)S(1)}, u32[]{:S(2)}) copy-start(bf16[136,1024]{1,0:T(8,128)(2,1)S(1)} %collective-permute-done.3.refs_4_) | copy-start | bytes 835588
  94.0 13.1 %collective-permute-start.4 = (bf16[136,1024]{1,0:T(8,128)(2,1)S(1)}, bf16[136,1024]{1,0:T(8,128)(2,1)S(1)}, u32[]{:S(2)}, u32[]{:S(2)}) collective-permute-start(bf16[136,1024]{1,0:T(8,128)(2,1)S(1)} %collective-permute-done.3.refs_4_), channel_id=1, source_target_pairs={{0,8},{8,16},{16,24},{24,32},{32,40},{40,48},{48,56},{56,64},{64,7... | collective-permute-start | bytes 835592 | tf_op jit(solution)/shard_map/ppermute | solution.py:58
  101.6 19.9 %copy-start.10 = (bf16[136,1024]{1,0:T(8,128)(2,1)}, bf16[136,1024]{1,0:T(8,128)(2,1)S(1)}, u32[]{:S(2)}) copy-start(bf16[136,1024]{1,0:T(8,128)(2,1)S(1)} %collective-permute-done.11.refs_4_) | copy-start | bytes 835588
  101.7 8.9 %collective-permute-start.12 = (bf16[136,1024]{1,0:T(8,128)(2,1)S(1)}, bf16[136,1024]{1,0:T(8,128)(2,1)S(1)}, u32[]{:S(2)}, u32[]{:S(2)}) collective-permute-start(bf16[136,1024]{1,0:T(8,128)(2,1)S(1)} %collective-permute-done.11.refs_4_), channel_id=1, source_target_pairs={{0,120},{8,0},{16,8},{24,16},{32,24},{40,32},{48,40},{56,48},{64,5... | collective-permute-start | bytes 835592 | tf_op jit(solution)/shard_map/ppermute | solution.py:59
  107.1 14.4 %copy-start.11 = (bf16[136,1024]{1,0:T(8,128)(2,1)}, bf16[136,1024]{1,0:T(8,128)(2,1)S(1)}, u32[]{:S(2)}) copy-start(bf16[136,1024]{1,0:T(8,128)(2,1)S(1)} %collective-permute-done.4.refs_0_) | copy-start | bytes 835588
  107.1 8.5 %collective-permute-start.5 = (bf16[136,1024]{1,0:T(8,128)(2,1)S(1)}, bf16[136,1024]{1,0:T(8,128)(2,1)S(1)}, u32[]{:S(2)}, u32[]{:S(2)}) collective-permute-start(bf16[136,1024]{1,0:T(8,128)(2,1)S(1)} %collective-permute-done.4.refs_0_), channel_id=1, source_target_pairs={{0,8},{8,16},{16,24},{24,32},{32,40},{40,48},{48,56},{56,64},{64,7... | collective-permute-start | bytes 835592 | tf_op jit(solution)/shard_map/ppermute | solution.py:58
  110.5 11.0 %copy-start.14 = (bf16[136,1024]{1,0:T(8,128)(2,1)}, bf16[136,1024]{1,0:T(8,128)(2,1)S(1)}, u32[]{:S(2)}) copy-start(bf16[136,1024]{1,0:T(8,128)(2,1)S(1)} %collective-permute-done.12.refs_5_) | copy-start | bytes 835588
  110.5 15.2 %collective-permute-start.13 = (bf16[136,1024]{1,0:T(8,128)(2,1)S(1)}, bf16[136,1024]{1,0:T(8,128)(2,1)S(1)}, u32[]{:S(2)}, u32[]{:S(2)}) collective-permute-start(bf16[136,1024]{1,0:T(8,128)(2,1)S(1)} %collective-permute-done.12.refs_5_), channel_id=1, source_target_pairs={{0,120},{8,0},{16,8},{24,16},{32,24},{40,32},{48,40},{56,48},{64,5... | collective-permute-start | bytes 835592 | tf_op jit(solution)/shard_map/ppermute | solution.py:59
  115.6 5.9 %copy-start.16 = (bf16[136,1024]{1,0:T(8,128)(2,1)}, bf16[136,1024]{1,0:T(8,128)(2,1)S(1)}, u32[]{:S(2)}) copy-start(bf16[136,1024]{1,0:T(8,128)(2,1)S(1)} %collective-permute-done.5.refs_1_) | copy-start | bytes 835588
  115.6 14.8 %collective-permute-start.6 = (bf16[136,1024]{1,0:T(8,128)(2,1)S(1)}, bf16[136,1024]{1,0:T(8,128)(2,1)S(1)}, u32[]{:S(2)}, u32[]{:S(2)}) collective-permute-start(bf16[136,1024]{1,0:T(8,128)(2,1)S(1)} %collective-permute-done.5.refs_1_), channel_id=1, source_target_pairs={{0,8},{8,16},{16,24},{24,32},{32,40},{40,48},{48,56},{56,64},{64,7... | collective-permute-start | bytes 835592 | tf_op jit(solution)/shard_map/ppermute | solution.py:58
  121.6 25.1 %all-to-all-start.3 = ((bf16[4,104,1024]{2,1,0:T(8,128)(2,1)}), bf16[4,104,1024]{2,1,0:T(8,128)(2,1)}, u32[]{:S(2)}, u32[]{:S(2)}) async-start(bf16[4,104,1024]{2,1,0:T(8,128)(2,1)} %get-tuple-element.20), calls=%async_computation.3 | async-start | bytes 1703936 | tf_op jit(solution)/shard_map/all_to_all | solution.py:228
  125.8 12.0 %copy-start.5 = (bf16[136,1024]{1,0:T(8,128)(2,1)}, bf16[136,1024]{1,0:T(8,128)(2,1)S(1)}, u32[]{:S(2)}) copy-start(bf16[136,1024]{1,0:T(8,128)(2,1)S(1)} %collective-permute-done.13.refs_6_) | copy-start | bytes 835588
  125.8 12.0 %collective-permute-start.15 = (bf16[72,1024]{1,0:T(8,128)(2,1)S(1)}, bf16[72,1024]{1,0:T(8,128)(2,1)S(1)}, u32[]{:S(2)}, u32[]{:S(2)}) collective-permute-start(bf16[72,1024]{1,0:T(8,128)(2,1)S(1)} %slice.29), channel_id=1, source_target_pairs={{0,120},{8,0},{16,8},{24,16},{32,24},{40,32},{48,40},{56,48},{64,5... | collective-permute-start | bytes 442376 | tf_op jit(solution)/shard_map/ppermute | solution.py:64
  130.4 7.4 %copy-start.6 = (bf16[136,1024]{1,0:T(8,128)(2,1)}, bf16[136,1024]{1,0:T(8,128)(2,1)S(1)}, u32[]{:S(2)}) copy-start(bf16[136,1024]{1,0:T(8,128)(2,1)S(1)} %collective-permute-done.6.refs_2_) | copy-start | bytes 835588
  130.5 7.3 %collective-permute-start.14 = (bf16[64,1024]{1,0:T(8,128)(2,1)S(1)}, bf16[64,1024]{1,0:T(8,128)(2,1)S(1)}, u32[]{:S(2)}, u32[]{:S(2)}) collective-permute-start(bf16[64,1024]{1,0:T(8,128)(2,1)S(1)} %slice.28), channel_id=1, source_target_pairs={{0,8},{8,16},{16,24},{24,32},{32,40},{40,48},{48,56},{56,64},{64,7... | collective-permute-start | bytes 393224 | tf_op jit(solution)/shard_map/ppermute | solution.py:63
  146.7 69.1 %copy-start.1 = (bf16[8,88,8,128]{3,2,1,0:T(8,128)(2,1)}, bf16[8,88,8,128]{3,2,1,0:T(8,128)(2,1)S(1)}, u32[]{:S(2)}) copy-start(bf16[8,88,8,128]{3,2,1,0:T(8,128)(2,1)S(1)} %get-tuple-element.25) | copy-start | bytes 4325380
  146.7 13.0 %all-to-all-start = ((bf16[4,104,1024]{2,1,0:T(8,128)(2,1)}), bf16[4,104,1024]{2,1,0:T(8,128)(2,1)}, u32[]{:S(2)}, u32[]{:S(2)}) async-start(bf16[4,104,1024]{2,1,0:T(8,128)(2,1)} %get-tuple-element.16), calls=%async_computation | async-start | bytes 1703936 | tf_op jit(solution)/shard_map/all_to_all | solution.py:228
  153.5 2.5 copy-start.22
  156.0 0.8 copy-start.2
  159.6 13.0 %all-to-all-start.4 = ((bf16[4,104,1024]{2,1,0:T(8,128)(2,1)}), bf16[4,104,1024]{2,1,0:T(8,128)(2,1)}, u32[]{:S(2)}, u32[]{:S(2)}) async-start(bf16[4,104,1024]{2,1,0:T(8,128)(2,1)} %bitcast.106), calls=%async_computation.4 | async-start | bytes 1703936 | tf_op jit(solution)/shard_map/all_to_all | solution.py:228
  166.5 2.5 copy-start.23
  171.6 4.8 %copy-start.21 = (s32[16]{0:T(128)S(1)}, s32[16]{0:T(128)}, u32[]{:S(2)}) copy-start(s32[16]{0:T(128)} %constant.43) | copy-start | bytes 196
  172.6 12.9 %all-to-all-start.2 = ((bf16[4,104,1024]{2,1,0:T(8,128)(2,1)}), bf16[4,104,1024]{2,1,0:T(8,128)(2,1)S(1)}, u32[]{:S(2)}, u32[]{:S(2)}) async-start(bf16[4,104,1024]{2,1,0:T(8,128)(2,1)} %bitcast.12), calls=%async_computation.2 | async-start | bytes 1703936 | tf_op jit(solution)/shard_map/all_to_all | solution.py:228
  176.1 118.6 %reduce-scatter.2.cloned.1.call-start = ((), (), s32[]{:S(2)}) async-start(), calls=%async_computation.10 | async-start | bytes 4456448 | tf_op jit(solution)/shard_map/reduce_scatter | solution.py:266
  185.5 0.9 copy-start
  199.5 12.7 %all-to-all-start.5 = ((bf16[4,104,1024]{2,1,0:T(8,128)(2,1)}), bf16[4,104,1024]{2,1,0:T(8,128)(2,1)S(1)}, u32[]{:S(2)}, u32[]{:S(2)}) async-start(bf16[4,104,1024]{2,1,0:T(8,128)(2,1)} %pick_weighted.2), calls=%async_computation.6 | async-start | bytes 1703936 | tf_op jit(solution)/shard_map/all_to_all | solution.py:228
  212.2 13.8 %all-to-all-start.6 = ((bf16[4,104,1024]{2,1,0:T(8,128)(2,1)}), bf16[4,104,1024]{2,1,0:T(8,128)(2,1)S(1)}, u32[]{:S(2)}, u32[]{:S(2)}) async-start(bf16[4,104,1024]{2,1,0:T(8,128)(2,1)} %pick_weighted.3), calls=%async_computation.7 | async-start | bytes 1703936 | tf_op jit(solution)/shard_map/all_to_all | solution.py:228
  232.6 35.4 %all-to-all-start.7 = ((bf16[8,128,704]{1,2,0:T(8,128)(2,1)}), bf16[8,128,704]{1,2,0:T(8,128)(2,1)S(1)}, u32[]{:S(2)}, u32[]{:S(2)}) async-start(bf16[8,128,704]{1,2,0:T(8,128)(2,1)} %bitcast.102), calls=%async_computation.8 | async-start | bytes 2883584 | tf_op jit(solution)/shard_map/all_to_all | solution.py:280
  248.8 2.1 copy-start.4
  268.0 24.4 %all-to-all-start.8 = ((bf16[8,128,704]{1,2,0:T(8,128)(2,1)}), bf16[8,128,704]{1,2,0:T(8,128)(2,1)}, u32[]{:S(2)}, u32[]{:S(2)}) async-start(bf16[8,128,704]{1,2,0:T(8,128)(2,1)} %bitcast.103), calls=%async_computation.9 | async-start | bytes 2883584 | tf_op jit(solution)/shard_map/all_to_all | solution.py:280
  (3 other events, 2.1 us)
Sparse Core Ops, SparseCore 0:
  10.1 93.3 all-gather.1
  195.1 75.1 reduce-scatter.1

commit v2 on v1

--- a/solution.py
+++ b/solution.py
@@ -6,6 +6,7 @@
 from jax.experimental import pallas as pl
 from jax.experimental.pallas import tpu as pltpu
 from jax.sharding import PartitionSpec as P
+
 
 NX, NZ = 4, 16
 CAP = 13
@@ -48,22 +49,6 @@
         cost_estimate=pl.CostEstimate(flops=0, bytes_accessed=4 * TOK * tokens.shape[1], transcendentals=0),
         name="pack",
     )(tokens, ids.T, gates.T)
-
-
-def ring(a):
-    held = {0: (a,)}
-    fwd = back = a
-    half = NZ // 2
-    for i in range(1, half):
-        fwd = lax.ppermute(fwd, "ep", zperm(1))
-        back = lax.ppermute(back, "ep", zperm(-1))
-        held[i], held[-i] = (fwd,), (back,)
-    mid = TOK // 2
-    held[half] = (
-        lax.ppermute(fwd[:mid], "ep", zperm(1)),
-        lax.ppermute(back[mid:], "ep", zperm(-1)),
-    )
-    return held
 
 
 def pick_rows(code, gate, all_rows, out_ref, weighted):
@@ -179,41 +164,54 @@
 
 
 def mix_body(dest_ref, code_ref, gate_ref, rows_ref, *refs):
-    out_ref, stage = refs[-2], refs[-1]
-    width = out_ref.shape[1]
-
-    @pl.when(pl.program_id(0) == 0)
-    def _():
-        for j in range(NX):
-            stage[j * PAD : j * PAD + ROWS, :] = rows_ref[j]
-            stage[j * PAD + ROWS : (j + 1) * PAD, :] = jnp.zeros((PAD - ROWS, width), jnp.bfloat16)
-
+    out_ref, stage, ready, sems = refs[-4:]
+    width = stage.shape[1]
+    for j in range(NX):
+        stage[j * PAD : j * PAD + ROWS, :] = rows_ref[j]
+        stage[j * PAD + ROWS : (j + 1) * PAD, :] = jnp.zeros((PAD - ROWS, width), jnp.bfloat16)
     slot = lax.broadcasted_iota(jnp.int32, (TOK, PAD), 1).astype(jnp.float32)
-    code, gate = code_ref[0], gate_ref[0]
-    full = jnp.concatenate(
-        [jnp.where(slot == code[:, j : j + 1], gate[:, j : j + 1], 0.0) for j in range(NX)], axis=1
-    )
-    high = full.astype(jnp.bfloat16)
-    low = (full - high.astype(jnp.float32)).astype(jnp.bfloat16)
-    both = jnp.dot(jnp.concatenate([high, low], axis=0), stage[...], preferred_element_type=jnp.float32)
-    out_ref[...] = (both[:TOK] + both[TOK:]).astype(jnp.bfloat16)
+
+    def copy(n):
+        at = pl.multiple_of(dest_ref[n] * TOK, TOK)
+        return pltpu.make_async_copy(ready.at[n], out_ref.at[pl.ds(at, TOK), :], sems.at[n])
+
+    def one(n, carry):
+        code, gate = code_ref[n], gate_ref[n]
+        full = jnp.concatenate(
+            [jnp.where(slot == code[:, j : j + 1], gate[:, j : j + 1], 0.0) for j in range(NX)], axis=1
+        )
+        high = full.astype(jnp.bfloat16)
+        low = (full - high.astype(jnp.float32)).astype(jnp.bfloat16)
+        both = jnp.dot(
+            jnp.concatenate([high, low], axis=0), stage[...], preferred_element_type=jnp.float32
+        )
+        ready[n] = (both[:TOK] + both[TOK:]).astype(jnp.bfloat16)
+        copy(n).start()
+        return carry
+
+    def finish(n, carry):
+        copy(n).wait()
+        return carry
+
+    lax.fori_loop(0, COUNT, one, 0)
+    lax.fori_loop(0, COUNT, finish, 0)
 
 
 def mix(dest, code_t, gate_t, rows, before):
     width = rows.shape[2]
-    small = pl.BlockSpec((1, TOK, NX), lambda i, dest: (i, 0, 0))
     chained = before is not None
+    vmem = pl.BlockSpec(memory_space=pltpu.VMEM)
+    whole = pl.BlockSpec(memory_space=pl.ANY)
     return pl.pallas_call(
         mix_body,
         out_shape=jax.ShapeDtypeStruct((NZ * TOK, width), jnp.bfloat16),
-        grid_spec=pltpu.PrefetchScalarGridSpec(
-            num_scalar_prefetch=1,
-            grid=(COUNT,),
-            in_specs=[small, small, pl.BlockSpec((NX, ROWS, width), lambda i, dest: (0, 0, 0))]
-            + ([pl.BlockSpec(memory_space=pl.ANY)] if chained else []),
-            out_specs=pl.BlockSpec((TOK, width), lambda i, dest: (dest[i], 0)),
-            scratch_shapes=[pltpu.VMEM((NX * PAD, width), jnp.bfloat16)],
-        ),
+        in_specs=[pl.BlockSpec(memory_space=pltpu.SMEM), vmem, vmem, vmem] + ([whole] if chained else []),
+        out_specs=whole,
+        scratch_shapes=[
+            pltpu.VMEM((NX * PAD, width), jnp.bfloat16),
+            pltpu.VMEM((COUNT, TOK, width), jnp.bfloat16),
+            pltpu.SemaphoreType.DMA((COUNT,)),
+        ],
         input_output_aliases={4: 0} if chained else {},
         cost_estimate=pl.CostEstimate(
             flops=4 * NX * PAD * COUNT * TOK * width,
@@ -230,44 +228,81 @@
 
 def local(tokens, expert_ids, gate_weights, cotangent, w_gate, w_up, w_down):
     width = tokens.shape[1]
+    hidden_width = w_gate.shape[2]
+    share = w_gate.shape[1]
     z = lax.axis_index("ep") % NZ
+    core = lax.axis_index("rep") % 2
     n_rep = lax.axis_size("rep")
-    all_cot = lax.all_gather(cotangent, "ep", axis_index_groups=ZG, axis=0, tiled=True)
-    held = ring(pack(tokens, expert_ids, gate_weights))
     source = (z - jnp.array(NEAR + FAR, jnp.int32)) % NZ
     place = z.reshape(1)
-
-    hidden_width = w_gate.shape[2]
-    share = w_gate.shape[1]
+    last = (((1,), (1,)), ((), ()))
+    first = (((0,), (0,)), ((), ()))
+    tied = lax.optimization_barrier
+
+    fwd = back = pack(tokens, expert_ids, gate_weights)
+    held = {0: (fwd,)}
+
+    def step(i):
+        nonlocal fwd, back
+        sent_fwd, sent_back = fwd, back
+        if i > 1:
+            sent_fwd, _ = tied((fwd, held[2 - i][0]))
+            sent_back, _ = tied((back, held[i - 2][0]))
+        fwd = lax.ppermute(sent_fwd, "ep", zperm(1))
+        back = lax.ppermute(sent_back, "ep", zperm(-1))
+        held[i], held[-i] = (fwd,), (back,)
+
+    def send(b):
+        group = (NEAR, FAR)[b]
+        rows, code, gate, code_t, gate_t = pick(place, [held[d] for d in group])
+        rows = across_x(rows)
+        return rows.reshape(NX * ROWS, width), (code, gate), (code_t, gate_t)
+
+    def forward(rows):
+        gate_pre = lax.dot_general(rows, full_gate, last, preferred_element_type=jnp.float32)
+        up_pre = lax.dot_general(rows, full_up, last, preferred_element_type=jnp.float32)
+        silu = jax.nn.silu(gate_pre)
+        hidden = (silu * up_pre).astype(jnp.bfloat16)
+        out = jnp.dot(hidden, full_down, preferred_element_type=jnp.float32).astype(jnp.bfloat16)
+        return out, silu, hidden
+
+    step(1)
     shards = jnp.concatenate([w_gate[0].T, w_up[0].T, w_down[0]], axis=1)
-    shards, _, _ = lax.optimization_barrier((shards, held[1][0], held[-1][0]))
+    shards, _, _ = tied((shards, fwd, back))
     shards = jnp.broadcast_to(shards[None], (n_rep,) + shards.shape)
     shards = lax.all_to_all(shards, "rep", split_axis=0, concat_axis=0, tiled=True)
     full_gate, full_up, full_down = (
         shards[:, :, n * share : (n + 1) * share].transpose(1, 0, 2).reshape(hidden_width, width)
         for n in range(3)
     )
-    last = (((1,), (1,)), ((), ()))
-    first = (((0,), (0,)), ((), ()))
-
-    mixed = None
-    kept = []
-    for b, group in enumerate((NEAR, FAR)):
-        sources = source[b * COUNT : (b + 1) * COUNT]
-        rows, code, gate, code_t, gate_t = pick(place, [held[d] for d in group])
-        rows = across_x(rows).reshape(NX * ROWS, width)
-        gate_pre = lax.dot_general(rows, full_gate, last, preferred_element_type=jnp.float32)
-        up_pre = lax.dot_general(rows, full_up, last, preferred_element_type=jnp.float32)
-        silu = jax.nn.silu(gate_pre)
-        hidden = (silu * up_pre).astype(jnp.bfloat16)
-        out = jnp.dot(hidden, full_down, preferred_element_type=jnp.float32).astype(jnp.bfloat16)
-        mixed = mix(sources, code_t, gate_t, across_x(out.reshape(NX, ROWS, width)), mixed)
-        kept.append((sources, code, gate, rows, silu, hidden))
+    for i in range(2, 6):
+        step(i)
+    cotangent, _, _ = tied((cotangent, fwd, back))
+    all_cot = lax.all_gather(cotangent, "ep", axis_index_groups=ZG, axis=0, tiled=True)
+    near_rows, near_routes, near_weights = send(0)
+    step(6)
+    near_out, near_silu, near_hidden = forward(near_rows)
+    near_out, fwd, back = tied((near_out, fwd, back))
+    step(7)
+    near_back = across_x(near_out.reshape(NX, ROWS, width))
+    near_back, fwd, back = tied((near_back, fwd, back))
+    mid = TOK // 2
+    held[NZ // 2] = (
+        lax.ppermute(fwd[:mid], "ep", zperm(1)),
+        lax.ppermute(back[mid:], "ep", zperm(-1)),
+    )
+    far_rows, far_routes, far_weights = send(1)
+    mixed = mix(source[:COUNT], *near_weights, near_back, None)
+    far_out, far_silu, far_hidden = forward(far_rows)
+    mixed = mix(source[COUNT:], *far_weights, across_x(far_out.reshape(NX, ROWS, width)), mixed)
     mixed_out = lax.psum_scatter(mixed, "ep", axis_index_groups=ZG, scatter_dimension=0, tiled=True)
 
     part_up = part_down = None
-    for sources, code, gate, rows, silu, hidden in kept:
-        grad_rows = across_x(pick_from(sources, code, gate, all_cot)).reshape(NX * ROWS, width)
+    for b, (routes, rows, silu, hidden) in enumerate(
+        ((near_routes, near_rows, near_silu, near_hidden), (far_routes, far_rows, far_silu, far_hidden))
+    ):
+        picked = pick_from(source[b * COUNT : (b + 1) * COUNT], *routes, all_cot)
+        grad_rows = across_x(picked).reshape(NX * ROWS, width)
         hidden_grad = lax.dot_general(grad_rows, full_down, last, preferred_element_type=jnp.float32)
         up_grad = (hidden_grad * silu).astype(jnp.bfloat16)
         down = lax.dot_general(grad_rows, hidden, first, preferred_element_type=jnp.float32)
@@ -276,9 +311,15 @@
         part_up = up if part_up is None else part_up + up
 
     def summed(part):
-        part = part.astype(jnp.bfloat16).reshape(n_rep, width // n_rep, hidden_width)
-        part = lax.all_to_all(part, "rep", split_axis=0, concat_axis=0, tiled=True)
-        return jnp.sum(part.astype(jnp.float32), axis=0)
+        part = part.astype(jnp.bfloat16).reshape(n_rep // 2, 2, width // n_rep, hidden_width)
+        kept = lax.dynamic_index_in_dim(part, core, 1, keepdims=False)
+        sent = lax.dynamic_index_in_dim(part, 1 - core, 1, keepdims=False)
+        swap = [(r, r ^ 1) for r in range(n_rep)]
+        got = lax.ppermute(sent, "rep", swap)
+        pair = (kept.astype(jnp.float32) + got.astype(jnp.float32)).astype(jnp.bfloat16)
+        groups = [list(range(c, n_rep, 2)) for c in range(2)]
+        pair = lax.all_to_all(pair, "rep", split_axis=0, concat_axis=0, axis_index_groups=groups, tiled=True)
+        return jnp.sum(pair.astype(jnp.float32), axis=0)
 
     grad_down = summed(part_down).T
     grad_up = summed(part_up)
@@ -296,4 +337,5 @@
         P("ep", None, "rep"),
     )
     out_specs = (P(("ep", "rep"), None), P("ep", "rep", None), P("ep", None, "rep"))
+
     return jax.shard_map(local, mesh=mesh, in_specs=in_specs, out_specs=out_specs, check_vma=False)

time: 304 us -> 309 us (1.016)
  blocking collectives: 0 us -> 12.9 us
  local copies, waits for them, and re-layouts: 13.4 us -> 25.7 us
  waiting for transfers between devices: 93.5 us -> 81.5 us
  starting transfers between devices: 113 us -> 106 us
  Pallas kernels: 35.7 us -> 32.4 us
    all_to_all x2, waiting for transfers between devices: 33 us -> 18.4 us  [summed(): lax.all_to_all(pair, 'rep', split_axis=0, concat_axis=0, axis_index_group...]
    all_to_all x2, starting transfers between devices: 21.3 us -> 7.11 us  [summed(): lax.all_to_all(pair, 'rep', split_axis=0, concat_axis=0, axis_index_group...]
    all_to_all x1, waiting for transfers between devices: 0.01 us -> 13.2 us  [local(): lax.all_to_all(shards, 'rep', split_axis=0, concat_axis=0, tiled=True)]
    all_to_all x0 -> x1, blocking collectives: none -> 12.9 us  [across_x(): lax.all_to_all(blocks, 'ep', split_axis=0, concat_axis=0, axis_index_grou...]
    ppermute x16 -> x18, waiting for transfers between devices: 48.6 us -> 36.3 us  [the longest x7 26.3 us: step(): fwd = lax.ppermute(sent_fwd, 'ep', zperm(1))]
    ppermute x16 -> x18, starting transfers between devices: 61.2 us -> 72.4 us  [the longest x7 36.9 us: step(): back = lax.ppermute(sent_back, 'ep', zperm(-1))]
    dynamic_slice x0 -> x1, local copies, waits for them, and re-layouts: none -> 6.8 us  [summed(): kept = lax.dynamic_index_in_dim(part, core, 1, keepdims=False)]
    reshape x2, local copies, waits for them, and re-layouts: 2.85 us -> 7.68 us  [summed(): part.astype(jnp.bfloat16)]
  transfers between devices with their start and end apart: 27 -> 28, of which waited for: 15 -> 15; matrix products, arithmetic and copies ran while one was open for 14% -> 19% of each run, Pallas kernels for 12% -> 10%
where the time goes in v2:
time: 309 us; the launch traced here: 307 us
  starting transfers between devices  106 us (34%)
  waiting for transfers between devices  81.5 us (26%)
  Pallas kernels  32.4 us (10%)
  matrix products  28.1 us (9%)
  local copies, waits for them, and re-layouts  25.7 us (8%)
  between operations  14.6 us (5%)
  blocking collectives  12.9 us (4%)
  other arithmetic  6 us (2%)
    ppermute x7, starting transfers between devices, step(): back = lax.ppermute(sent_back, 'ep', zperm(-1))  36.9 us
    ppermute x7, waiting for transfers between devices, step(): fwd = lax.ppermute(sent_fwd, 'ep', zperm(1))  26.3 us
    all_to_all x5, starting transfers between devices, across_x(): lax.all_to_all(blocks, 'ep', split_axis=0, concat_axis=0, axis_index_grou...  19.7 us
    all_to_all x2, waiting for transfers between devices, summed(): lax.all_to_all(pair, 'rep', split_axis=0, concat_axis=0, axis_index_group...  18.4 us
    ppermute x7, starting transfers between devices, step(): fwd = lax.ppermute(sent_fwd, 'ep', zperm(1))  15.8 us
    pallas_call x2, Pallas kernels, mix(): pl.pallas_call(mix_body, out_shape=jax.ShapeDtypeStruct((NZ * TOK, width)...  13.8 us
    all_to_all x5, waiting for transfers between devices, across_x(): lax.all_to_all(blocks, 'ep', split_axis=0, concat_axis=0, axis_index_grou...  13.5 us
    all_to_all x1, waiting for transfers between devices, local(): lax.all_to_all(shards, 'rep', split_axis=0, concat_axis=0, tiled=True)  13.2 us
  transfers between devices with their start and end apart: 28, of which 15 were waited for; matrix products, arithmetic and copies ran while one was open for 19% of the time, Pallas kernels for 10%

profile of v2, /device:TPU:1, one launch (start us, length us, event | category | flops | bytes accessed | tf_op | source)
XLA Modules:
  0.0 306.9 jit_solution(14301453649898971313)
XLA Ops:
  8.9 4.4 %collective-permute-start = (bf16[136,1024]{1,0:T(8,128)(2,1)}, bf16[136,1024]{1,0:T(8,128)(2,1)S(1)}, u32[]{:S(2)}, u32[]{:S(2)}) collective-permute-start(bf16[136,1024]{1,0:T(8,128)(2,1)} %pack.1.refs_0_), channel_id=1, source_target_pairs={{0,8},{8,16},{16,24},{24,32},{32,40},{40,48},{48,56},{56,64},{64,7... | collective-permute-start | bytes 835592 | tf_op jit(solution)/shard_map/ppermute | solution.py:251
  13.2 9.5 %collective-permute-start.2 = (bf16[136,1024]{1,0:T(8,128)(2,1)}, bf16[136,1024]{1,0:T(8,128)(2,1)S(1)}, u32[]{:S(2)}, u32[]{:S(2)}) collective-permute-start(bf16[136,1024]{1,0:T(8,128)(2,1)} %pack.1.refs_0_), channel_id=1, source_target_pairs={{0,120},{8,0},{16,8},{24,16},{32,24},{40,32},{48,40},{56,48},{64,5... | collective-permute-start | bytes 835592 | tf_op jit(solution)/shard_map/ppermute | solution.py:252
  22.7 4.6 %collective-permute-done.refs_1_ = bf16[136,1024]{1,0:T(8,128)(2,1)S(1)} collective-permute-done((bf16[136,1024]{1,0:T(8,128)(2,1)}, bf16[136,1024]{1,0:T(8,128)(2,1)S(1)}, u32[]{:S(2)}, u32[]{:S(2)}) %collective-permute-start) | collective-permute-done | bytes 278560 | tf_op jit(solution)/shard_map/ppermute | solution.py:251
  29.3 4.6 %collective-permute-start.4 = (bf16[136,1024]{1,0:T(8,128)(2,1)S(1)}, bf16[136,1024]{1,0:T(8,128)(2,1)S(1)}, u32[]{:S(2)}, u32[]{:S(2)}) collective-permute-start(bf16[136,1024]{1,0:T(8,128)(2,1)S(1)} %collective-permute-done.2.refs_5_), channel_id=1, source_target_pairs={{0,120},{8,0},{16,8},{24,16},{32,24},{40,32},{48,40},{56,48},{64,5... | collective-permute-start | bytes 835592 | tf_op jit(solution)/shard_map/ppermute | solution.py:252
  35.1 2.4 broadcast_in_dim.12
  37.5 6.3 %all-to-all-start.1 = ((bf16[8,704,384]{2,1,0:T(8,128)(2,1)}), bf16[8,704,384]{2,1,0:T(8,128)(2,1)}, u32[]{:S(2)}, u32[]{:S(2)}) async-start(bf16[8,704,384]{2,1,0:T(8,128)(2,1)} %broadcast_in_dim.12), calls=%async_computation.1 | async-start | bytes 8650752 | tf_op jit(solution)/shard_map/all_to_all | solution.py:273
  45.7 4.6 %collective-permute-start.6 = (bf16[136,1024]{1,0:T(8,128)(2,1)S(1)}, bf16[136,1024]{1,0:T(8,128)(2,1)S(1)}, u32[]{:S(2)}, u32[]{:S(2)}) collective-permute-start(bf16[136,1024]{1,0:T(8,128)(2,1)S(1)} %collective-permute-done.4.refs_6_), channel_id=1, source_target_pairs={{0,120},{8,0},{16,8},{24,16},{32,24},{40,32},{48,40},{56,48},{64,5... | collective-permute-start | bytes 835592 | tf_op jit(solution)/shard_map/ppermute | solution.py:252
  50.3 4.7 %collective-permute-done.3.refs_3_ = bf16[136,1024]{1,0:T(8,128)(2,1)S(1)} collective-permute-done((bf16[136,1024]{1,0:T(8,128)(2,1)S(1)}, bf16[136,1024]{1,0:T(8,128)(2,1)S(1)}, u32[]{:S(2)}, u32[]{:S(2)}) %collective-permute-start.3) | collective-permute-done | bytes 278560 | tf_op jit(solution)/shard_map/ppermute | solution.py:251
  56.9 4.6 %collective-permute-start.8 = (bf16[136,1024]{1,0:T(8,128)(2,1)S(1)}, bf16[136,1024]{1,0:T(8,128)(2,1)S(1)}, u32[]{:S(2)}, u32[]{:S(2)}) collective-permute-start(bf16[136,1024]{1,0:T(8,128)(2,1)S(1)} %collective-permute-done.6.refs_7_), channel_id=1, source_target_pairs={{0,120},{8,0},{16,8},{24,16},{32,24},{40,32},{48,40},{56,48},{64,5... | collective-permute-start | bytes 835592 | tf_op jit(solution)/shard_map/ppermute | solution.py:252
  61.5 4.0 %collective-permute-done.5.refs_4_ = bf16[136,1024]{1,0:T(8,128)(2,1)S(1)} collective-permute-done((bf16[136,1024]{1,0:T(8,128)(2,1)S(1)}, bf16[136,1024]{1,0:T(8,128)(2,1)S(1)}, u32[]{:S(2)}, u32[]{:S(2)}) %collective-permute-start.5) | collective-permute-done | bytes 278560 | tf_op jit(solution)/shard_map/ppermute | solution.py:251
  68.1 4.6 %collective-permute-start.10 = (bf16[136,1024]{1,0:T(8,128)(2,1)S(1)}, bf16[136,1024]{1,0:T(8,128)(2,1)}, u32[]{:S(2)}, u32[]{:S(2)}) collective-permute-start(bf16[136,1024]{1,0:T(8,128)(2,1)S(1)} %collective-permute-done.8.refs_3_), channel_id=1, source_target_pairs={{0,120},{8,0},{16,8},{24,16},{32,24},{40,32},{48,40},{56,48},{64,5... | collective-permute-start | bytes 835592 | tf_op jit(solution)/shard_map/ppermute | solution.py:252
  72.7 2.5 collective-permute-done.7.refs_0_
  76.8 3.9 %pick.2 = (bf16[4,104,1024]{2,1,0:T(8,128)(2,1)}, s32[4,1024]{1,0:T(4,128)}, f32[4,1024]{1,0:T(4,128)}, f32[8,128,4]{2,1,0:T(8,128)}, f32[8,128,4]{2,1,0:T(8,128)}) custom-call(s32[1]{0:T(128)} %bitcast.place_ref, bf16[136,1024]{1,0:T(8,128)(2,1)} %pack.1.refs_0_, bf16[136,1024]{1,0:T(8,128)(2,1)} %copy-done.10, bf16[136,1024]{1,0:T(8,128)(2,1)} %copy-done.12, ...), custom_call_target="tpu_custom_call" | custom-call | flops 872415232 | bytes 2949120 | tf_op jit(solution)/shard_map/pick/pallas_call | solution.py:129
  80.8 13.2 %all-to-all-done.1 = bf16[8,704,384]{2,1,0:T(8,128)(2,1)} async-done(((bf16[8,704,384]{2,1,0:T(8,128)(2,1)}), bf16[8,704,384]{2,1,0:T(8,128)(2,1)}, u32[]{:S(2)}, u32[]{:S(2)}) %all-to-all-start.1) | async-done | bytes 4325408 | tf_op jit(solution)/shard_map/all_to_all | solution.py:273
  93.9 4.2 %all-to-all-start = ((bf16[4,104,1024]{2,1,0:T(8,128)(2,1)}), bf16[4,104,1024]{2,1,0:T(8,128)(2,1)}, u32[]{:S(2)}, u32[]{:S(2)}) async-start(bf16[4,104,1024]{2,1,0:T(8,128)(2,1)} %get-tuple-element.41), calls=%async_computation | async-start | bytes 1703936 | tf_op jit(solution)/shard_map/all_to_all | solution.py:226
  100.1 4.6 %collective-permute-start.11 = (bf16[136,1024]{1,0:T(8,128)(2,1)}, bf16[136,1024]{1,0:T(8,128)(2,1)}, u32[]{:S(2)}, u32[]{:S(2)}) collective-permute-start(bf16[136,1024]{1,0:T(8,128)(2,1)} %collective-permute-done.10.refs_4_), channel_id=1, source_target_pairs={{0,120},{8,0},{16,8},{24,16},{32,24},{40,32},{48,40},{56,48},{64,5... | collective-permute-start | bytes 835592 | tf_op jit(solution)/shard_map/ppermute | solution.py:252
  104.7 3.7 %slice_bitcast_fusion = (bf16[8,88,8,128]{3,2,1,0:T(8,128)(2,1)S(1)}, bf16[8,88,8,128]{3,2,1,0:T(8,128)(2,1)S(1)}, bf16[8,88,8,128]{3,2,1,0:T(8,128)(2,1)}) fusion(bf16[8,704,384]{2,1,0:T(8,128)(2,1)} %all-to-all-done.1), kind=kLoop, calls=%fused_computation.18 | loop fusion | bytes 8650752
  110.2 2.6 divide_multiply_fusion.1
  112.8 2.5 fusion.45
  117.1 4.2 %all-to-all-start.2 = ((bf16[4,104,1024]{2,1,0:T(8,128)(2,1)}), bf16[4,104,1024]{2,1,0:T(8,128)(2,1)}, u32[]{:S(2)}, u32[]{:S(2)}) async-start(bf16[4,104,1024]{2,1,0:T(8,128)(2,1)} %bitcast.115), calls=%async_computation.2 | async-start | bytes 1703936 | tf_op jit(solution)/shard_map/all_to_all | solution.py:226
  123.2 4.6 %collective-permute-start.13 = (bf16[136,1024]{1,0:T(8,128)(2,1)}, bf16[136,1024]{1,0:T(8,128)(2,1)}, u32[]{:S(2)}, u32[]{:S(2)}) collective-permute-start(bf16[136,1024]{1,0:T(8,128)(2,1)} %collective-permute-done.11.refs_5_), channel_id=1, source_target_pairs={{0,120},{8,0},{16,8},{24,16},{32,24},{40,32},{48,40},{56,48},{64,5... | collective-permute-start | bytes 835592 | tf_op jit(solution)/shard_map/ppermute | solution.py:252
  127.8 10.5 %collective-permute-done.12.refs_2_ = bf16[136,1024]{1,0:T(8,128)(2,1)} collective-permute-done((bf16[136,1024]{1,0:T(8,128)(2,1)}, bf16[136,1024]{1,0:T(8,128)(2,1)}, u32[]{:S(2)}, u32[]{:S(2)}) %collective-permute-start.12) | collective-permute-done | bytes 278560 | tf_op jit(solution)/shard_map/ppermute | solution.py:251
  140.3 5.3 %collective-permute-start.15 = (bf16[72,1024]{1,0:T(8,128)(2,1)S(1)}, bf16[72,1024]{1,0:T(8,128)(2,1)}, u32[]{:S(2)}, u32[]{:S(2)}) collective-permute-start(bf16[72,1024]{1,0:T(8,128)(2,1)S(1)} %slice.28), channel_id=1, source_target_pairs={{0,120},{8,0},{16,8},{24,16},{32,24},{40,32},{48,40},{56,48},{64,5... | collective-permute-start | bytes 442376 | tf_op jit(solution)/shard_map/ppermute | solution.py:292
  148.5 7.3 %collective-permute-done.14.refs_7_ = bf16[64,1024]{1,0:T(8,128)(2,1)S(1)} collective-permute-done((bf16[64,1024]{1,0:T(8,128)(2,1)S(1)}, bf16[64,1024]{1,0:T(8,128)(2,1)S(1)}, u32[]{:S(2)}, u32[]{:S(2)}) %collective-permute-start.14) | collective-permute-done | bytes 131104 | tf_op jit(solution)/shard_map/ppermute | solution.py:291
  156.5 3.9 %pick.3 = (bf16[4,104,1024]{2,1,0:T(8,128)(2,1)}, s32[4,1024]{1,0:T(4,128)}, f32[4,1024]{1,0:T(4,128)}, f32[8,128,4]{2,1,0:T(8,128)}, f32[8,128,4]{2,1,0:T(8,128)}) custom-call(s32[1]{0:T(128)} %bitcast.place_ref, bf16[136,1024]{1,0:T(8,128)(2,1)} %collective-permute-done.7.refs_0_, bf16[136,1024]{1,0:T(8,128)(2,1)} %collective-permute-done.9.refs_1_, ...), custom_call_target="tpu_custom_call" | custom-call | flops 872415232 | bytes 2949120 | tf_op jit(solution)/shard_map/pick/pallas_call | solution.py:129
  160.4 12.9 %all_to_all.45 = bf16[4,104,1024]{2,1,0:T(8,128)(2,1)S(1)} all-to-all(bf16[4,104,1024]{2,1,0:T(8,128)(2,1)} %get-tuple-element.54), channel_id=1, replica_groups={{0,128,256,384},{8,136,264,392},{16,144,272,400},{24,152,280,408},{32,1..., dimensions={0} | all-to-all | bytes 1703936 | tf_op jit(solution)/shard_map/all_to_all | solution.py:226
  177.1 3.6 %all-to-all-start.4 = ((bf16[4,104,1024]{2,1,0:T(8,128)(2,1)}), bf16[4,104,1024]{2,1,0:T(8,128)(2,1)S(1)}, u32[]{:S(2)}, u32[]{:S(2)}) async-start(bf16[4,104,1024]{2,1,0:T(8,128)(2,1)} %bitcast.14), calls=%async_computation.4 | async-start | bytes 1703936 | tf_op jit(solution)/shard_map/all_to_all | solution.py:226
  181.6 6.9 %mix.2.refs_0_ = bf16[2048,1024]{1,0:T(8,128)(2,1)} custom-call(s32[8]{0:T(128)} %get-tuple-element.70.dest_ref.source_ref, f32[8,128,4]{2,1,0:T(8,128)} %get-tuple-element.55.code_ref, f32[8,128,4]{2,1,0:T(8,128)} %get-tuple-element.56.gate_ref, bf16[4,104,1024]{2,1,0:T(8,128)(2,1)} %all-to-all-done.2.rows_ref), custom_call_target="tpu_custom_call" | custom-call | flops 2147483648 | bytes 2949120 | tf_op jit(solution)/shard_map/mix/pallas_call | solution.py:205
  190.3 6.9 %mix.3 = bf16[2048,1024]{1,0:T(8,128)(2,1)} custom-call(s32[8]{0:T(128)} %get-tuple-element.71.dest_ref.source_ref, f32[8,128,4]{2,1,0:T(8,128)} %get-tuple-element.52.code_ref, f32[8,128,4]{2,1,0:T(8,128)} %get-tuple-element.53.gate_ref, bf16[4,104,1024]{2,1,0:T(8,128)(2,1)} %copy-done.3, bf16[2048,1024]{1,0:T(8,128)(2,1)} %mix.2.refs_0_), custom_call_target="tpu_custom_call", output_to_operand_aliasing={{}: (4, {})} | custom-call | flops 2147483648 | bytes 2949120 | tf_op jit(solution)/shard_map/mix/pallas_call | solution.py:205
  197.3 4.5 %pick_weighted.2 = bf16[4,104,1024]{2,1,0:T(8,128)(2,1)} custom-call(s32[8]{0:T(128)} %get-tuple-element.70.dest_ref.source_ref, s32[4,1024]{1,0:T(4,128)} %get-tuple-element.58.code_ref, f32[4,1024]{1,0:T(4,128)} %get-tuple-element.59.gate_ref, ...), custom_call_target="tpu_custom_call" | custom-call | flops 872415232 | bytes 2949120 | tf_op jit(solution)/shard_map/pick_weighted/pallas_call | solution.py:151
  201.8 3.5 %all-to-all-start.5 = ((bf16[4,104,1024]{2,1,0:T(8,128)(2,1)}), bf16[4,104,1024]{2,1,0:T(8,128)(2,1)S(1)}, u32[]{:S(2)}, u32[]{:S(2)}) async-start(bf16[4,104,1024]{2,1,0:T(8,128)(2,1)} %pick_weighted.2), calls=%async_computation.6 | async-start | bytes 1703936 | tf_op jit(solution)/shard_map/all_to_all | solution.py:226
  205.3 4.5 %pick_weighted.3 = bf16[4,104,1024]{2,1,0:T(8,128)(2,1)} custom-call(s32[8]{0:T(128)} %get-tuple-element.71.dest_ref.source_ref, s32[4,1024]{1,0:T(4,128)} %get-tuple-element.61.code_ref, f32[4,1024]{1,0:T(4,128)} %get-tuple-element.62.gate_ref, ...), custom_call_target="tpu_custom_call" | custom-call | flops 872415232 | bytes 2949120 | tf_op jit(solution)/shard_map/pick_weighted/pallas_call | solution.py:151
  209.8 4.1 %all-to-all-done.5 = bf16[4,104,1024]{2,1,0:T(8,128)(2,1)S(1)} async-done(((bf16[4,104,1024]{2,1,0:T(8,128)(2,1)}), bf16[4,104,1024]{2,1,0:T(8,128)(2,1)S(1)}, u32[]{:S(2)}, u32[]{:S(2)}) %all-to-all-start.5) | async-done | bytes 852000 | tf_op jit(solution)/shard_map/all_to_all | solution.py:226
  214.0 4.2 %all-to-all-start.6 = ((bf16[4,104,1024]{2,1,0:T(8,128)(2,1)}), bf16[4,104,1024]{2,1,0:T(8,128)(2,1)}, u32[]{:S(2)}, u32[]{:S(2)}) async-start(bf16[4,104,1024]{2,1,0:T(8,128)(2,1)} %pick_weighted.3), calls=%async_computation.7 | async-start | bytes 1703936 | tf_op jit(solution)/shard_map/all_to_all | solution.py:226
  218.2 2.1 fusion.68
  220.3 6.6 %all-to-all-done.6 = bf16[4,104,1024]{2,1,0:T(8,128)(2,1)} async-done(((bf16[4,104,1024]{2,1,0:T(8,128)(2,1)}), bf16[4,104,1024]{2,1,0:T(8,128)(2,1)}, u32[]{:S(2)}, u32[]{:S(2)}) %all-to-all-start.6) | async-done | bytes 852000 | tf_op jit(solution)/shard_map/all_to_all | solution.py:226
  226.9 3.4 %add_convert_fusion = bf16[1024,704]{0,1:T(8,128)(2,1)} fusion(f32[1024,704]{0,1:T(8,128)S(1)} %fusion.68, bf16[416,1024]{1,0:T(8,128)(2,1)} %bitcast.16, bf16[416,704]{1,0:T(8,128)(2,1)} %copy-done.8), kind=kOutput, calls=%fused_computation | convolution fusion | flops 601227264 | bytes 5763072 | tf_op jit(solution)/shard_map/dot_general | solution.py:308
  230.4 3.9 %reshape.58 = bf16[4,2,128,704]{2,1,0,3:T(2,128)(2,1)S(1)} reshape(bf16[1024,704]{0,1:T(8,128)(2,1)} %add_convert_fusion) | data formatting | bytes 2883584 | tf_op jit(solution)/shard_map/reshape | solution.py:314
  234.3 5.8 %fusion.53 = f32[1024,704]{0,1:T(8,128)} fusion(bf16[416,1024]{1,0:T(8,128)(2,1)S(1)} %bitcast.114, f32[416,704]{1,0:T(8,128)} %copy-done.20, bf16[416,1024]{1,0:T(8,128)(2,1)} %bitcast.16, bf16[8,88,8,128]{3,2,1,0:T(8,128)(2,1)} %copy-done.4), kind=kOutput, calls=%fused_computation.43 | convolution fusion | flops 1200156672 | bytes 7200768 | tf_op jit(solution)/shard_map/dot_general | solution.py:309
  240.1 6.3 %add_convert_fusion.1 = bf16[1024,704]{0,1:T(8,128)(2,1)} fusion(f32[1024,704]{0,1:T(8,128)} %fusion.53, bf16[416,1024]{1,0:T(8,128)(2,1)} %bitcast.3, f32[416,704]{1,0:T(8,128)} %copy-done.19, bf16[416,1024]{1,0:T(8,128)(2,1)S(1)} %bitcast.111, bf16[8,88,8,128]{3,2,1,0:T(8,128)(2,1)} %copy-done.4), kind=kOutput, calls=%fused_computation.1 | convolution fusion | flops 1201598464 | bytes 8642560 | tf_op jit(solution)/shard_map/dot_general | solution.py:309
  246.3 3.8 %reshape.57 = bf16[4,2,128,704]{2,1,0,3:T(2,128)(2,1)S(1)} reshape(bf16[1024,704]{0,1:T(8,128)(2,1)} %add_convert_fusion.1) | data formatting | bytes 2883584 | tf_op jit(solution)/shard_map/reshape | solution.py:314
  250.2 6.8 %constant_dynamic-slice_fusion.1 = (bf16[4,1,128,704]{2,1,0,3:T(2,128)(2,1)}, bf16[4,1,128,704]{2,1,0,3:T(2,128)(2,1)S(1)}, bf16[4,1,128,704]{2,1,0,3:T(2,128)(2,1)S(1)}, bf16[4,1,128,704]{2,1,0,3:T(2,128)(2,1)S(1)}) fusion(bf16[4,2,128,704]{2,1,0,3:T(2,128)(2,1)S(1)} %reshape.58, s32[]{:T(128)S(6)} %select_n.29, s32[]{:T(128)S(6)} %select_n.30, ...), kind=kLoop, calls=%fused_computation.57 | loop fusion | bytes 5767176 | tf_op jit(solution)/shard_map/jit(dynamic_index_in_dim)/dynamic_slice | solution.py:315
  257.1 10.5 %collective-permute-start.16 = (bf16[4,128,704]{1,2,0:T(8,128)(2,1)S(1)}, bf16[4,128,704]{1,2,0:T(8,128)(2,1)S(1)}, u32[]{:S(2)}, u32[]{:S(2)}) collective-permute-start(bf16[4,128,704]{1,2,0:T(8,128)(2,1)S(1)} %bitcast.117), channel_id=1, source_target_pairs={{0,1},{1,0},{2,3},{3,2},{4,5},{5,4},{6,7},{7,6},{8,9},{9,8},{10,11... | collective-permute-start | bytes 2162696 | tf_op jit(solution)/shard_map/ppermute | solution.py:318
  270.7 3.6 %all-to-all-start.7 = ((bf16[4,128,704]{1,2,0:T(8,128)(2,1)}), bf16[4,128,704]{1,2,0:T(8,128)(2,1)S(1)}, u32[]{:S(2)}, u32[]{:S(2)}) async-start(bf16[4,128,704]{1,2,0:T(8,128)(2,1)} %fusion.17), calls=%async_computation.8 | async-start | bytes 1441792 | tf_op jit(solution)/shard_map/all_to_all | solution.py:321
  274.3 2.1 fusion.16
  276.5 9.0 %all-to-all-done.7 = bf16[4,128,704]{1,2,0:T(8,128)(2,1)S(1)} async-done(((bf16[4,128,704]{1,2,0:T(8,128)(2,1)}), bf16[4,128,704]{1,2,0:T(8,128)(2,1)S(1)}, u32[]{:S(2)}, u32[]{:S(2)}) %all-to-all-start.7) | async-done | bytes 720928 | tf_op jit(solution)/shard_map/all_to_all | solution.py:321
  285.5 3.5 %all-to-all-start.8 = ((bf16[4,128,704]{1,2,0:T(8,128)(2,1)}), bf16[4,128,704]{1,2,0:T(8,128)(2,1)S(1)}, u32[]{:S(2)}, u32[]{:S(2)}) async-start(bf16[4,128,704]{1,2,0:T(8,128)(2,1)} %fusion.16), calls=%async_computation.9 | async-start | bytes 1441792 | tf_op jit(solution)/shard_map/all_to_all | solution.py:321
  289.8 9.5 %all-to-all-done.8 = bf16[4,128,704]{1,2,0:T(8,128)(2,1)S(1)} async-done(((bf16[4,128,704]{1,2,0:T(8,128)(2,1)}), bf16[4,128,704]{1,2,0:T(8,128)(2,1)S(1)}, u32[]{:S(2)}, u32[]{:S(2)}) %all-to-all-start.8) | async-done | bytes 720928 | tf_op jit(solution)/shard_map/all_to_all | solution.py:321
  (86 shorter events, 37.1 us)
Async XLA Ops:
  8.9 18.5 %collective-permute-start = (bf16[136,1024]{1,0:T(8,128)(2,1)}, bf16[136,1024]{1,0:T(8,128)(2,1)S(1)}, u32[]{:S(2)}, u32[]{:S(2)}) collective-permute-start(bf16[136,1024]{1,0:T(8,128)(2,1)} %pack.1.refs_0_), channel_id=1, source_target_pairs={{0,8},{8,16},{16,24},{24,32},{32,40},{40,48},{48,56},{56,64},{64,7... | collective-permute-start | bytes 835592 | tf_op jit(solution)/shard_map/ppermute | solution.py:251
  13.2 16.1 %collective-permute-start.2 = (bf16[136,1024]{1,0:T(8,128)(2,1)}, bf16[136,1024]{1,0:T(8,128)(2,1)S(1)}, u32[]{:S(2)}, u32[]{:S(2)}) collective-permute-start(bf16[136,1024]{1,0:T(8,128)(2,1)} %pack.1.refs_0_), channel_id=1, source_target_pairs={{0,120},{8,0},{16,8},{24,16},{32,24},{40,32},{48,40},{56,48},{64,5... | collective-permute-start | bytes 835592 | tf_op jit(solution)/shard_map/ppermute | solution.py:252
  27.4 10.1 %copy-start.10 = (bf16[136,1024]{1,0:T(8,128)(2,1)}, bf16[136,1024]{1,0:T(8,128)(2,1)S(1)}, u32[]{:S(2)}) copy-start(bf16[136,1024]{1,0:T(8,128)(2,1)S(1)} %collective-permute-done.refs_1_) | copy-start | bytes 835588
  27.4 16.4 %collective-permute-start.1 = (bf16[136,1024]{1,0:T(8,128)(2,1)S(1)}, bf16[136,1024]{1,0:T(8,128)(2,1)S(1)}, u32[]{:S(2)}, u32[]{:S(2)}) collective-permute-start(bf16[136,1024]{1,0:T(8,128)(2,1)S(1)} %collective-permute-done.refs_1_), channel_id=1, source_target_pairs={{0,8},{8,16},{16,24},{24,32},{32,40},{40,48},{48,56},{56,64},{64,7... | collective-permute-start | bytes 835592 | tf_op jit(solution)/shard_map/ppermute | solution.py:251
  29.3 8.2 %copy-start.11 = (bf16[136,1024]{1,0:T(8,128)(2,1)}, bf16[136,1024]{1,0:T(8,128)(2,1)S(1)}, u32[]{:S(2)}) copy-start(bf16[136,1024]{1,0:T(8,128)(2,1)S(1)} %collective-permute-done.2.refs_5_) | copy-start | bytes 835588
  29.3 16.4 %collective-permute-start.4 = (bf16[136,1024]{1,0:T(8,128)(2,1)S(1)}, bf16[136,1024]{1,0:T(8,128)(2,1)S(1)}, u32[]{:S(2)}, u32[]{:S(2)}) collective-permute-start(bf16[136,1024]{1,0:T(8,128)(2,1)S(1)} %collective-permute-done.2.refs_5_), channel_id=1, source_target_pairs={{0,120},{8,0},{16,8},{24,16},{32,24},{40,32},{48,40},{56,48},{64,5... | collective-permute-start | bytes 835592 | tf_op jit(solution)/shard_map/ppermute | solution.py:252
  37.5 56.5 %all-to-all-start.1 = ((bf16[8,704,384]{2,1,0:T(8,128)(2,1)}), bf16[8,704,384]{2,1,0:T(8,128)(2,1)}, u32[]{:S(2)}, u32[]{:S(2)}) async-start(bf16[8,704,384]{2,1,0:T(8,128)(2,1)} %broadcast_in_dim.12), calls=%async_computation.1 | async-start | bytes 8650752 | tf_op jit(solution)/shard_map/all_to_all | solution.py:273
  43.7 153.6 %all-gather.2.cloned.1.call-start = ((), (), s32[]{:S(2)}) async-start(), calls=%async_computation.11 | async-start | bytes 4456448 | tf_op jit(solution)/shard_map/all_gather | solution.py:281
  43.7 33.0 %copy-start.12 = (bf16[136,1024]{1,0:T(8,128)(2,1)}, bf16[136,1024]{1,0:T(8,128)(2,1)S(1)}, u32[]{:S(2)}) copy-start(bf16[136,1024]{1,0:T(8,128)(2,1)S(1)} %collective-permute-done.1.refs_2_) | copy-start | bytes 835588
  43.8 11.3 %collective-permute-start.3 = (bf16[136,1024]{1,0:T(8,128)(2,1)S(1)}, bf16[136,1024]{1,0:T(8,128)(2,1)S(1)}, u32[]{:S(2)}, u32[]{:S(2)}) collective-permute-start(bf16[136,1024]{1,0:T(8,128)(2,1)S(1)} %collective-permute-done.1.refs_2_), channel_id=1, source_target_pairs={{0,8},{8,16},{16,24},{24,32},{32,40},{40,48},{48,56},{56,64},{64,7... | collective-permute-start | bytes 835592 | tf_op jit(solution)/shard_map/ppermute | solution.py:251
  45.7 31.1 %copy-start.13 = (bf16[136,1024]{1,0:T(8,128)(2,1)}, bf16[136,1024]{1,0:T(8,128)(2,1)S(1)}, u32[]{:S(2)}) copy-start(bf16[136,1024]{1,0:T(8,128)(2,1)S(1)} %collective-permute-done.4.refs_6_) | copy-start | bytes 835588
  45.7 11.2 %collective-permute-start.6 = (bf16[136,1024]{1,0:T(8,128)(2,1)S(1)}, bf16[136,1024]{1,0:T(8,128)(2,1)S(1)}, u32[]{:S(2)}, u32[]{:S(2)}) collective-permute-start(bf16[136,1024]{1,0:T(8,128)(2,1)S(1)} %collective-permute-done.4.refs_6_), channel_id=1, source_target_pairs={{0,120},{8,0},{16,8},{24,16},{32,24},{40,32},{48,40},{56,48},{64,5... | collective-permute-start | bytes 835592 | tf_op jit(solution)/shard_map/ppermute | solution.py:252
  55.0 21.8 %copy-start.14 = (bf16[136,1024]{1,0:T(8,128)(2,1)}, bf16[136,1024]{1,0:T(8,128)(2,1)S(1)}, u32[]{:S(2)}) copy-start(bf16[136,1024]{1,0:T(8,128)(2,1)S(1)} %collective-permute-done.3.refs_3_) | copy-start | bytes 835588
  55.0 10.5 %collective-permute-start.5 = (bf16[136,1024]{1,0:T(8,128)(2,1)S(1)}, bf16[136,1024]{1,0:T(8,128)(2,1)S(1)}, u32[]{:S(2)}, u32[]{:S(2)}) collective-permute-start(bf16[136,1024]{1,0:T(8,128)(2,1)S(1)} %collective-permute-done.3.refs_3_), channel_id=1, source_target_pairs={{0,8},{8,16},{16,24},{24,32},{32,40},{40,48},{48,56},{56,64},{64,7... | collective-permute-start | bytes 835592 | tf_op jit(solution)/shard_map/ppermute | solution.py:251
  56.9 19.9 %copy-start.15 = (bf16[136,1024]{1,0:T(8,128)(2,1)}, bf16[136,1024]{1,0:T(8,128)(2,1)S(1)}, u32[]{:S(2)}) copy-start(bf16[136,1024]{1,0:T(8,128)(2,1)S(1)} %collective-permute-done.6.refs_7_) | copy-start | bytes 835588
  56.9 10.5 %collective-permute-start.8 = (bf16[136,1024]{1,0:T(8,128)(2,1)S(1)}, bf16[136,1024]{1,0:T(8,128)(2,1)S(1)}, u32[]{:S(2)}, u32[]{:S(2)}) collective-permute-start(bf16[136,1024]{1,0:T(8,128)(2,1)S(1)} %collective-permute-done.6.refs_7_), channel_id=1, source_target_pairs={{0,120},{8,0},{16,8},{24,16},{32,24},{40,32},{48,40},{56,48},{64,5... | collective-permute-start | bytes 835592 | tf_op jit(solution)/shard_map/ppermute | solution.py:252
  65.5 11.3 %copy-start.16 = (bf16[136,1024]{1,0:T(8,128)(2,1)}, bf16[136,1024]{1,0:T(8,128)(2,1)S(1)}, u32[]{:S(2)}) copy-start(bf16[136,1024]{1,0:T(8,128)(2,1)S(1)} %collective-permute-done.5.refs_4_) | copy-start | bytes 835588
  65.5 9.7 %collective-permute-start.7 = (bf16[136,1024]{1,0:T(8,128)(2,1)S(1)}, bf16[136,1024]{1,0:T(8,128)(2,1)}, u32[]{:S(2)}, u32[]{:S(2)}) collective-permute-start(bf16[136,1024]{1,0:T(8,128)(2,1)S(1)} %collective-permute-done.5.refs_4_), channel_id=1, source_target_pairs={{0,8},{8,16},{16,24},{24,32},{32,40},{40,48},{48,56},{56,64},{64,7... | collective-permute-start | bytes 835592 | tf_op jit(solution)/shard_map/ppermute | solution.py:251
  67.4 0.7 copy-start.9
  68.1 8.6 %collective-permute-start.10 = (bf16[136,1024]{1,0:T(8,128)(2,1)S(1)}, bf16[136,1024]{1,0:T(8,128)(2,1)}, u32[]{:S(2)}, u32[]{:S(2)}) collective-permute-start(bf16[136,1024]{1,0:T(8,128)(2,1)S(1)} %collective-permute-done.8.refs_3_), channel_id=1, source_target_pairs={{0,120},{8,0},{16,8},{24,16},{32,24},{40,32},{48,40},{56,48},{64,5... | collective-permute-start | bytes 835592 | tf_op jit(solution)/shard_map/ppermute | solution.py:252
  93.9 16.3 %all-to-all-start = ((bf16[4,104,1024]{2,1,0:T(8,128)(2,1)}), bf16[4,104,1024]{2,1,0:T(8,128)(2,1)}, u32[]{:S(2)}, u32[]{:S(2)}) async-start(bf16[4,104,1024]{2,1,0:T(8,128)(2,1)} %get-tuple-element.41), calls=%async_computation | async-start | bytes 1703936 | tf_op jit(solution)/shard_map/all_to_all | solution.py:226
  98.2 18.9 %collective-permute-start.9 = (bf16[136,1024]{1,0:T(8,128)(2,1)}, bf16[136,1024]{1,0:T(8,128)(2,1)}, u32[]{:S(2)}, u32[]{:S(2)}) collective-permute-start(bf16[136,1024]{1,0:T(8,128)(2,1)} %collective-permute-done.7.refs_0_), channel_id=1, source_target_pairs={{0,8},{8,16},{16,24},{24,32},{32,40},{40,48},{48,56},{56,64},{64,7... | collective-permute-start | bytes 835592 | tf_op jit(solution)/shard_map/ppermute | solution.py:251
  100.1 17.0 %collective-permute-start.11 = (bf16[136,1024]{1,0:T(8,128)(2,1)}, bf16[136,1024]{1,0:T(8,128)(2,1)}, u32[]{:S(2)}, u32[]{:S(2)}) collective-permute-start(bf16[136,1024]{1,0:T(8,128)(2,1)} %collective-permute-done.10.refs_4_), channel_id=1, source_target_pairs={{0,120},{8,0},{16,8},{24,16},{32,24},{40,32},{48,40},{56,48},{64,5... | collective-permute-start | bytes 835592 | tf_op jit(solution)/shard_map/ppermute | solution.py:252
  108.3 66.9 %copy-start.4 = (bf16[8,88,8,128]{3,2,1,0:T(8,128)(2,1)}, bf16[8,88,8,128]{3,2,1,0:T(8,128)(2,1)S(1)}, u32[]{:S(2)}) copy-start(bf16[8,88,8,128]{3,2,1,0:T(8,128)(2,1)S(1)} %get-tuple-element.63) | copy-start | bytes 4325380
  112.8 2.5 copy-start.19
  117.1 22.3 %all-to-all-start.2 = ((bf16[4,104,1024]{2,1,0:T(8,128)(2,1)}), bf16[4,104,1024]{2,1,0:T(8,128)(2,1)}, u32[]{:S(2)}, u32[]{:S(2)}) async-start(bf16[4,104,1024]{2,1,0:T(8,128)(2,1)} %bitcast.115), calls=%async_computation.2 | async-start | bytes 1703936 | tf_op jit(solution)/shard_map/all_to_all | solution.py:226
  121.3 17.0 %collective-permute-start.12 = (bf16[136,1024]{1,0:T(8,128)(2,1)}, bf16[136,1024]{1,0:T(8,128)(2,1)}, u32[]{:S(2)}, u32[]{:S(2)}) collective-permute-start(bf16[136,1024]{1,0:T(8,128)(2,1)} %collective-permute-done.9.refs_1_), channel_id=1, source_target_pairs={{0,8},{8,16},{16,24},{24,32},{32,40},{40,48},{48,56},{56,64},{64,7... | collective-permute-start | bytes 835592 | tf_op jit(solution)/shard_map/ppermute | solution.py:251
  123.2 16.2 %collective-permute-start.13 = (bf16[136,1024]{1,0:T(8,128)(2,1)}, bf16[136,1024]{1,0:T(8,128)(2,1)}, u32[]{:S(2)}, u32[]{:S(2)}) collective-permute-start(bf16[136,1024]{1,0:T(8,128)(2,1)} %collective-permute-done.11.refs_5_), channel_id=1, source_target_pairs={{0,120},{8,0},{16,8},{24,16},{32,24},{40,32},{48,40},{56,48},{64,5... | collective-permute-start | bytes 835592 | tf_op jit(solution)/shard_map/ppermute | solution.py:252
  140.3 16.1 %collective-permute-start.15 = (bf16[72,1024]{1,0:T(8,128)(2,1)S(1)}, bf16[72,1024]{1,0:T(8,128)(2,1)}, u32[]{:S(2)}, u32[]{:S(2)}) collective-permute-start(bf16[72,1024]{1,0:T(8,128)(2,1)S(1)} %slice.28), channel_id=1, source_target_pairs={{0,120},{8,0},{16,8},{24,16},{32,24},{40,32},{48,40},{56,48},{64,5... | collective-permute-start | bytes 442376 | tf_op jit(solution)/shard_map/ppermute | solution.py:292
  146.6 9.2 %collective-permute-start.14 = (bf16[64,1024]{1,0:T(8,128)(2,1)S(1)}, bf16[64,1024]{1,0:T(8,128)(2,1)S(1)}, u32[]{:S(2)}, u32[]{:S(2)}) collective-permute-start(bf16[64,1024]{1,0:T(8,128)(2,1)S(1)} %slice.27), channel_id=1, source_target_pairs={{0,8},{8,16},{16,24},{24,32},{32,40},{40,48},{48,56},{56,64},{64,7... | collective-permute-start | bytes 393224 | tf_op jit(solution)/shard_map/ppermute | solution.py:291
  160.4 12.9 %copy-start.5 = (bf16[8,88,8,128]{3,2,1,0:T(8,128)(2,1)S(1)}, bf16[8,88,8,128]{3,2,1,0:T(8,128)(2,1)}, u32[]{:S(2)}) copy-start(bf16[8,88,8,128]{3,2,1,0:T(8,128)(2,1)} %get-tuple-element.65) | copy-start | bytes 4325380
  173.3 1.0 copy-start.6
  174.3 1.1 copy-start.20
  175.4 1.8 copy-start.8
  177.1 3.9 %copy-start.18 = (s32[16]{0:T(128)S(1)}, s32[16]{0:T(128)}, u32[]{:S(2)}) copy-start(s32[16]{0:T(128)} %constant.69) | copy-start | bytes 196
  177.1 12.3 %all-to-all-start.4 = ((bf16[4,104,1024]{2,1,0:T(8,128)(2,1)}), bf16[4,104,1024]{2,1,0:T(8,128)(2,1)S(1)}, u32[]{:S(2)}, u32[]{:S(2)}) async-start(bf16[4,104,1024]{2,1,0:T(8,128)(2,1)} %bitcast.14), calls=%async_computation.4 | async-start | bytes 1703936 | tf_op jit(solution)/shard_map/all_to_all | solution.py:226
  180.8 119.3 %reduce-scatter.2.cloned.1.call-start = ((), (), s32[]{:S(2)}) async-start(), calls=%async_computation.10 | async-start | bytes 4456448 | tf_op jit(solution)/shard_map/reduce_scatter | solution.py:298
  189.4 0.9 copy-start.3
  201.8 12.2 %all-to-all-start.5 = ((bf16[4,104,1024]{2,1,0:T(8,128)(2,1)}), bf16[4,104,1024]{2,1,0:T(8,128)(2,1)S(1)}, u32[]{:S(2)}, u32[]{:S(2)}) async-start(bf16[4,104,1024]{2,1,0:T(8,128)(2,1)} %pick_weighted.2), calls=%async_computation.6 | async-start | bytes 1703936 | tf_op jit(solution)/shard_map/all_to_all | solution.py:226
  214.0 4.2 %copy-start = (bf16[4,104,1024]{2,1,0:T(8,128)(2,1)}, bf16[4,104,1024]{2,1,0:T(8,128)(2,1)S(1)}, u32[]{:S(2)}) copy-start(bf16[4,104,1024]{2,1,0:T(8,128)(2,1)S(1)} %all-to-all-done.5) | copy-start | bytes 2555908
  214.0 13.0 %all-to-all-start.6 = ((bf16[4,104,1024]{2,1,0:T(8,128)(2,1)}), bf16[4,104,1024]{2,1,0:T(8,128)(2,1)}, u32[]{:S(2)}, u32[]{:S(2)}) async-start(bf16[4,104,1024]{2,1,0:T(8,128)(2,1)} %pick_weighted.3), calls=%async_computation.7 | async-start | bytes 1703936 | tf_op jit(solution)/shard_map/all_to_all | solution.py:226
  230.4 3.9 %copy-start.7 = (bf16[4,104,1024]{2,1,0:T(8,128)(2,1)S(1)}, bf16[4,104,1024]{2,1,0:T(8,128)(2,1)}, u32[]{:S(2)}) copy-start(bf16[4,104,1024]{2,1,0:T(8,128)(2,1)} %copy-done.6) | copy-start | bytes 2555908
  234.3 5.8 %copy-start.1 = (bf16[4,104,1024]{2,1,0:T(8,128)(2,1)S(1)}, bf16[4,104,1024]{2,1,0:T(8,128)(2,1)}, u32[]{:S(2)}) copy-start(bf16[4,104,1024]{2,1,0:T(8,128)(2,1)} %copy-done) | copy-start | bytes 2555908
  257.1 12.6 %collective-permute-start.16 = (bf16[4,128,704]{1,2,0:T(8,128)(2,1)S(1)}, bf16[4,128,704]{1,2,0:T(8,128)(2,1)S(1)}, u32[]{:S(2)}, u32[]{:S(2)}) collective-permute-start(bf16[4,128,704]{1,2,0:T(8,128)(2,1)S(1)} %bitcast.117), channel_id=1, source_target_pairs={{0,1},{1,0},{2,3},{3,2},{4,5},{5,4},{6,7},{7,6},{8,9},{9,8},{10,11... | collective-permute-start | bytes 2162696 | tf_op jit(solution)/shard_map/ppermute | solution.py:318
  267.7 6.6 %collective-permute-start.17 = (bf16[4,128,704]{1,2,0:T(8,128)(2,1)S(1)}, bf16[4,128,704]{1,2,0:T(8,128)(2,1)}, u32[]{:S(2)}, u32[]{:S(2)}) collective-permute-start(bf16[4,128,704]{1,2,0:T(8,128)(2,1)S(1)} %bitcast.116), channel_id=1, source_target_pairs={{0,1},{1,0},{2,3},{3,2},{4,5},{5,4},{6,7},{7,6},{8,9},{9,8},{10,11... | collective-permute-start | bytes 2162696 | tf_op jit(solution)/shard_map/ppermute | solution.py:318
  270.7 3.6 %copy-start.2 = (bf16[4,1,128,704]{2,1,0,3:T(2,128)(2,1)S(1)}, bf16[4,1,128,704]{2,1,0,3:T(2,128)(2,1)}, u32[]{:S(2)}) copy-start(bf16[4,1,128,704]{2,1,0,3:T(2,128)(2,1)} %get-tuple-element.66) | copy-start | bytes 2162692
  270.7 14.8 %all-to-all-start.7 = ((bf16[4,128,704]{1,2,0:T(8,128)(2,1)}), bf16[4,128,704]{1,2,0:T(8,128)(2,1)S(1)}, u32[]{:S(2)}, u32[]{:S(2)}) async-start(bf16[4,128,704]{1,2,0:T(8,128)(2,1)} %fusion.17), calls=%async_computation.8 | async-start | bytes 1441792 | tf_op jit(solution)/shard_map/all_to_all | solution.py:321
  285.5 13.8 %all-to-all-start.8 = ((bf16[4,128,704]{1,2,0:T(8,128)(2,1)}), bf16[4,128,704]{1,2,0:T(8,128)(2,1)S(1)}, u32[]{:S(2)}, u32[]{:S(2)}) async-start(bf16[4,128,704]{1,2,0:T(8,128)(2,1)} %fusion.16), calls=%async_computation.9 | async-start | bytes 1441792 | tf_op jit(solution)/shard_map/all_to_all | solution.py:321
  (1 other events, 0.7 us)
Sparse Core Ops, SparseCore 0:
  76.9 82.0 all-gather.1
  197.4 70.6 reduce-scatter.1

commit v3 on v1

v3 whole, which is shorter than its diff:
```python
import functools

import jax
import jax.numpy as jnp
from jax import lax
from jax.experimental import pallas as pl
from jax.experimental.pallas import tpu as pltpu
from jax.sharding import PartitionSpec as P


NX, NZ = 4, 16
CAP = 13
TOP = 6
TOK = 128
EXTRA = 8
NEAR = (0, 1, 2, 3, 4, -1, -2, -3)
FAR = (5, 6, 7, -4, -5, -6, -7, 8)
COUNT = len(NEAR)
ROWS = CAP * COUNT
PAD = 128
STEP = 112
ZG = [[x * NZ + z for z in range(NZ)] for x in range(NX)]
XG = [[x * NZ + z for x in range(NX)] for z in range(NZ)]


def zperm(d):
    return [(x * NZ + z, x * NZ + (z + d) % NZ) for x in range(NX) for z in range(NZ)]


def pack_body(tokens_ref, ids_ref, gates_ref, out_ref):
    out_ref[:TOK, :] = tokens_ref[...]
    gates = gates_ref[...]
    high = gates.astype(jnp.bfloat16).astype(jnp.float32)
    mid = (gates - high).astype(jnp.bfloat16).astype(jnp.float32)
    low = gates - high - mid
    ids = ids_ref[...].astype(jnp.float32)
    blank = jnp.zeros((EXTRA - 4, TOK), jnp.float32)
    for k in range(TOP):
        at = slice(k, k + 1)
        rows = jnp.concatenate([ids[at], high[at], mid[at], low[at], blank], axis=0)
        out_ref[TOK:, k * TOK : (k + 1) * TOK] = rows.astype(jnp.bfloat16)
    rest = out_ref.shape[1] - TOP * TOK
    out_ref[TOK:, TOP * TOK :] = jnp.zeros((EXTRA, rest), jnp.bfloat16)


def pack(tokens, ids, gates):
    return pl.pallas_call(
        pack_body,
        out_shape=jax.ShapeDtypeStruct((TOK + EXTRA, tokens.shape[1]), jnp.bfloat16),
        cost_estimate=pl.CostEstimate(flops=0, bytes_accessed=4 * TOK * tokens.shape[1], transcendentals=0),
        name="pack",
    )(tokens, ids.T, gates.T)


def pick_rows(code, gate, all_rows, out_ref, weighted):
    slot = lax.broadcasted_iota(jnp.int32, (STEP, all_rows.shape[0]), 0)
    hits = [slot == code[j : j + 1, :] for j in range(NX)]
    ones = jnp.concatenate([jnp.where(h, 1.0, 0.0).astype(jnp.bfloat16) for h in hits], axis=0)
    got = jnp.dot(ones, all_rows, preferred_element_type=jnp.float32)
    for j in range(NX):
        part = got[j * STEP : j * STEP + ROWS]
        if weighted:
            scale = jnp.sum(jnp.where(hits[j], gate[j : j + 1, :], 0.0), axis=1, keepdims=True)
            part = part * scale[:ROWS]
        out_ref[j] = part.astype(jnp.bfloat16)


def pick_body(place_ref, *refs, spots):
    chunks, (out_ref, code_ref, gate_ref, code_t_ref, gate_t_ref, stage, extra, found) = refs[:-8], refs[-8:]
    for c, (n, row) in zip(chunks, spots):
        end = row + c.shape[0]
        if end <= TOK:
            stage[n * TOK + row : n * TOK + end, :] = c[...]
        else:
            stage[n * TOK + row : (n + 1) * TOK, :] = c[: TOK - row, :]
            extra[n] = c[TOK - row :, :].astype(jnp.float32)
    mine = place_ref[0] + NZ * lax.broadcasted_iota(jnp.int32, (NX, TOK), 0)
    mine = mine.astype(jnp.float32)

    def match(n, carry):
        rows = extra[n]
        hit = jnp.zeros((NX, TOK), jnp.float32)
        weight = jnp.zeros((NX, TOK), jnp.float32)
        for k in range(TOP):
            part = rows[0:4, k * TOK : (k + 1) * TOK]
            same = part[0:1] == mine
            hit = jnp.where(same, 1.0, hit)
            weight = jnp.where(same, part[1:2] + part[2:3] + part[3:4], weight)
        found[0, n] = hit
        found[1, n] = weight
        return carry

    lax.fori_loop(0, COUNT, match, 0)
    hits = jnp.concatenate([found[0, n] for n in range(COUNT)], axis=0)
    weights = jnp.concatenate([found[1, n] for n in range(COUNT)], axis=0)
    shape = (TOK, TOK)
    earlier = lax.broadcasted_iota(jnp.int32, shape, 0) < lax.broadcasted_iota(jnp.int32, shape, 1)
    position = jnp.dot(
        hits.astype(jnp.bfloat16),
        jnp.where(earlier, 1.0, 0.0).astype(jnp.bfloat16),
        preferred_element_type=jnp.float32,
    )
    first = CAP * (lax.broadcasted_iota(jnp.int32, (NX * COUNT, TOK), 0) // NX)
    codes = jnp.where(hits > 0, position.astype(jnp.int32) + first, -1)
    codes_f = codes.astype(jnp.float32)
    fill = jnp.zeros((TOK - NX * COUNT, TOK), jnp.float32)
    code_t = jnp.concatenate([codes_f, fill], axis=0).T
    gate_t = jnp.concatenate([weights, fill], axis=0).T
    for n in range(COUNT):
        at = slice(n * NX, (n + 1) * NX)
        code_ref[:, n * TOK : (n + 1) * TOK] = codes[at]
        gate_ref[:, n * TOK : (n + 1) * TOK] = weights[at]
        code_t_ref[n] = code_t[:, at]
        gate_t_ref[n] = gate_t[:, at]
    pick_rows(code_ref[...], None, stage[...], out_ref, False)


def pick_cost(rows, width):
    return pl.CostEstimate(
        flops=2 * NX * ROWS * rows * width, bytes_accessed=2 * (rows + NX * ROWS) * width, transcendentals=0
    )


def placed(groups):
    pieces, spots = [], []
    for n, group in enumerate(groups):
        row = 0
        for piece in group:
            pieces.append(piece)
            spots.append((n, row))
            row += piece.shape[0]
    return pieces, spots


def pick(place, groups):
    pieces, spots = placed(groups)
    width = pieces[0].shape[1]
    rows = COUNT * TOK
    shapes = [((NX, ROWS, width), jnp.bfloat16), ((NX, rows), jnp.int32), ((NX, rows), jnp.float32)]
    shapes += [((COUNT, TOK, NX), jnp.float32)] * 2
    return pl.pallas_call(
        functools.partial(pick_body, spots=spots),
        out_shape=[jax.ShapeDtypeStruct(s, t) for s, t in shapes],
        in_specs=[pl.BlockSpec(memory_space=pltpu.SMEM)] + [pl.BlockSpec(memory_space=pltpu.VMEM)] * len(pieces),
        scratch_shapes=[
            pltpu.VMEM((rows, width), jnp.bfloat16),
            pltpu.VMEM((COUNT, EXTRA, width), jnp.float32),
            pltpu.VMEM((2, COUNT, NX, TOK), jnp.float32),
        ],
        cost_estimate=pick_cost(rows, width),
        name="pick",
    )(place, *pieces)


def pick_weighted_body(code_ref, gate_ref, *refs, spots):
    chunks, out_ref, stage = refs[:-2], refs[-2], refs[-1]
    for c, (n, row) in zip(chunks, spots):
        stage[n * TOK + row : n * TOK + row + c.shape[0], :] = c[...]
    pick_rows(code_ref[...], gate_ref[...], stage[...], out_ref, True)


def pick_weighted(code, gate, groups):
    pieces, spots = placed(groups)
    width = pieces[0].shape[1]
    rows = COUNT * TOK
    return pl.pallas_call(
        functools.partial(pick_weighted_body, spots=spots),
        out_shape=jax.ShapeDtypeStruct((NX, ROWS, width), jnp.bfloat16),
        scratch_shapes=[pltpu.VMEM((rows, width), jnp.bfloat16)],
        cost_estimate=pick_cost(rows, width),
        name="pick_weighted",
    )(code, gate, *pieces)


def mix_body(dest_ref, code_ref, gate_ref, rows_ref, *refs):
    out_ref, stage, weights, ready, sems = refs[-5:]
    width = stage.shape[1]
    half = NX * PAD
    blank = jnp.zeros((PAD - ROWS, width), jnp.bfloat16)
    for j in range(NX):
        for at in (j * PAD, half + j * PAD):
            stage[at : at + ROWS, :] = rows_ref[j]
            stage[at + ROWS : at + PAD, :] = blank
    slot = lax.broadcasted_iota(jnp.int32, (TOK, PAD), 1).astype(jnp.float32)

    def weigh(n, carry):
        code, gate = code_ref[n], gate_ref[n]
        at = pl.ds(pl.multiple_of(n * TOK, TOK), TOK)
        for j in range(NX):
            full = jnp.where(slot == code[:, j : j + 1], gate[:, j : j + 1], 0.0)
            high = full.astype(jnp.bfloat16)
            weights[at, j * PAD : (j + 1) * PAD] = high
            weights[at, half + j * PAD : half + (j + 1) * PAD] = (full - high.astype(jnp.float32)).astype(
                jnp.bfloat16
            )
        return carry

    lax.fori_loop(0, COUNT, weigh, 0)

    def copy(n):
        at = pl.multiple_of(dest_ref[n] * TOK, TOK)
        return pltpu.make_async_copy(
            ready.at[pl.ds(n * TOK, TOK), :], out_ref.at[pl.ds(at, TOK), :], sems.at[n]
        )

    some = COUNT // 2
    for part in range(2):
        at = slice(part * some * TOK, (part + 1) * some * TOK)
        ready[at, :] = jnp.dot(weights[at, :], stage[...], preferred_element_type=jnp.float32).astype(jnp.bfloat16)
        for n in range(part * some, (part + 1) * some):
            copy(n).start()
    for n in range(COUNT):
        copy(n).wait()


def mix(dest, code_t, gate_t, rows, before):
    width = rows.shape[2]
    chained = before is not None
    vmem = pl.BlockSpec(memory_space=pltpu.VMEM)
    whole = pl.BlockSpec(memory_space=pl.ANY)
    return pl.pallas_call(
        mix_body,
        out_shape=jax.ShapeDtypeStruct((NZ * TOK, width), jnp.bfloat16),
        in_specs=[pl.BlockSpec(memory_space=pltpu.SMEM), vmem, vmem, vmem] + ([whole] if chained else []),
        out_specs=whole,
        scratch_shapes=[
            pltpu.VMEM((2 * NX * PAD, width), jnp.bfloat16),
            pltpu.VMEM((COUNT * TOK, 2 * NX * PAD), jnp.bfloat16),
            pltpu.VMEM((COUNT * TOK, width), jnp.bfloat16),
            pltpu.SemaphoreType.DMA((COUNT,)),
        ],
        input_output_aliases={4: 0} if chained else {},
        cost_estimate=pl.CostEstimate(
            flops=4 * NX * PAD * COUNT * TOK * width,
            bytes_accessed=2 * (NX * ROWS + COUNT * TOK) * width,
            transcendentals=0,
        ),
        name="mix",
    )(dest, code_t, gate_t, rows, *((before,) if chained else ()))


def across_x(blocks):
    return lax.all_to_all(blocks, "ep", split_axis=0, concat_axis=0, axis_index_groups=XG, tiled=True)


def local(tokens, expert_ids, gate_weights, cotangent, w_gate, w_up, w_down):
    width = tokens.shape[1]
    hidden_width = w_gate.shape[2]
    z = lax.axis_index("ep") % NZ
    n_rep = lax.axis_size("rep")
    source = (z - jnp.array(NEAR + FAR, jnp.int32)) % NZ
    place = z.reshape(1)
    last = (((1,), (1,)), ((), ()))
    first = (((0,), (0,)), ((), ()))
    tied = lax.optimization_barrier

    both = jnp.concatenate([w_gate[0], w_up[0]], axis=1)
    both = lax.all_gather(both, "rep", axis=0, tiled=True)
    full_gate, full_up = both[:, :hidden_width], both[:, hidden_width:]
    full_down = lax.all_gather(w_down[0], "rep", axis=1, tiled=True)

    held = [{0: pack(tokens, expert_ids, gate_weights)}, {0: cotangent}]

    def step(i, after=()):
        for a in range(2):
            mine = held[a]
            for sign in (1, -1):
                sent = mine[sign * (i - 1)]
                waits = list(after)
                if i > 1:
                    waits += [mine[-sign * (i - 2)], *(held[1 - a][s * (i - 2 + a)] for s in (1, -1))]
                sent, *_ = tied((sent, *waits))
                if i < NZ // 2:
                    mine[sign * i] = lax.ppermute(sent, "ep", zperm(sign))
                else:
                    mid = TOK // 2
                    piece = sent[:mid] if sign == 1 else sent[mid:]
                    mine[sign * i] = lax.ppermute(piece, "ep", zperm(sign))

    def chunks(a, group):
        half = NZ // 2
        return [(held[a][half], held[a][-half]) if d == half else (held[a][d],) for d in group]

    def send_tok(group):
        rows, code, gate, code_t, gate_t = pick(place, chunks(0, group))
        rows = across_x(rows)
        return rows.reshape(NX * ROWS, width), (code, gate), (code_t, gate_t)

    def send_cot(group, routes):
        rows = pick_weighted(*routes, chunks(1, group))
        rows = across_x(rows)
        return rows.reshape(NX * ROWS, width)

    def forward(rows):
        gate_pre = jnp.dot(rows, full_gate, preferred_element_type=jnp.float32)
        up_pre = jnp.dot(rows, full_up, preferred_element_type=jnp.float32)
        silu = jax.nn.silu(gate_pre)
        hidden = (silu * up_pre).astype(jnp.bfloat16)
        out = jnp.dot(hidden, full_down, preferred_element_type=jnp.float32).astype(jnp.bfloat16)
        return out.reshape(NX, ROWS, width), silu, hidden

    def backward(rows, grad_rows, silu, hidden):
        hidden_grad = lax.dot_general(grad_rows, full_down, last, preferred_element_type=jnp.float32)
        up_grad = (hidden_grad * silu).astype(jnp.bfloat16)
        down = lax.dot_general(grad_rows, hidden, first, preferred_element_type=jnp.float32)
        up = lax.dot_general(rows, up_grad, first, preferred_element_type=jnp.float32)
        return down, up

    for i in range(1, 6):
        step(i)
    near_rows, near_routes, near_weights = send_tok(NEAR)
    step(6)
    near_grads = send_cot(NEAR, near_routes)
    step(7)
    near_out, near_silu, near_hidden = forward(near_rows)
    step(8, (near_out,))
    near_back = across_x(near_out)
    far_rows, far_routes, far_weights = send_tok(FAR)
    mixed = mix(source[:COUNT], *near_weights, near_back, None)
    far_rows, mixed = tied((far_rows, mixed))
    far_out, far_silu, far_hidden = forward(far_rows)
    far_back = across_x(far_out)
    mixed = mix(source[COUNT:], *far_weights, far_back, mixed)
    mixed_out = lax.psum_scatter(mixed, "ep", axis_index_groups=ZG, scatter_dimension=0, tiled=True)
    far_grads = send_cot(FAR, far_routes)

    near_down, near_up = backward(near_rows, near_grads, near_silu, near_hidden)
    far_down, far_up = backward(far_rows, far_grads, far_silu, far_hidden)

    def summed(part):
        part = part.astype(jnp.bfloat16).reshape(n_rep, width // n_rep, hidden_width)
        part = lax.all_to_all(part, "rep", split_axis=0, concat_axis=0, tiled=True)
        return jnp.sum(part.astype(jnp.float32), axis=0)

    grad_down = summed(near_down + far_down).T
    grad_up = summed(near_up + far_up)
    return mixed_out, grad_up[None], grad_down[None]


def solution(mesh):
    in_specs = (
        P(("ep", "rep"), None),
        P(("ep", "rep"), None),
        P(("ep", "rep"), None),
        P(("ep", "rep"), None),
        P("ep", "rep", None),
        P("ep", "rep", None),
        P("ep", None, "rep"),
    )
    out_specs = (P(("ep", "rep"), None), P("ep", "rep", None), P("ep", None, "rep"))

    return jax.shard_map(local, mesh=mesh, in_specs=in_specs, out_specs=out_specs, check_vma=False)
```

time: 304 us -> 343 us (1.13)
  starting transfers between devices: 113 us -> 155 us
  blocking collectives: 0 us -> 14.7 us
  waiting for transfers between devices: 93.5 us -> 87.8 us
  Pallas kernels: 35.7 us -> 30.4 us
  local copies, waits for them, and re-layouts: 13.4 us -> 8.11 us
    ppermute x16 -> x32, starting transfers between devices: 61.2 us -> 101 us  [the longest x28 89.5 us: step(): mine[sign * i] = lax.ppermute(sent, 'ep', zperm(sign))]
    all_to_all x0 -> x1, blocking collectives: none -> 14.7 us  [across_x(): lax.all_to_all(blocks, 'ep', split_axis=0, concat_axis=0, axis_index_grou...]
    all_to_all x2, starting transfers between devices: 21.3 us -> 33.6 us  [summed(): part = lax.all_to_all(part, 'rep', split_axis=0, concat_axis=0, tiled=True)]
    all_to_all x1 -> x0, starting transfers between devices: 6.28 us -> none  [local(): lax.all_to_all(shards, 'rep', split_axis=0, concat_axis=0, tiled=True)]
    pallas_call x2, Pallas kernels: 17.1 us -> 13.4 us  [mix(): pl.pallas_call(mix_body, out_shape=jax.ShapeDtypeStruct((NZ * TOK, width)...]
    ppermute x16 -> x32, waiting for transfers between devices: 48.6 us -> 45.3 us  [the longest x28 36.2 us: step(): mine[sign * i] = lax.ppermute(sent, 'ep', zperm(sign))]
    all_to_all x6 -> x5, starting transfers between devices: 23.6 us -> 20.4 us  [across_x(): lax.all_to_all(blocks, 'ep', split_axis=0, concat_axis=0, axis_index_grou...]
    unnamed x49 -> x84, local copies, waits for them, and re-layouts: 7.6 us -> 4.73 us
  transfers between devices with their start and end apart: 27 -> 42, of which waited for: 15 -> 21; matrix products, arithmetic and copies ran while one was open for 14% -> 8% of each run, Pallas kernels for 12% -> 7%
where the time goes in v3:
time: 343 us; the launch traced here: 341 us
  starting transfers between devices  155 us (45%)
  waiting for transfers between devices  87.8 us (26%)
  Pallas kernels  30.4 us (9%)
  matrix products  24.9 us (7%)
  blocking collectives  14.7 us (4%)
  between operations  14.6 us (4%)
  local copies, waits for them, and re-layouts  8.11 us (2%)
  other arithmetic  5.07 us (1%)
    ppermute x28, starting transfers between devices, step(): mine[sign * i] = lax.ppermute(sent, 'ep', zperm(sign))  89.5 us
    ppermute x28, waiting for transfers between devices, step(): mine[sign * i] = lax.ppermute(sent, 'ep', zperm(sign))  36.2 us
    all_to_all x2, starting transfers between devices, summed(): part = lax.all_to_all(part, 'rep', split_axis=0, concat_axis=0, tiled=True)  33.6 us
    all_to_all x2, waiting for transfers between devices, summed(): part = lax.all_to_all(part, 'rep', split_axis=0, concat_axis=0, tiled=True)  33 us
    all_to_all x5, starting transfers between devices, across_x(): lax.all_to_all(blocks, 'ep', split_axis=0, concat_axis=0, axis_index_grou...  20.4 us
    all_to_all x1, blocking collectives, across_x(): lax.all_to_all(blocks, 'ep', split_axis=0, concat_axis=0, axis_index_grou...  14.7 us
    pallas_call x2, Pallas kernels, mix(): pl.pallas_call(mix_body, out_shape=jax.ShapeDtypeStruct((NZ * TOK, width)...  13.4 us
    ppermute x4, starting transfers between devices, step(): mine[sign * i] = lax.ppermute(piece, 'ep', zperm(sign))  11.5 us
  transfers between devices with their start and end apart: 42, of which 21 were waited for; matrix products, arithmetic and copies ran while one was open for 8% of the time, Pallas kernels for 7%

profile of v3, /device:TPU:1, one launch (start us, length us, event | category | flops | bytes accessed | tf_op | source)
XLA Modules:
  0.0 340.6 jit_solution(4450988072414462378)
XLA Ops:
  10.8 4.4 %collective-permute-start = (bf16[136,1024]{1,0:T(8,128)(2,1)}, bf16[136,1024]{1,0:T(8,128)(2,1)S(1)}, u32[]{:S(2)}, u32[]{:S(2)}) collective-permute-start(bf16[136,1024]{1,0:T(8,128)(2,1)} %pack.1.refs_0_), channel_id=1, source_target_pairs={{0,8},{8,16},{16,24},{24,32},{32,40},{40,48},{48,56},{56,64},{64,7... | collective-permute-start | bytes 835592 | tf_op jit(solution)/shard_map/ppermute | solution.py:274
  15.2 9.5 %collective-permute-start.2 = (bf16[136,1024]{1,0:T(8,128)(2,1)}, bf16[136,1024]{1,0:T(8,128)(2,1)S(1)}, u32[]{:S(2)}, u32[]{:S(2)}) collective-permute-start(bf16[136,1024]{1,0:T(8,128)(2,1)} %pack.1.refs_0_), channel_id=1, source_target_pairs={{0,120},{8,0},{16,8},{24,16},{32,24},{40,32},{48,40},{56,48},{64,5... | collective-permute-start | bytes 835592 | tf_op jit(solution)/shard_map/ppermute | solution.py:274
  24.7 4.6 %collective-permute-done.refs_1_ = bf16[136,1024]{1,0:T(8,128)(2,1)S(1)} collective-permute-done((bf16[136,1024]{1,0:T(8,128)(2,1)}, bf16[136,1024]{1,0:T(8,128)(2,1)S(1)}, u32[]{:S(2)}, u32[]{:S(2)}) %collective-permute-start) | collective-permute-done | bytes 278560 | tf_op jit(solution)/shard_map/ppermute | solution.py:274
  31.2 4.6 %collective-permute-start.4 = (bf16[128,1024]{1,0:T(8,128)(2,1)S(1)}, bf16[128,1024]{1,0:T(8,128)(2,1)S(1)}, u32[]{:S(2)}, u32[]{:S(2)}) collective-permute-start(bf16[128,1024]{1,0:T(8,128)(2,1)S(1)} %copy-done.26), channel_id=1, source_target_pairs={{0,120},{8,0},{16,8},{24,16},{32,24},{40,32},{48,40},{56,48},{64,5... | collective-permute-start | bytes 786440 | tf_op jit(solution)/shard_map/ppermute | solution.py:274
  37.8 4.6 %collective-permute-start.6 = (bf16[136,1024]{1,0:T(8,128)(2,1)S(1)}, bf16[136,1024]{1,0:T(8,128)(2,1)S(1)}, u32[]{:S(2)}, u32[]{:S(2)}) collective-permute-start(bf16[136,1024]{1,0:T(8,128)(2,1)S(1)} %collective-permute-done.2.refs_5_), channel_id=1, source_target_pairs={{0,120},{8,0},{16,8},{24,16},{32,24},{40,32},{48,40},{56,48},{64,5... | collective-permute-start | bytes 835592 | tf_op jit(solution)/shard_map/ppermute | solution.py:274
  42.4 2.7 collective-permute-done.3.refs_1_
  48.9 4.6 %collective-permute-start.8 = (bf16[128,1024]{1,0:T(8,128)(2,1)S(1)}, bf16[128,1024]{1,0:T(8,128)(2,1)S(1)}, u32[]{:S(2)}, u32[]{:S(2)}) collective-permute-start(bf16[128,1024]{1,0:T(8,128)(2,1)S(1)} %collective-permute-done.4.refs_5_), channel_id=1, source_target_pairs={{0,120},{8,0},{16,8},{24,16},{32,24},{40,32},{48,40},{56,48},{64,5... | collective-permute-start | bytes 786440 | tf_op jit(solution)/shard_map/ppermute | solution.py:274
  53.5 3.4 collective-permute-start.10
  63.4 4.6 %collective-permute-done.9.refs_4_ = bf16[136,1024]{1,0:T(8,128)(2,1)S(1)} collective-permute-done((bf16[136,1024]{1,0:T(8,128)(2,1)S(1)}, bf16[136,1024]{1,0:T(8,128)(2,1)S(1)}, u32[]{:S(2)}, u32[]{:S(2)}) %collective-permute-start.9) | collective-permute-done | bytes 278560 | tf_op jit(solution)/shard_map/ppermute | solution.py:274
  68.7 4.0 %pick.2 = (bf16[4,104,1024]{2,1,0:T(8,128)(2,1)}, s32[4,1024]{1,0:T(4,128)}, f32[4,1024]{1,0:T(4,128)}, f32[8,128,4]{2,1,0:T(8,128)}, f32[8,128,4]{2,1,0:T(8,128)}) custom-call(s32[1]{0:T(128)} %bitcast.place_ref, bf16[136,1024]{1,0:T(8,128)(2,1)} %pack.1.refs_0_, bf16[136,1024]{1,0:T(8,128)(2,1)} %copy-done.15, bf16[136,1024]{1,0:T(8,128)(2,1)} %copy-done.19, ...), custom_call_target="tpu_custom_call" | custom-call | flops 872415232 | bytes 2949120 | tf_op jit(solution)/shard_map/pick/pallas_call | solution.py:141
  72.7 4.2 %all-to-all-start = ((bf16[4,104,1024]{2,1,0:T(8,128)(2,1)}), bf16[4,104,1024]{2,1,0:T(8,128)(2,1)S(1)}, u32[]{:S(2)}, u32[]{:S(2)}) async-start(bf16[4,104,1024]{2,1,0:T(8,128)(2,1)} %get-tuple-element.63), calls=%async_computation | async-start | bytes 1703936 | tf_op jit(solution)/shard_map/all_to_all | solution.py:243
  78.8 3.4 collective-permute-start.11
  82.2 3.1 collective-permute-start.12
  87.5 4.0 %collective-permute-done.12.refs_7_ = bf16[128,1024]{1,0:T(8,128)(2,1)S(1)} collective-permute-done((bf16[128,1024]{1,0:T(8,128)(2,1)S(1)}, bf16[128,1024]{1,0:T(8,128)(2,1)S(1)}, u32[]{:S(2)}, u32[]{:S(2)}) %collective-permute-start.12) | collective-permute-done | bytes 262176 | tf_op jit(solution)/shard_map/ppermute | solution.py:274
  93.4 4.6 %collective-permute-start.18 = (bf16[136,1024]{1,0:T(8,128)(2,1)S(1)}, bf16[136,1024]{1,0:T(8,128)(2,1)S(1)}, u32[]{:S(2)}, u32[]{:S(2)}) collective-permute-start(bf16[136,1024]{1,0:T(8,128)(2,1)S(1)} %collective-permute-done.14.refs_3_), channel_id=1, source_target_pairs={{0,120},{8,0},{16,8},{24,16},{32,24},{40,32},{48,40},{56,48},{64,5... | collective-permute-start | bytes 835592 | tf_op jit(solution)/shard_map/ppermute | solution.py:274
  98.0 2.7 collective-permute-start.16
  103.3 3.2 collective-permute-done.16.refs_3_
  106.5 3.2 collective-permute-done.15.refs_4_
  111.6 4.6 %collective-permute-start.20 = (bf16[128,1024]{1,0:T(8,128)(2,1)}, bf16[128,1024]{1,0:T(8,128)(2,1)}, u32[]{:S(2)}, u32[]{:S(2)}) collective-permute-start(bf16[128,1024]{1,0:T(8,128)(2,1)} %collective-permute-done.16.refs_3_), channel_id=1, source_target_pairs={{0,120},{8,0},{16,8},{24,16},{32,24},{40,32},{48,40},{56,48},{64,5... | collective-permute-start | bytes 786440 | tf_op jit(solution)/shard_map/ppermute | solution.py:274
  118.2 4.6 %collective-permute-start.22 = (bf16[136,1024]{1,0:T(8,128)(2,1)S(1)}, bf16[136,1024]{1,0:T(8,128)(2,1)S(1)}, u32[]{:S(2)}, u32[]{:S(2)}) collective-permute-start(bf16[136,1024]{1,0:T(8,128)(2,1)S(1)} %collective-permute-done.18.refs_4_), channel_id=1, source_target_pairs={{0,120},{8,0},{16,8},{24,16},{32,24},{40,32},{48,40},{56,48},{64,5... | collective-permute-start | bytes 835592 | tf_op jit(solution)/shard_map/ppermute | solution.py:274
  122.8 2.7 divide_multiply_fusion.1
  127.6 3.3 fusion.16
  130.9 4.5 %all-to-all-start.2 = ((bf16[4,104,1024]{2,1,0:T(8,128)(2,1)}), bf16[4,104,1024]{2,1,0:T(8,128)(2,1)S(1)}, u32[]{:S(2)}, u32[]{:S(2)}) async-start(bf16[4,104,1024]{2,1,0:T(8,128)(2,1)} %bitcast.7), calls=%async_computation.2 | async-start | bytes 1703936 | tf_op jit(solution)/shard_map/all_to_all | solution.py:243
  137.4 3.4 collective-permute-start.24
  140.8 3.1 collective-permute-start.25
  148.1 4.3 %collective-permute-start.27 = (bf16[72,1024]{1,0:T(8,128)(2,1)S(1)}, bf16[72,1024]{1,0:T(8,128)(2,1)S(1)}, u32[]{:S(2)}, u32[]{:S(2)}) collective-permute-start(bf16[72,1024]{1,0:T(8,128)(2,1)S(1)} %slice.28), channel_id=1, source_target_pairs={{0,120},{8,0},{16,8},{24,16},{32,24},{40,32},{48,40},{56,48},{64,5... | collective-permute-start | bytes 442376 | tf_op jit(solution)/shard_map/ppermute | solution.py:278
  154.7 5.5 %collective-permute-done.26.refs_7_ = bf16[64,1024]{1,0:T(8,128)(2,1)S(1)} collective-permute-done((bf16[64,1024]{1,0:T(8,128)(2,1)S(1)}, bf16[64,1024]{1,0:T(8,128)(2,1)S(1)}, u32[]{:S(2)}, u32[]{:S(2)}) %collective-permute-start.26) | collective-permute-done | bytes 131104 | tf_op jit(solution)/shard_map/ppermute | solution.py:278
  161.5 4.0 %pick.3 = (bf16[4,104,1024]{2,1,0:T(8,128)(2,1)}, s32[4,1024]{1,0:T(4,128)}, f32[4,1024]{1,0:T(4,128)}, f32[8,128,4]{2,1,0:T(8,128)}, f32[8,128,4]{2,1,0:T(8,128)}) custom-call(s32[1]{0:T(128)} %bitcast.place_ref, bf16[136,1024]{1,0:T(8,128)(2,1)} %copy-done.13, bf16[136,1024]{1,0:T(8,128)(2,1)} %copy-done.20, bf16[136,1024]{1,0:T(8,128)(2,1)} %copy-done.8, ...), custom_call_target="tpu_custom_call" | custom-call | flops 872415232 | bytes 2949120 | tf_op jit(solution)/shard_map/pick/pallas_call | solution.py:141
  165.5 4.5 %all-to-all-start.1 = ((bf16[4,104,1024]{2,1,0:T(8,128)(2,1)}), bf16[4,104,1024]{2,1,0:T(8,128)(2,1)S(1)}, u32[]{:S(2)}, u32[]{:S(2)}) async-start(bf16[4,104,1024]{2,1,0:T(8,128)(2,1)} %get-tuple-element.70), calls=%async_computation.1 | async-start | bytes 1703936 | tf_op jit(solution)/shard_map/all_to_all | solution.py:243
  170.6 6.7 %mix.2.refs_0_ = bf16[2048,1024]{1,0:T(8,128)(2,1)} custom-call(s32[8]{0:T(128)} %get-tuple-element.83.dest_ref, f32[8,128,4]{2,1,0:T(8,128)} %get-tuple-element.71.code_ref, f32[8,128,4]{2,1,0:T(8,128)} %get-tuple-element.72.gate_ref, bf16[4,104,1024]{2,1,0:T(8,128)(2,1)} %copy-done.1), custom_call_target="tpu_custom_call" | custom-call | flops 2147483648 | bytes 2949120 | tf_op jit(solution)/shard_map/mix/pallas_call | solution.py:221
  183.9 14.7 %all_to_all.40.rows_ref = bf16[4,104,1024]{2,1,0:T(8,128)(2,1)} all-to-all(bf16[4,104,1024]{2,1,0:T(8,128)(2,1)S(1)} %bitcast.76), channel_id=1, replica_groups={{0,128,256,384},{8,136,264,392},{16,144,272,400},{24,152,280,408},{32,1..., dimensions={0} | all-to-all | bytes 1703936 | tf_op jit(solution)/shard_map/all_to_all | solution.py:243
  198.6 6.7 %mix.3 = bf16[2048,1024]{1,0:T(8,128)(2,1)} custom-call(s32[8]{0:T(128)} %get-tuple-element.84.dest_ref, f32[8,128,4]{2,1,0:T(8,128)} %get-tuple-element.68.code_ref, f32[8,128,4]{2,1,0:T(8,128)} %get-tuple-element.69.gate_ref, bf16[4,104,1024]{2,1,0:T(8,128)(2,1)} %all_to_all.40.rows_ref, bf16[2048,1024]{1,0:T(8,128)(2,1)} %mix.2.refs_0_), custom_call_target="tpu_custom_call", output_to_operand_aliasing={{}: (4, {})} | custom-call | flops 2147483648 | bytes 2949120 | tf_op jit(solution)/shard_map/mix/pallas_call | solution.py:221
  207.3 3.4 collective-permute-start.28
  212.8 2.7 collective-permute-done.28.refs_2_
  217.5 3.4 collective-permute-start.30
  221.3 3.1 collective-permute-done.30.refs_7_
  225.1 3.7 %pick_weighted.3 = bf16[4,104,1024]{2,1,0:T(8,128)(2,1)} custom-call(s32[4,1024]{1,0:T(4,128)} %get-tuple-element.77.code_ref, f32[4,1024]{1,0:T(4,128)} %get-tuple-element.78.gate_ref, bf16[128,1024]{1,0:T(8,128)(2,1)} %collective-permute-done.19.refs_0_, bf16[128,1024]{1,0:T(8,128)(2,1)} %copy-done.33, bf16[128,1024]{1,0:T(8,128)(2,1)} %copy-done.7, ...), custom_call_target="tpu_custom_call" | custom-call | flops 872415232 | bytes 2949120 | tf_op jit(solution)/shard_map/pick_weighted/pallas_call | solution.py:166
  228.8 3.5 %all-to-all-start.5 = ((bf16[4,104,1024]{2,1,0:T(8,128)(2,1)}), bf16[4,104,1024]{2,1,0:T(8,128)(2,1)S(1)}, u32[]{:S(2)}, u32[]{:S(2)}) async-start(bf16[4,104,1024]{2,1,0:T(8,128)(2,1)} %pick_weighted.3), calls=%async_computation.6 | async-start | bytes 1703936 | tf_op jit(solution)/shard_map/all_to_all | solution.py:243
  232.3 3.6 %pick_weighted.2 = bf16[4,104,1024]{2,1,0:T(8,128)(2,1)} custom-call(s32[4,1024]{1,0:T(4,128)} %get-tuple-element.75.code_ref, f32[4,1024]{1,0:T(4,128)} %get-tuple-element.76.gate_ref, bf16[128,1024]{1,0:T(8,128)(2,1)} %refs_0_.1, bf16[128,1024]{1,0:T(8,128)(2,1)} %copy-done.28, bf16[128,1024]{1,0:T(8,128)(2,1)} %copy-done.29, ...), custom_call_target="tpu_custom_call" | custom-call | flops 872415232 | bytes 2949120 | tf_op jit(solution)/shard_map/pick_weighted/pallas_call | solution.py:166
  235.9 5.1 %all-to-all-done.5 = bf16[4,104,1024]{2,1,0:T(8,128)(2,1)S(1)} async-done(((bf16[4,104,1024]{2,1,0:T(8,128)(2,1)}), bf16[4,104,1024]{2,1,0:T(8,128)(2,1)S(1)}, u32[]{:S(2)}, u32[]{:S(2)}) %all-to-all-start.5) | async-done | bytes 852000 | tf_op jit(solution)/shard_map/all_to_all | solution.py:243
  241.0 3.7 %all-to-all-start.4 = ((bf16[4,104,1024]{2,1,0:T(8,128)(2,1)}), bf16[4,104,1024]{2,1,0:T(8,128)(2,1)S(1)}, u32[]{:S(2)}, u32[]{:S(2)}) async-start(bf16[4,104,1024]{2,1,0:T(8,128)(2,1)} %pick_weighted.2), calls=%async_computation.5 | async-start | bytes 1703936 | tf_op jit(solution)/shard_map/all_to_all | solution.py:243
  244.7 5.5 %fusion.37 = f32[1024,704]{0,1:T(8,128)} fusion(bf16[416,1024]{1,0:T(8,128)(2,1)S(1)} %bitcast.75, f32[416,704]{1,0:T(8,128)} %copy-done.41, bf16[416,1024]{1,0:T(8,128)(2,1)S(1)} %bitcast.64, bf16[1,704,1024]{2,1,0:T(8,128)(2,1)} %all-gather.6.cloned.1.call-done), kind=kOutput, calls=%fused_computation.34 | convolution fusion | flops 1200156672 | bytes 7200768 | tf_op jit(solution)/shard_map/dot_general | solution.py:306
  250.2 2.9 all-to-all-done.4
  253.2 5.1 %fusion = bf16[88,8,8,128]{3,2,1,0:T(8,128)(2,1)S(1)} fusion(f32[1024,704]{0,1:T(8,128)} %fusion.37, bf16[416,1024]{1,0:T(8,128)(2,1)} %bitcast.72, f32[416,704]{1,0:T(8,128)} %copy-done.40, bf16[416,1024]{1,0:T(8,128)(2,1)S(1)} %bitcast.68, bf16[1,704,1024]{2,1,0:T(8,128)(2,1)} %all-gather.6.cloned.1.call-done), kind=kOutput, calls=%fused_computation.4 | convolution fusion | flops 1201598464 | bytes 8642560 | tf_op jit(solution)/shard_map/dot_general | solution.py:306
  259.7 28.5 %all-to-all-start.6 = ((bf16[8,128,704]{1,2,0:T(8,128)(2,1)}), bf16[8,128,704]{1,2,0:T(8,128)(2,1)S(1)}, u32[]{:S(2)}, u32[]{:S(2)}) async-start(bf16[8,128,704]{1,2,0:T(8,128)(2,1)} %bitcast.66), calls=%async_computation.7 | async-start | bytes 2883584 | tf_op jit(solution)/shard_map/all_to_all | solution.py:332
  292.7 14.6 %all-to-all-done.6 = bf16[8,128,704]{1,2,0:T(8,128)(2,1)S(1)} async-done(((bf16[8,128,704]{1,2,0:T(8,128)(2,1)}), bf16[8,128,704]{1,2,0:T(8,128)(2,1)S(1)}, u32[]{:S(2)}, u32[]{:S(2)}) %all-to-all-start.6) | async-done | bytes 1441824 | tf_op jit(solution)/shard_map/all_to_all | solution.py:332
  307.3 5.1 %all-to-all-start.7 = ((bf16[8,128,704]{1,2,0:T(8,128)(2,1)}), bf16[8,128,704]{1,2,0:T(8,128)(2,1)}, u32[]{:S(2)}, u32[]{:S(2)}) async-start(bf16[8,128,704]{1,2,0:T(8,128)(2,1)} %bitcast.67), calls=%async_computation.8 | async-start | bytes 2883584 | tf_op jit(solution)/shard_map/all_to_all | solution.py:332
  313.4 18.4 %all-to-all-done.7 = bf16[8,128,704]{1,2,0:T(8,128)(2,1)} async-done(((bf16[8,128,704]{1,2,0:T(8,128)(2,1)}), bf16[8,128,704]{1,2,0:T(8,128)(2,1)}, u32[]{:S(2)}, u32[]{:S(2)}) %all-to-all-start.7) | async-done | bytes 1441824 | tf_op jit(solution)/shard_map/all_to_all | solution.py:332
  (152 shorter events, 65.9 us)
Async XLA Ops:
  7.2 115.7 %all-gather.4.cloned.1.call-start = ((), (), s32[]{:S(2)}) async-start(), calls=%async_computation.9 | async-start | bytes 3244032 | tf_op jit(solution)/shard_map/all_gather | solution.py:258
  9.0 118.6 %all-gather.6.cloned.1.call-start = ((), (), s32[]{:S(2)}) async-start(), calls=%async_computation.11 | async-start | bytes 1622016 | tf_op jit(solution)/shard_map/all_gather | solution.py:260
  10.8 18.5 %collective-permute-start = (bf16[136,1024]{1,0:T(8,128)(2,1)}, bf16[136,1024]{1,0:T(8,128)(2,1)S(1)}, u32[]{:S(2)}, u32[]{:S(2)}) collective-permute-start(bf16[136,1024]{1,0:T(8,128)(2,1)} %pack.1.refs_0_), channel_id=1, source_target_pairs={{0,8},{8,16},{16,24},{24,32},{32,40},{40,48},{48,56},{56,64},{64,7... | collective-permute-start | bytes 835592 | tf_op jit(solution)/shard_map/ppermute | solution.py:274
  15.2 22.5 %collective-permute-start.2 = (bf16[136,1024]{1,0:T(8,128)(2,1)}, bf16[136,1024]{1,0:T(8,128)(2,1)S(1)}, u32[]{:S(2)}, u32[]{:S(2)}) collective-permute-start(bf16[136,1024]{1,0:T(8,128)(2,1)} %pack.1.refs_0_), channel_id=1, source_target_pairs={{0,120},{8,0},{16,8},{24,16},{32,24},{40,32},{48,40},{56,48},{64,5... | collective-permute-start | bytes 835592 | tf_op jit(solution)/shard_map/ppermute | solution.py:274
  29.3 38.7 %copy-start.15 = (bf16[136,1024]{1,0:T(8,128)(2,1)}, bf16[136,1024]{1,0:T(8,128)(2,1)S(1)}, u32[]{:S(2)}) copy-start(bf16[136,1024]{1,0:T(8,128)(2,1)S(1)} %collective-permute-done.refs_1_) | copy-start | bytes 835588
  29.3 15.8 %collective-permute-start.1 = (bf16[136,1024]{1,0:T(8,128)(2,1)S(1)}, bf16[136,1024]{1,0:T(8,128)(2,1)S(1)}, u32[]{:S(2)}, u32[]{:S(2)}) collective-permute-start(bf16[136,1024]{1,0:T(8,128)(2,1)S(1)} %collective-permute-done.refs_1_), channel_id=1, source_target_pairs={{0,8},{8,16},{16,24},{24,32},{32,40},{40,48},{48,56},{56,64},{64,7... | collective-permute-start | bytes 835592 | tf_op jit(solution)/shard_map/ppermute | solution.py:274
  31.2 11.1 %collective-permute-start.4 = (bf16[128,1024]{1,0:T(8,128)(2,1)S(1)}, bf16[128,1024]{1,0:T(8,128)(2,1)S(1)}, u32[]{:S(2)}, u32[]{:S(2)}) collective-permute-start(bf16[128,1024]{1,0:T(8,128)(2,1)S(1)} %copy-done.26), channel_id=1, source_target_pairs={{0,120},{8,0},{16,8},{24,16},{32,24},{40,32},{48,40},{56,48},{64,5... | collective-permute-start | bytes 786440 | tf_op jit(solution)/shard_map/ppermute | solution.py:274
  35.8 9.3 %collective-permute-start.3 = (bf16[128,1024]{1,0:T(8,128)(2,1)S(1)}, bf16[128,1024]{1,0:T(8,128)(2,1)S(1)}, u32[]{:S(2)}, u32[]{:S(2)}) collective-permute-start(bf16[128,1024]{1,0:T(8,128)(2,1)S(1)} %copy-done.26), channel_id=1, source_target_pairs={{0,8},{8,16},{16,24},{24,32},{32,40},{40,48},{48,56},{56,64},{64,7... | collective-permute-start | bytes 786440 | tf_op jit(solution)/shard_map/ppermute | solution.py:274
  37.8 15.8 %collective-permute-start.6 = (bf16[136,1024]{1,0:T(8,128)(2,1)S(1)}, bf16[136,1024]{1,0:T(8,128)(2,1)S(1)}, u32[]{:S(2)}, u32[]{:S(2)}) collective-permute-start(bf16[136,1024]{1,0:T(8,128)(2,1)S(1)} %collective-permute-done.2.refs_5_), channel_id=1, source_target_pairs={{0,120},{8,0},{16,8},{24,16},{32,24},{40,32},{48,40},{56,48},{64,5... | collective-permute-start | bytes 835592 | tf_op jit(solution)/shard_map/ppermute | solution.py:274
  42.3 83.2 %copy-start.27 = (bf16[128,1024]{1,0:T(8,128)(2,1)}, bf16[128,1024]{1,0:T(8,128)(2,1)S(1)}, u32[]{:S(2)}) copy-start(bf16[128,1024]{1,0:T(8,128)(2,1)S(1)} %collective-permute-done.4.refs_5_) | copy-start | bytes 786436
  45.1 14.4 %collective-permute-start.5 = (bf16[136,1024]{1,0:T(8,128)(2,1)S(1)}, bf16[136,1024]{1,0:T(8,128)(2,1)S(1)}, u32[]{:S(2)}, u32[]{:S(2)}) collective-permute-start(bf16[136,1024]{1,0:T(8,128)(2,1)S(1)} %collective-permute-done.1.refs_2_), channel_id=1, source_target_pairs={{0,8},{8,16},{16,24},{24,32},{32,40},{40,48},{48,56},{56,64},{64,7... | collective-permute-start | bytes 835592 | tf_op jit(solution)/shard_map/ppermute | solution.py:274
  47.0 12.4 %collective-permute-start.7 = (bf16[128,1024]{1,0:T(8,128)(2,1)S(1)}, bf16[128,1024]{1,0:T(8,128)(2,1)S(1)}, u32[]{:S(2)}, u32[]{:S(2)}) collective-permute-start(bf16[128,1024]{1,0:T(8,128)(2,1)S(1)} %collective-permute-done.3.refs_1_), channel_id=1, source_target_pairs={{0,8},{8,16},{16,24},{24,32},{32,40},{40,48},{48,56},{56,64},{64,7... | collective-permute-start | bytes 786440 | tf_op jit(solution)/shard_map/ppermute | solution.py:274
  48.9 10.5 %collective-permute-start.8 = (bf16[128,1024]{1,0:T(8,128)(2,1)S(1)}, bf16[128,1024]{1,0:T(8,128)(2,1)S(1)}, u32[]{:S(2)}, u32[]{:S(2)}) collective-permute-start(bf16[128,1024]{1,0:T(8,128)(2,1)S(1)} %collective-permute-done.4.refs_5_), channel_id=1, source_target_pairs={{0,120},{8,0},{16,8},{24,16},{32,24},{40,32},{48,40},{56,48},{64,5... | collective-permute-start | bytes 786440 | tf_op jit(solution)/shard_map/ppermute | solution.py:274
  53.5 9.8 %collective-permute-start.10 = (bf16[136,1024]{1,0:T(8,128)(2,1)S(1)}, bf16[136,1024]{1,0:T(8,128)(2,1)S(1)}, u32[]{:S(2)}, u32[]{:S(2)}) collective-permute-start(bf16[136,1024]{1,0:T(8,128)(2,1)S(1)} %collective-permute-done.6.refs_6_), channel_id=1, source_target_pairs={{0,120},{8,0},{16,8},{24,16},{32,24},{40,32},{48,40},{56,48},{64,5... | collective-permute-start | bytes 835592 | tf_op jit(solution)/shard_map/ppermute | solution.py:274
  59.5 66.1 %copy-start.29 = (bf16[128,1024]{1,0:T(8,128)(2,1)}, bf16[128,1024]{1,0:T(8,128)(2,1)S(1)}, u32[]{:S(2)}) copy-start(bf16[128,1024]{1,0:T(8,128)(2,1)S(1)} %collective-permute-done.7.refs_2_) | copy-start | bytes 786436
  59.5 8.5 %collective-permute-start.9 = (bf16[136,1024]{1,0:T(8,128)(2,1)S(1)}, bf16[136,1024]{1,0:T(8,128)(2,1)S(1)}, u32[]{:S(2)}, u32[]{:S(2)}) collective-permute-start(bf16[136,1024]{1,0:T(8,128)(2,1)S(1)} %collective-permute-done.5.refs_3_), channel_id=1, source_target_pairs={{0,8},{8,16},{16,24},{24,32},{32,40},{40,48},{48,56},{56,64},{64,7... | collective-permute-start | bytes 835592 | tf_op jit(solution)/shard_map/ppermute | solution.py:274
  72.7 50.1 %all-to-all-start = ((bf16[4,104,1024]{2,1,0:T(8,128)(2,1)}), bf16[4,104,1024]{2,1,0:T(8,128)(2,1)S(1)}, u32[]{:S(2)}, u32[]{:S(2)}) async-start(bf16[4,104,1024]{2,1,0:T(8,128)(2,1)} %get-tuple-element.63), calls=%async_computation | async-start | bytes 1703936 | tf_op jit(solution)/shard_map/all_to_all | solution.py:243
  76.9 16.6 %collective-permute-start.14 = (bf16[136,1024]{1,0:T(8,128)(2,1)S(1)}, bf16[136,1024]{1,0:T(8,128)(2,1)S(1)}, u32[]{:S(2)}, u32[]{:S(2)}) collective-permute-start(bf16[136,1024]{1,0:T(8,128)(2,1)S(1)} %copy-done.22), channel_id=1, source_target_pairs={{0,120},{8,0},{16,8},{24,16},{32,24},{40,32},{48,40},{56,48},{64,5... | collective-permute-start | bytes 835592 | tf_op jit(solution)/shard_map/ppermute | solution.py:274
  78.8 8.7 %collective-permute-start.11 = (bf16[128,1024]{1,0:T(8,128)(2,1)S(1)}, bf16[128,1024]{1,0:T(8,128)(2,1)S(1)}, u32[]{:S(2)}, u32[]{:S(2)}) collective-permute-start(bf16[128,1024]{1,0:T(8,128)(2,1)S(1)} %collective-permute-done.7.refs_2_), channel_id=1, source_target_pairs={{0,8},{8,16},{16,24},{24,32},{32,40},{40,48},{48,56},{56,64},{64,7... | collective-permute-start | bytes 786440 | tf_op jit(solution)/shard_map/ppermute | solution.py:274
  82.2 9.3 %collective-permute-start.12 = (bf16[128,1024]{1,0:T(8,128)(2,1)S(1)}, bf16[128,1024]{1,0:T(8,128)(2,1)S(1)}, u32[]{:S(2)}, u32[]{:S(2)}) collective-permute-start(bf16[128,1024]{1,0:T(8,128)(2,1)S(1)} %collective-permute-done.8.refs_6_), channel_id=1, source_target_pairs={{0,120},{8,0},{16,8},{24,16},{32,24},{40,32},{48,40},{56,48},{64,5... | collective-permute-start | bytes 786440 | tf_op jit(solution)/shard_map/ppermute | solution.py:274
  91.5 24.7 %collective-permute-start.13 = (bf16[136,1024]{1,0:T(8,128)(2,1)S(1)}, bf16[136,1024]{1,0:T(8,128)(2,1)S(1)}, u32[]{:S(2)}, u32[]{:S(2)}) collective-permute-start(bf16[136,1024]{1,0:T(8,128)(2,1)S(1)} %copy-done.18), channel_id=1, source_target_pairs={{0,8},{8,16},{16,24},{24,32},{32,40},{40,48},{48,56},{56,64},{64,7... | collective-permute-start | bytes 835592 | tf_op jit(solution)/shard_map/ppermute | solution.py:274
  93.4 32.1 %copy-start.12 = (bf16[136,1024]{1,0:T(8,128)(2,1)}, bf16[136,1024]{1,0:T(8,128)(2,1)S(1)}, u32[]{:S(2)}) copy-start(bf16[136,1024]{1,0:T(8,128)(2,1)S(1)} %collective-permute-done.14.refs_3_) | copy-start | bytes 835588
  93.4 24.7 %collective-permute-start.18 = (bf16[136,1024]{1,0:T(8,128)(2,1)S(1)}, bf16[136,1024]{1,0:T(8,128)(2,1)S(1)}, u32[]{:S(2)}, u32[]{:S(2)}) collective-permute-start(bf16[136,1024]{1,0:T(8,128)(2,1)S(1)} %collective-permute-done.14.refs_3_), channel_id=1, source_target_pairs={{0,120},{8,0},{16,8},{24,16},{32,24},{40,32},{48,40},{56,48},{64,5... | collective-permute-start | bytes 835592 | tf_op jit(solution)/shard_map/ppermute | solution.py:274
  98.0 8.5 %collective-permute-start.16 = (bf16[128,1024]{1,0:T(8,128)(2,1)S(1)}, bf16[128,1024]{1,0:T(8,128)(2,1)}, u32[]{:S(2)}, u32[]{:S(2)}) collective-permute-start(bf16[128,1024]{1,0:T(8,128)(2,1)S(1)} %collective-permute-done.12.refs_7_), channel_id=1, source_target_pairs={{0,120},{8,0},{16,8},{24,16},{32,24},{40,32},{48,40},{56,48},{64,5... | collective-permute-start | bytes 786440 | tf_op jit(solution)/shard_map/ppermute | solution.py:274
  100.7 9.0 %collective-permute-start.15 = (bf16[128,1024]{1,0:T(8,128)(2,1)S(1)}, bf16[128,1024]{1,0:T(8,128)(2,1)}, u32[]{:S(2)}, u32[]{:S(2)}) collective-permute-start(bf16[128,1024]{1,0:T(8,128)(2,1)S(1)} %collective-permute-done.11.refs_3_), channel_id=1, source_target_pairs={{0,8},{8,16},{16,24},{24,32},{32,40},{40,48},{48,56},{56,64},{64,7... | collective-permute-start | bytes 786440 | tf_op jit(solution)/shard_map/ppermute | solution.py:274
  109.7 25.7 %collective-permute-start.19 = (bf16[128,1024]{1,0:T(8,128)(2,1)}, bf16[128,1024]{1,0:T(8,128)(2,1)}, u32[]{:S(2)}, u32[]{:S(2)}) collective-permute-start(bf16[128,1024]{1,0:T(8,128)(2,1)} %collective-permute-done.15.refs_4_), channel_id=1, source_target_pairs={{0,8},{8,16},{16,24},{24,32},{32,40},{40,48},{48,56},{56,64},{64,7... | collective-permute-start | bytes 786440 | tf_op jit(solution)/shard_map/ppermute | solution.py:274
  111.6 23.8 %collective-permute-start.20 = (bf16[128,1024]{1,0:T(8,128)(2,1)}, bf16[128,1024]{1,0:T(8,128)(2,1)}, u32[]{:S(2)}, u32[]{:S(2)}) collective-permute-start(bf16[128,1024]{1,0:T(8,128)(2,1)} %collective-permute-done.16.refs_3_), channel_id=1, source_target_pairs={{0,120},{8,0},{16,8},{24,16},{32,24},{40,32},{48,40},{56,48},{64,5... | collective-permute-start | bytes 786440 | tf_op jit(solution)/shard_map/ppermute | solution.py:274
  116.3 27.7 %collective-permute-start.17 = (bf16[136,1024]{1,0:T(8,128)(2,1)S(1)}, bf16[136,1024]{1,0:T(8,128)(2,1)S(1)}, u32[]{:S(2)}, u32[]{:S(2)}) collective-permute-start(bf16[136,1024]{1,0:T(8,128)(2,1)S(1)} %collective-permute-done.13.refs_0_), channel_id=1, source_target_pairs={{0,8},{8,16},{16,24},{24,32},{32,40},{40,48},{48,56},{56,64},{64,7... | collective-permute-start | bytes 835592 | tf_op jit(solution)/shard_map/ppermute | solution.py:274
  118.2 17.2 %collective-permute-start.22 = (bf16[136,1024]{1,0:T(8,128)(2,1)S(1)}, bf16[136,1024]{1,0:T(8,128)(2,1)S(1)}, u32[]{:S(2)}, u32[]{:S(2)}) collective-permute-start(bf16[136,1024]{1,0:T(8,128)(2,1)S(1)} %collective-permute-done.18.refs_4_), channel_id=1, source_target_pairs={{0,120},{8,0},{16,8},{24,16},{32,24},{40,32},{48,40},{56,48},{64,5... | collective-permute-start | bytes 835592 | tf_op jit(solution)/shard_map/ppermute | solution.py:274
  130.9 34.5 %all-to-all-start.2 = ((bf16[4,104,1024]{2,1,0:T(8,128)(2,1)}), bf16[4,104,1024]{2,1,0:T(8,128)(2,1)S(1)}, u32[]{:S(2)}, u32[]{:S(2)}) async-start(bf16[4,104,1024]{2,1,0:T(8,128)(2,1)} %bitcast.7), calls=%async_computation.2 | async-start | bytes 1703936 | tf_op jit(solution)/shard_map/all_to_all | solution.py:243
  135.5 12.6 %collective-permute-start.23 = (bf16[136,1024]{1,0:T(8,128)(2,1)S(1)}, bf16[136,1024]{1,0:T(8,128)(2,1)S(1)}, u32[]{:S(2)}, u32[]{:S(2)}) collective-permute-start(bf16[136,1024]{1,0:T(8,128)(2,1)S(1)} %collective-permute-done.22.refs_5_), channel_id=1, source_target_pairs={{0,120},{8,0},{16,8},{24,16},{32,24},{40,32},{48,40},{56,48},{64,5... | collective-permute-start | bytes 835592 | tf_op jit(solution)/shard_map/ppermute | solution.py:274
  137.4 8.7 %collective-permute-start.24 = (bf16[128,1024]{1,0:T(8,128)(2,1)}, bf16[128,1024]{1,0:T(8,128)(2,1)S(1)}, u32[]{:S(2)}, u32[]{:S(2)}) collective-permute-start(bf16[128,1024]{1,0:T(8,128)(2,1)} %collective-permute-done.19.refs_0_), channel_id=1, source_target_pairs={{0,8},{8,16},{16,24},{24,32},{32,40},{40,48},{48,56},{56,64},{64,7... | collective-permute-start | bytes 786440 | tf_op jit(solution)/shard_map/ppermute | solution.py:274
  140.8 7.3 %collective-permute-start.25 = (bf16[128,1024]{1,0:T(8,128)(2,1)}, bf16[128,1024]{1,0:T(8,128)(2,1)S(1)}, u32[]{:S(2)}, u32[]{:S(2)}) collective-permute-start(bf16[128,1024]{1,0:T(8,128)(2,1)} %collective-permute-done.20.refs_4_), channel_id=1, source_target_pairs={{0,120},{8,0},{16,8},{24,16},{32,24},{40,32},{48,40},{56,48},{64,5... | collective-permute-start | bytes 786440 | tf_op jit(solution)/shard_map/ppermute | solution.py:274
  143.9 8.8 %collective-permute-start.21 = (bf16[136,1024]{1,0:T(8,128)(2,1)S(1)}, bf16[136,1024]{1,0:T(8,128)(2,1)S(1)}, u32[]{:S(2)}, u32[]{:S(2)}) collective-permute-start(bf16[136,1024]{1,0:T(8,128)(2,1)S(1)} %collective-permute-done.17.refs_1_), channel_id=1, source_target_pairs={{0,8},{8,16},{16,24},{24,32},{32,40},{40,48},{48,56},{56,64},{64,7... | collective-permute-start | bytes 835592 | tf_op jit(solution)/shard_map/ppermute | solution.py:274
  146.1 61.1 %copy-start.33 = (bf16[128,1024]{1,0:T(8,128)(2,1)}, bf16[128,1024]{1,0:T(8,128)(2,1)S(1)}, u32[]{:S(2)}) copy-start(bf16[128,1024]{1,0:T(8,128)(2,1)S(1)} %collective-permute-done.24.refs_1_) | copy-start | bytes 786436
  148.1 57.2 %copy-start.34 = (bf16[128,1024]{1,0:T(8,128)(2,1)}, bf16[128,1024]{1,0:T(8,128)(2,1)S(1)}, u32[]{:S(2)}) copy-start(bf16[128,1024]{1,0:T(8,128)(2,1)S(1)} %collective-permute-done.25.refs_5_) | copy-start | bytes 786436
  148.1 12.0 %collective-permute-start.27 = (bf16[72,1024]{1,0:T(8,128)(2,1)S(1)}, bf16[72,1024]{1,0:T(8,128)(2,1)S(1)}, u32[]{:S(2)}, u32[]{:S(2)}) collective-permute-start(bf16[72,1024]{1,0:T(8,128)(2,1)S(1)} %slice.28), channel_id=1, source_target_pairs={{0,120},{8,0},{16,8},{24,16},{32,24},{40,32},{48,40},{56,48},{64,5... | collective-permute-start | bytes 442376 | tf_op jit(solution)/shard_map/ppermute | solution.py:278
  152.7 7.4 %collective-permute-start.26 = (bf16[64,1024]{1,0:T(8,128)(2,1)S(1)}, bf16[64,1024]{1,0:T(8,128)(2,1)S(1)}, u32[]{:S(2)}, u32[]{:S(2)}) collective-permute-start(bf16[64,1024]{1,0:T(8,128)(2,1)S(1)} %slice.27), channel_id=1, source_target_pairs={{0,8},{8,16},{16,24},{24,32},{32,40},{40,48},{48,56},{56,64},{64,7... | collective-permute-start | bytes 393224 | tf_op jit(solution)/shard_map/ppermute | solution.py:278
  165.5 13.2 %all-to-all-start.1 = ((bf16[4,104,1024]{2,1,0:T(8,128)(2,1)}), bf16[4,104,1024]{2,1,0:T(8,128)(2,1)S(1)}, u32[]{:S(2)}, u32[]{:S(2)}) async-start(bf16[4,104,1024]{2,1,0:T(8,128)(2,1)} %get-tuple-element.70), calls=%async_computation.1 | async-start | bytes 1703936 | tf_op jit(solution)/shard_map/all_to_all | solution.py:243
  170.0 164.1 %reduce-scatter.2.cloned.1.call-start = ((), (), s32[]{:S(2)}) async-start(), calls=%async_computation.10 | async-start | bytes 4456448 | tf_op jit(solution)/shard_map/reduce_scatter | solution.py:324
  205.3 7.5 %collective-permute-start.29 = (bf16[128,1024]{1,0:T(8,128)(2,1)S(1)}, bf16[128,1024]{1,0:T(8,128)(2,1)S(1)}, u32[]{:S(2)}, u32[]{:S(2)}) collective-permute-start(bf16[128,1024]{1,0:T(8,128)(2,1)S(1)} %collective-permute-done.25.refs_5_), channel_id=1, source_target_pairs={{0,120},{8,0},{16,8},{24,16},{32,24},{40,32},{48,40},{56,48},{64,5... | collective-permute-start | bytes 786440 | tf_op jit(solution)/shard_map/ppermute | solution.py:274
  207.3 8.3 %collective-permute-start.28 = (bf16[128,1024]{1,0:T(8,128)(2,1)S(1)}, bf16[128,1024]{1,0:T(8,128)(2,1)S(1)}, u32[]{:S(2)}, u32[]{:S(2)}) collective-permute-start(bf16[128,1024]{1,0:T(8,128)(2,1)S(1)} %collective-permute-done.24.refs_1_), channel_id=1, source_target_pairs={{0,8},{8,16},{16,24},{24,32},{32,40},{40,48},{48,56},{56,64},{64,7... | collective-permute-start | bytes 786440 | tf_op jit(solution)/shard_map/ppermute | solution.py:274
  215.6 5.7 %collective-permute-start.31 = (bf16[64,1024]{1,0:T(8,128)(2,1)S(1)}, bf16[64,1024]{1,0:T(8,128)(2,1)S(1)}, u32[]{:S(2)}, u32[]{:S(2)}) collective-permute-start(bf16[64,1024]{1,0:T(8,128)(2,1)S(1)} %slice.31), channel_id=1, source_target_pairs={{0,120},{8,0},{16,8},{24,16},{32,24},{40,32},{48,40},{56,48},{64,5... | collective-permute-start | bytes 393224 | tf_op jit(solution)/shard_map/ppermute | solution.py:278
  217.5 6.9 %collective-permute-start.30 = (bf16[64,1024]{1,0:T(8,128)(2,1)S(1)}, bf16[64,1024]{1,0:T(8,128)(2,1)S(1)}, u32[]{:S(2)}, u32[]{:S(2)}) collective-permute-start(bf16[64,1024]{1,0:T(8,128)(2,1)S(1)} %slice.30), channel_id=1, source_target_pairs={{0,8},{8,16},{16,24},{24,32},{32,40},{40,48},{48,56},{56,64},{64,7... | collective-permute-start | bytes 393224 | tf_op jit(solution)/shard_map/ppermute | solution.py:278
  228.8 12.2 %all-to-all-start.5 = ((bf16[4,104,1024]{2,1,0:T(8,128)(2,1)}), bf16[4,104,1024]{2,1,0:T(8,128)(2,1)S(1)}, u32[]{:S(2)}, u32[]{:S(2)}) async-start(bf16[4,104,1024]{2,1,0:T(8,128)(2,1)} %pick_weighted.3), calls=%async_computation.6 | async-start | bytes 1703936 | tf_op jit(solution)/shard_map/all_to_all | solution.py:243
  241.0 12.2 %all-to-all-start.4 = ((bf16[4,104,1024]{2,1,0:T(8,128)(2,1)}), bf16[4,104,1024]{2,1,0:T(8,128)(2,1)S(1)}, u32[]{:S(2)}, u32[]{:S(2)}) async-start(bf16[4,104,1024]{2,1,0:T(8,128)(2,1)} %pick_weighted.2), calls=%async_computation.5 | async-start | bytes 1703936 | tf_op jit(solution)/shard_map/all_to_all | solution.py:243
  259.7 47.7 %all-to-all-start.6 = ((bf16[8,128,704]{1,2,0:T(8,128)(2,1)}), bf16[8,128,704]{1,2,0:T(8,128)(2,1)S(1)}, u32[]{:S(2)}, u32[]{:S(2)}) async-start(bf16[8,128,704]{1,2,0:T(8,128)(2,1)} %bitcast.66), calls=%async_computation.7 | async-start | bytes 2883584 | tf_op jit(solution)/shard_map/all_to_all | solution.py:332
  307.3 24.4 %all-to-all-start.7 = ((bf16[8,128,704]{1,2,0:T(8,128)(2,1)}), bf16[8,128,704]{1,2,0:T(8,128)(2,1)}, u32[]{:S(2)}, u32[]{:S(2)}) async-start(bf16[8,128,704]{1,2,0:T(8,128)(2,1)} %bitcast.67), calls=%async_computation.8 | async-start | bytes 2883584 | tf_op jit(solution)/shard_map/all_to_all | solution.py:332
  (36 other events, 356.4 us)
Sparse Core Ops, SparseCore 0:
  10.7 43.4 all-gather.3
  56.3 33.1 all-gather.5
  205.4 83.5 reduce-scatter.1

commit v4 on v3

v4 whole, which is shorter than its diff:
```python
import jax
import jax.numpy as jnp
from jax import lax
from jax.experimental import pallas as pl
from jax.experimental.pallas import tpu as pltpu
from jax.sharding import PartitionSpec as P

NX, NZ = 4, 16
CAP = 13
TOP = 6
TOK = 128
EXTRA = 8
COUNT = NZ // 2
ROWS = CAP * COUNT
PAD = 128
STEP = 112
ZG = [[x * NZ + z for z in range(NZ)] for x in range(NX)]
XG = [[x * NZ + z for x in range(NX)] for z in range(NZ)]


def pack_body(tokens_ref, ids_ref, gates_ref, out_ref):
    out_ref[:TOK, :] = tokens_ref[...]
    gates = gates_ref[...]
    high = gates.astype(jnp.bfloat16).astype(jnp.float32)
    mid = (gates - high).astype(jnp.bfloat16).astype(jnp.float32)
    low = gates - high - mid
    ids = ids_ref[...].astype(jnp.float32)
    blank = jnp.zeros((EXTRA - 4, TOK), jnp.float32)
    for k in range(TOP):
        at = slice(k, k + 1)
        rows = jnp.concatenate([ids[at], high[at], mid[at], low[at], blank], axis=0)
        out_ref[TOK:, k * TOK : (k + 1) * TOK] = rows.astype(jnp.bfloat16)
    rest = out_ref.shape[1] - TOP * TOK
    out_ref[TOK:, TOP * TOK :] = jnp.zeros((EXTRA, rest), jnp.bfloat16)


def pack(tokens, ids, gates):
    return pl.pallas_call(
        pack_body,
        out_shape=jax.ShapeDtypeStruct((TOK + EXTRA, tokens.shape[1]), jnp.bfloat16),
        cost_estimate=pl.CostEstimate(flops=0, bytes_accessed=4 * TOK * tokens.shape[1], transcendentals=0),
        name="pack",
    )(tokens, ids.T, gates.T)


def pick_rows(code, gate, all_rows, out_ref, weighted):
    slot = lax.broadcasted_iota(jnp.int32, (STEP, all_rows.shape[0]), 0)
    hits = [slot == code[j : j + 1, :] for j in range(NX)]
    ones = jnp.concatenate([jnp.where(h, 1.0, 0.0).astype(jnp.bfloat16) for h in hits], axis=0)
    got = jnp.dot(ones, all_rows, preferred_element_type=jnp.float32)
    for j in range(NX):
        part = got[j * STEP : j * STEP + ROWS]
        if weighted:
            scale = jnp.sum(jnp.where(hits[j], gate[j : j + 1, :], 0.0), axis=1, keepdims=True)
            part = part * scale[:ROWS]
        out_ref[j] = part.astype(jnp.bfloat16)


def pick_body(place_ref, all_ref, out_ref, code_ref, gate_ref, code_t_ref, gate_t_ref, stage, extra, found):
    for n in range(COUNT):
        row = n * (TOK + EXTRA)
        stage[n * TOK : (n + 1) * TOK, :] = all_ref[row : row + TOK, :]
        extra[n] = all_ref[row + TOK : row + TOK + EXTRA, :].astype(jnp.float32)
    mine = place_ref[0] + NZ * lax.broadcasted_iota(jnp.int32, (NX, TOK), 0)
    mine = mine.astype(jnp.float32)

    def match(n, carry):
        rows = extra[n]
        hit = jnp.zeros((NX, TOK), jnp.float32)
        weight = jnp.zeros((NX, TOK), jnp.float32)
        for k in range(TOP):
            part = rows[0:4, k * TOK : (k + 1) * TOK]
            same = part[0:1] == mine
            hit = jnp.where(same, 1.0, hit)
            weight = jnp.where(same, part[1:2] + part[2:3] + part[3:4], weight)
        found[0, n] = hit
        found[1, n] = weight
        return carry

    lax.fori_loop(0, COUNT, match, 0)
    hits = jnp.concatenate([found[0, n] for n in range(COUNT)], axis=0)
    weights = jnp.concatenate([found[1, n] for n in range(COUNT)], axis=0)
    shape = (TOK, TOK)
    earlier = lax.broadcasted_iota(jnp.int32, shape, 0) < lax.broadcasted_iota(jnp.int32, shape, 1)
    position = jnp.dot(
        hits.astype(jnp.bfloat16),
        jnp.where(earlier, 1.0, 0.0).astype(jnp.bfloat16),
        preferred_element_type=jnp.float32,
    )
    first = CAP * (lax.broadcasted_iota(jnp.int32, (NX * COUNT, TOK), 0) // NX)
    codes = jnp.where(hits > 0, position.astype(jnp.int32) + first, -1)
    codes_f = codes.astype(jnp.float32)
    fill = jnp.zeros((TOK - NX * COUNT, TOK), jnp.float32)
    code_t = jnp.concatenate([codes_f, fill], axis=0).T
    gate_t = jnp.concatenate([weights, fill], axis=0).T
    for n in range(COUNT):
        at = slice(n * NX, (n + 1) * NX)
        code_ref[:, n * TOK : (n + 1) * TOK] = codes[at]
        gate_ref[:, n * TOK : (n + 1) * TOK] = weights[at]
        code_t_ref[n] = code_t[:, at]
        gate_t_ref[n] = gate_t[:, at]
    pick_rows(code_ref[...], None, stage[...], out_ref, False)


def pick_cost(rows, width):
    return pl.CostEstimate(
        flops=2 * NX * ROWS * rows * width, bytes_accessed=2 * (rows + NX * ROWS) * width, transcendentals=0
    )


def pick(place, gathered, b):
    width = gathered.shape[1]
    rows = COUNT * TOK
    shapes = [((NX, ROWS, width), jnp.bfloat16), ((NX, rows), jnp.int32), ((NX, rows), jnp.float32)]
    shapes += [((COUNT, TOK, NX), jnp.float32)] * 2
    return pl.pallas_call(
        pick_body,
        out_shape=[jax.ShapeDtypeStruct(s, t) for s, t in shapes],
        grid=(1,),
        in_specs=[
            pl.BlockSpec(memory_space=pltpu.SMEM),
            pl.BlockSpec((COUNT * (TOK + EXTRA), width), lambda i: (b, 0)),
        ],
        out_specs=[pl.BlockSpec(s, lambda i, s=s: (0,) * len(s)) for s, _ in shapes],
        scratch_shapes=[
            pltpu.VMEM((rows, width), jnp.bfloat16),
            pltpu.VMEM((COUNT, EXTRA, width), jnp.float32),
            pltpu.VMEM((2, COUNT, NX, TOK), jnp.float32),
        ],
        cost_estimate=pick_cost(rows, width),
        name="pick",
    )(place, gathered)


def pick_weighted_body(code_ref, gate_ref, all_ref, out_ref):
    pick_rows(code_ref[...], gate_ref[...], all_ref[...], out_ref, True)


def pick_weighted(code, gate, gathered, b):
    width = gathered.shape[1]
    rows = COUNT * TOK
    small = pl.BlockSpec((NX, rows), lambda i: (0, 0))
    return pl.pallas_call(
        pick_weighted_body,
        out_shape=jax.ShapeDtypeStruct((NX, ROWS, width), jnp.bfloat16),
        grid=(1,),
        in_specs=[small, small, pl.BlockSpec((rows, width), lambda i: (b, 0))],
        out_specs=pl.BlockSpec((NX, ROWS, width), lambda i: (0, 0, 0)),
        cost_estimate=pick_cost(rows, width),
        name="pick_weighted",
    )(code, gate, gathered)


def mix_body(code_ref, gate_ref, rows_ref, *refs):
    out_ref, stage, weights = refs[-3:]
    width = stage.shape[1]
    half = NX * PAD
    blank = jnp.zeros((PAD - ROWS, width), jnp.bfloat16)
    for j in range(NX):
        for at in (j * PAD, half + j * PAD):
            stage[at : at + ROWS, :] = rows_ref[j]
            stage[at + ROWS : at + PAD, :] = blank
    slot = lax.broadcasted_iota(jnp.int32, (TOK, PAD), 1).astype(jnp.float32)

    def weigh(n, carry):
        code, gate = code_ref[n], gate_ref[n]
        at = pl.ds(pl.multiple_of(n * TOK, TOK), TOK)
        for j in range(NX):
            full = jnp.where(slot == code[:, j : j + 1], gate[:, j : j + 1], 0.0)
            high = full.astype(jnp.bfloat16)
            weights[at, j * PAD : (j + 1) * PAD] = high
            weights[at, half + j * PAD : half + (j + 1) * PAD] = (full - high.astype(jnp.float32)).astype(
                jnp.bfloat16
            )
        return carry

    lax.fori_loop(0, COUNT, weigh, 0)
    out_ref[...] = jnp.dot(weights[...], stage[...], preferred_element_type=jnp.float32).astype(jnp.bfloat16)


def mix(code_t, gate_t, rows, before, b):
    width = rows.shape[2]
    chained = before is not None
    small = pl.BlockSpec((COUNT, TOK, NX), lambda i: (0, 0, 0))
    return pl.pallas_call(
        mix_body,
        out_shape=jax.ShapeDtypeStruct((NZ * TOK, width), jnp.bfloat16),
        grid=(1,),
        in_specs=[small, small, pl.BlockSpec((NX, ROWS, width), lambda i: (0, 0, 0))]
        + ([pl.BlockSpec(memory_space=pl.ANY)] if chained else []),
        out_specs=pl.BlockSpec((COUNT * TOK, width), lambda i: (b, 0)),
        scratch_shapes=[
            pltpu.VMEM((2 * NX * PAD, width), jnp.bfloat16),
            pltpu.VMEM((COUNT * TOK, 2 * NX * PAD), jnp.bfloat16),
        ],
        input_output_aliases={3: 0} if chained else {},
        cost_estimate=pl.CostEstimate(
            flops=4 * NX * PAD * COUNT * TOK * width,
            bytes_accessed=2 * (NX * ROWS + COUNT * TOK) * width,
            transcendentals=0,
        ),
        name="mix",
    )(code_t, gate_t, rows, *((before,) if chained else ()))


def across_x(blocks):
    return lax.all_to_all(blocks, "ep", split_axis=0, concat_axis=0, axis_index_groups=XG, tiled=True)


def local(tokens, expert_ids, gate_weights, cotangent, w_gate, w_up, w_down):
    width = tokens.shape[1]
    hidden_width = w_gate.shape[2]
    share = w_gate.shape[1]
    place = (lax.axis_index("ep") % NZ).reshape(1)
    n_rep = lax.axis_size("rep")
    last = (((1,), (1,)), ((), ()))
    first = (((0,), (0,)), ((), ()))
    tied = lax.optimization_barrier

    def along_z(rows):
        return lax.all_gather(rows, "ep", axis_index_groups=ZG, axis=0, tiled=True)

    with jax.named_scope("tok_gather"):
        all_tok = along_z(pack(tokens, expert_ids, gate_weights))
    with jax.named_scope("cot_gather"):
        all_cot = along_z(cotangent)
    shards = jnp.concatenate([w_gate[0].T, w_up[0].T, w_down[0]], axis=1)
    shards = jnp.broadcast_to(shards[None], (n_rep,) + shards.shape)
    shards = lax.all_to_all(shards, "rep", split_axis=0, concat_axis=0, tiled=True)
    full_gate, full_up, full_down = (
        shards[:, :, n * share : (n + 1) * share].transpose(1, 0, 2).reshape(hidden_width, width)
        for n in range(3)
    )

    def forward(rows):
        gate_pre = lax.dot_general(rows, full_gate, last, preferred_element_type=jnp.float32)
        up_pre = lax.dot_general(rows, full_up, last, preferred_element_type=jnp.float32)
        silu = jax.nn.silu(gate_pre)
        hidden = (silu * up_pre).astype(jnp.bfloat16)
        out = jnp.dot(hidden, full_down, preferred_element_type=jnp.float32).astype(jnp.bfloat16)
        return out.reshape(NX, ROWS, width), silu, hidden

    picked, routes, weights = [], [], []
    for b in range(2):
        rows, code, gate, code_t, gate_t = pick(place, all_tok, b)
        picked.append(across_x(rows).reshape(NX * ROWS, width))
        routes.append((code, gate))
        weights.append((code_t, gate_t))
    outs = [forward(rows) for rows in picked]
    mixed = None
    for b in range(2):
        mixed = mix(*weights[b], across_x(outs[b][0]), mixed, b)
    with jax.named_scope("mixed_scatter"):
        mixed_out = lax.psum_scatter(mixed, "ep", axis_index_groups=ZG, scatter_dimension=0, tiled=True)

    grads = [across_x(pick_weighted(*routes[b], all_cot, b)).reshape(NX * ROWS, width) for b in range(2)]
    part_up = part_down = None
    for b in range(2):
        _, silu, hidden = outs[b]
        down = lax.dot_general(grads[b], hidden, first, preferred_element_type=jnp.float32)
        hidden_grad = lax.dot_general(grads[b], full_down, last, preferred_element_type=jnp.float32)
        up_grad = (hidden_grad * silu).astype(jnp.bfloat16)
        up = lax.dot_general(picked[b], up_grad, first, preferred_element_type=jnp.float32)
        part_down = down if b == 0 else part_down + down
        part_up = up if b == 0 else part_up + up

    def summed(part):
        part = part.astype(jnp.bfloat16).reshape(n_rep, width // n_rep, hidden_width)
        part = lax.all_to_all(part, "rep", split_axis=0, concat_axis=0, tiled=True)
        return jnp.sum(part.astype(jnp.float32), axis=0)

    grad_down = summed(part_down).T
    grad_up = summed(part_up)
    return mixed_out, grad_up[None], grad_down[None]


def solution(mesh):
    in_specs = (
        P(("ep", "rep"), None),
        P(("ep", "rep"), None),
        P(("ep", "rep"), None),
        P(("ep", "rep"), None),
        P("ep", "rep", None),
        P("ep", "rep", None),
        P("ep", None, "rep"),
    )
    out_specs = (P(("ep", "rep"), None), P("ep", "rep", None), P("ep", None, "rep"))
    return jax.shard_map(local, mesh=mesh, in_specs=in_specs, out_specs=out_specs, check_vma=False)
```

time: 343 us -> 269 us (0.78)
  starting transfers between devices: 155 us -> 55.7 us
  waiting for transfers between devices: 87.8 us -> 125 us
  blocking collectives: 14.7 us -> 0 us
  local copies, waits for them, and re-layouts: 8.11 us -> 13.2 us
    ppermute x32 -> x0, starting transfers between devices: 101 us -> none  [the longest x28 89.5 us: step(): mine[sign * i] = lax.ppermute(sent, 'ep', zperm(sign))]
    all_gather x2, waiting for transfers between devices: 0.04 us -> 67.4 us  [along_z(): return lax.all_gather(rows, 'ep', axis_index_groups=ZG, axis=0, tiled=True)]
    ppermute x32 -> x0, waiting for transfers between devices: 45.3 us -> none  [the longest x28 36.2 us: step(): mine[sign * i] = lax.ppermute(sent, 'ep', zperm(sign))]
    all_to_all x5 -> x6, waiting for transfers between devices: 9.4 us -> 24.2 us  [across_x(): lax.all_to_all(blocks, 'ep', split_axis=0, concat_axis=0, axis_index_grou...]
    all_to_all x1 -> x0, blocking collectives: 14.7 us -> none  [across_x(): lax.all_to_all(blocks, 'ep', split_axis=0, concat_axis=0, axis_index_grou...]
    all_to_all x2, starting transfers between devices: 33.6 us -> 21.4 us  [summed(): part = lax.all_to_all(part, 'rep', split_axis=0, concat_axis=0, tiled=True)]
    all_to_all x0 -> x1, starting transfers between devices: none -> 11.3 us  [local(): lax.all_to_all(shards, 'rep', split_axis=0, concat_axis=0, tiled=True)]
    unnamed x84 -> x25, local copies, waits for them, and re-layouts: 4.73 us -> 7.97 us
  transfers between devices with their start and end apart: 42 -> 12, of which waited for: 21 -> 9; matrix products, arithmetic and copies ran while one was open for 8% -> 14% of each run, Pallas kernels for 7% -> 11%
where the time goes in v4:
time: 269 us; the launch traced here: 268 us
  waiting for transfers between devices  125 us (46%)
  starting transfers between devices  55.7 us (21%)
  Pallas kernels  31.8 us (12%)
  matrix products  23.8 us (9%)
  between operations  13.9 us (5%)
  local copies, waits for them, and re-layouts  13.2 us (5%)
  other arithmetic  4.43 us (2%)
    all_gather x2, waiting for transfers between devices, along_z(): return lax.all_gather(rows, 'ep', axis_index_groups=ZG, axis=0, tiled=True)  67.4 us
    all_to_all x2, waiting for transfers between devices, summed(): part = lax.all_to_all(part, 'rep', split_axis=0, concat_axis=0, tiled=True)  33 us
    all_to_all x6, waiting for transfers between devices, across_x(): lax.all_to_all(blocks, 'ep', split_axis=0, concat_axis=0, axis_index_grou...  24.2 us
    all_to_all x6, starting transfers between devices, across_x(): lax.all_to_all(blocks, 'ep', split_axis=0, concat_axis=0, axis_index_grou...  22.7 us
    all_to_all x2, starting transfers between devices, summed(): part = lax.all_to_all(part, 'rep', split_axis=0, concat_axis=0, tiled=True)  21.4 us
    pallas_call x2, Pallas kernels, mix(): pl.pallas_call(mix_body, out_shape=jax.ShapeDtypeStruct((NZ * TOK, width)...  13.9 us
    all_to_all x1, starting transfers between devices, local(): lax.all_to_all(shards, 'rep', split_axis=0, concat_axis=0, tiled=True)  11.3 us
    dot_general x2, matrix products, local(): lax.dot_general(picked[b], up_grad, first, preferred_element_type=jnp.flo...  10.5 us
  transfers between devices with their start and end apart: 12, of which 9 were waited for; matrix products, arithmetic and copies ran while one was open for 14% of the time, Pallas kernels for 11%

profile of v4, /device:TPU:1, one launch (start us, length us, event | category | flops | bytes accessed | tf_op | source)
XLA Modules:
  0.0 268.1 jit_solution(10967946783539448701)
XLA Ops:
  7.2 1.7 pack.1
  9.0 0.7 all-gather.5.cloned.1.call-update
  9.7 1.2 pad_maximum_fusion
  10.9 2.5 broadcast_in_dim.12
  13.3 11.3 %all-to-all-start.1 = ((bf16[8,704,384]{2,1,0:T(8,128)(2,1)}), bf16[8,704,384]{2,1,0:T(8,128)(2,1)}, u32[]{:S(2)}, u32[]{:S(2)}) async-start(bf16[8,704,384]{2,1,0:T(8,128)(2,1)} %broadcast_in_dim.12), calls=%async_computation.1 | async-start | bytes 8650752 | tf_op jit(solution)/shard_map/all_to_all | solution.py:229
  24.6 61.1 %all-gather.3.cloned.1.call-done.all_ref = bf16[2176,1024]{1,0:T(8,128)(2,1)} async-done(((bf16[136,1024]{1,0:T(8,128)(2,1)}), bf16[2176,1024]{1,0:T(8,128)(2,1)}) %all-gather.3.cloned.1.call-update) | async-done | bytes 4456464 | tf_op jit(solution)/shard_map/tok_gather/all_gather | solution.py:221
  85.7 4.1 %pick.3 = (bf16[4,104,1024]{2,1,0:T(8,128)(2,1)}, s32[4,1024]{1,0:T(4,128)}, f32[4,1024]{1,0:T(4,128)}, f32[8,128,4]{2,1,0:T(8,128)}, f32[8,128,4]{2,1,0:T(8,128)}) custom-call(s32[1]{0:T(128)} %bitcast.place_ref, bf16[2176,1024]{1,0:T(8,128)(2,1)} %all-gather.3.cloned.1.call-done.all_ref), custom_call_target="tpu_custom_call" | custom-call | flops 872415232 | bytes 2949120 | tf_op jit(solution)/shard_map/pick/pallas_call | solution.py:116
  89.9 4.1 %all-to-all-start.3 = ((bf16[4,104,1024]{2,1,0:T(8,128)(2,1)}), bf16[4,104,1024]{2,1,0:T(8,128)(2,1)S(1)}, u32[]{:S(2)}, u32[]{:S(2)}) async-start(bf16[4,104,1024]{2,1,0:T(8,128)(2,1)} %get-tuple-element.18), calls=%async_computation.3 | async-start | bytes 1703936 | tf_op jit(solution)/shard_map/all_to_all | solution.py:207
  94.0 4.1 %slice_bitcast_fusion = (bf16[8,88,8,128]{3,2,1,0:T(8,128)(2,1)S(1)}, bf16[8,88,8,128]{3,2,1,0:T(8,128)(2,1)}, bf16[8,88,8,128]{3,2,1,0:T(8,128)(2,1)}) fusion(bf16[8,704,384]{2,1,0:T(8,128)(2,1)} %all-to-all-done.1), kind=kLoop, calls=%fused_computation.24 | loop fusion | bytes 8650752
  98.1 4.6 %pick.2 = (bf16[4,104,1024]{2,1,0:T(8,128)(2,1)}, s32[4,1024]{1,0:T(4,128)}, f32[4,1024]{1,0:T(4,128)}, f32[8,128,4]{2,1,0:T(8,128)}, f32[8,128,4]{2,1,0:T(8,128)}) custom-call(s32[1]{0:T(128)} %bitcast.place_ref, bf16[2176,1024]{1,0:T(8,128)(2,1)} %all-gather.3.cloned.1.call-done.all_ref), custom_call_target="tpu_custom_call" | custom-call | flops 872415232 | bytes 2949120 | tf_op jit(solution)/shard_map/pick/pallas_call | solution.py:116
  102.7 4.2 %all-to-all-start = ((bf16[4,104,1024]{2,1,0:T(8,128)(2,1)}), bf16[4,104,1024]{2,1,0:T(8,128)(2,1)S(1)}, u32[]{:S(2)}, u32[]{:S(2)}) async-start(bf16[4,104,1024]{2,1,0:T(8,128)(2,1)} %get-tuple-element.15), calls=%async_computation | async-start | bytes 1703936 | tf_op jit(solution)/shard_map/all_to_all | solution.py:207
  107.0 2.5 divide_multiply_fusion
  109.4 0.9 fusion.42
  110.5 0.8 copy-done.7
  111.4 1.7 fusion.33
  113.1 3.8 %all-to-all-done = bf16[4,104,1024]{2,1,0:T(8,128)(2,1)S(1)} async-done(((bf16[4,104,1024]{2,1,0:T(8,128)(2,1)}), bf16[4,104,1024]{2,1,0:T(8,128)(2,1)S(1)}, u32[]{:S(2)}, u32[]{:S(2)}) %all-to-all-start) | async-done | bytes 852000 | tf_op jit(solution)/shard_map/all_to_all | solution.py:207
  116.9 3.5 %all-to-all-start.4 = ((bf16[4,104,1024]{2,1,0:T(8,128)(2,1)}), bf16[4,104,1024]{2,1,0:T(8,128)(2,1)S(1)}, u32[]{:S(2)}, u32[]{:S(2)}) async-start(bf16[4,104,1024]{2,1,0:T(8,128)(2,1)} %bitcast.112), calls=%async_computation.4 | async-start | bytes 1703936 | tf_op jit(solution)/shard_map/all_to_all | solution.py:207
  120.4 2.5 divide_multiply_fusion.1
  122.9 0.9 fusion.45
  124.0 0.8 copy-done.8
  124.8 1.8 fusion.30
  126.6 4.9 %all-to-all-done.4.rows_ref = bf16[4,104,1024]{2,1,0:T(8,128)(2,1)S(1)} async-done(((bf16[4,104,1024]{2,1,0:T(8,128)(2,1)}), bf16[4,104,1024]{2,1,0:T(8,128)(2,1)S(1)}, u32[]{:S(2)}, u32[]{:S(2)}) %all-to-all-start.4) | async-done | bytes 852000 | tf_op jit(solution)/shard_map/all_to_all | solution.py:207
  131.5 0.9 copy-done.6
  132.4 3.5 %all-to-all-start.2 = ((bf16[4,104,1024]{2,1,0:T(8,128)(2,1)}), bf16[4,104,1024]{2,1,0:T(8,128)(2,1)S(1)}, u32[]{:S(2)}, u32[]{:S(2)}) async-start(bf16[4,104,1024]{2,1,0:T(8,128)(2,1)} %bitcast.12), calls=%async_computation.2 | async-start | bytes 1703936 | tf_op jit(solution)/shard_map/all_to_all | solution.py:207
  135.9 0.2 reduce-scatter.2.cloned.1.call-start
  136.2 7.0 %mix.2.refs_0_ = bf16[2048,1024]{1,0:T(8,128)(2,1)} custom-call(f32[8,128,4]{2,1,0:T(8,128)} %get-tuple-element.16.code_ref, f32[8,128,4]{2,1,0:T(8,128)} %get-tuple-element.17.gate_ref, bf16[4,104,1024]{2,1,0:T(8,128)(2,1)} %copy-done.6), custom_call_target="tpu_custom_call" | custom-call | flops 2147483648 | bytes 2949120 | tf_op jit(solution)/shard_map/mix/pallas_call | solution.py:185
  143.1 4.1 %all-to-all-done.2.rows_ref = bf16[4,104,1024]{2,1,0:T(8,128)(2,1)S(1)} async-done(((bf16[4,104,1024]{2,1,0:T(8,128)(2,1)}), bf16[4,104,1024]{2,1,0:T(8,128)(2,1)S(1)}, u32[]{:S(2)}, u32[]{:S(2)}) %all-to-all-start.2) | async-done | bytes 852000 | tf_op jit(solution)/shard_map/all_to_all | solution.py:207
  147.2 0.9 copy-done
  148.1 6.9 %mix.3 = bf16[2048,1024]{1,0:T(8,128)(2,1)} custom-call(f32[8,128,4]{2,1,0:T(8,128)} %get-tuple-element.13.code_ref, f32[8,128,4]{2,1,0:T(8,128)} %get-tuple-element.14.gate_ref, bf16[4,104,1024]{2,1,0:T(8,128)(2,1)} %copy-done, bf16[2048,1024]{1,0:T(8,128)(2,1)} %mix.2.refs_0_), custom_call_target="tpu_custom_call", output_to_operand_aliasing={{}: (3, {})} | custom-call | flops 2147483648 | bytes 2949120 | tf_op jit(solution)/shard_map/mix/pallas_call | solution.py:185
  155.1 6.3 %all-gather.5.cloned.1.call-done.all_ref = bf16[2048,1024]{1,0:T(8,128)(2,1)} async-done(((bf16[128,1024]{1,0:T(8,128)(2,1)}), bf16[2048,1024]{1,0:T(8,128)(2,1)}) %all-gather.5.cloned.1.call-update) | async-done | bytes 4194320 | tf_op jit(solution)/shard_map/cot_gather/all_gather | solution.py:221
  161.4 3.7 %pick_weighted.2 = bf16[4,104,1024]{2,1,0:T(8,128)(2,1)} custom-call(s32[4,1024]{1,0:T(4,128)} %get-tuple-element.19.code_ref, f32[4,1024]{1,0:T(4,128)} %get-tuple-element.20.gate_ref, bf16[2048,1024]{1,0:T(8,128)(2,1)} %all-gather.5.cloned.1.call-done.all_ref), custom_call_target="tpu_custom_call" | custom-call | flops 872415232 | bytes 2949120 | tf_op jit(solution)/shard_map/pick_weighted/pallas_call | solution.py:143
  165.0 3.8 %all-to-all-start.5 = ((bf16[4,104,1024]{2,1,0:T(8,128)(2,1)}), bf16[4,104,1024]{2,1,0:T(8,128)(2,1)S(1)}, u32[]{:S(2)}, u32[]{:S(2)}) async-start(bf16[4,104,1024]{2,1,0:T(8,128)(2,1)} %pick_weighted.2), calls=%async_computation.6 | async-start | bytes 1703936 | tf_op jit(solution)/shard_map/all_to_all | solution.py:207
  168.8 3.7 %pick_weighted.3 = bf16[4,104,1024]{2,1,0:T(8,128)(2,1)} custom-call(s32[4,1024]{1,0:T(4,128)} %get-tuple-element.21.code_ref, f32[4,1024]{1,0:T(4,128)} %get-tuple-element.22.gate_ref, bf16[2048,1024]{1,0:T(8,128)(2,1)} %all-gather.5.cloned.1.call-done.all_ref), custom_call_target="tpu_custom_call" | custom-call | flops 872415232 | bytes 2949120 | tf_op jit(solution)/shard_map/pick_weighted/pallas_call | solution.py:143
  172.5 5.0 %all-to-all-done.5 = bf16[4,104,1024]{2,1,0:T(8,128)(2,1)S(1)} async-done(((bf16[4,104,1024]{2,1,0:T(8,128)(2,1)}), bf16[4,104,1024]{2,1,0:T(8,128)(2,1)S(1)}, u32[]{:S(2)}, u32[]{:S(2)}) %all-to-all-start.5) | async-done | bytes 852000 | tf_op jit(solution)/shard_map/all_to_all | solution.py:207
  177.5 3.5 %all-to-all-start.6 = ((bf16[4,104,1024]{2,1,0:T(8,128)(2,1)}), bf16[4,104,1024]{2,1,0:T(8,128)(2,1)S(1)}, u32[]{:S(2)}, u32[]{:S(2)}) async-start(bf16[4,104,1024]{2,1,0:T(8,128)(2,1)} %pick_weighted.3), calls=%async_computation.7 | async-start | bytes 1703936 | tf_op jit(solution)/shard_map/all_to_all | solution.py:207
  181.0 5.4 %fusion.53 = f32[1024,704]{0,1:T(8,128)} fusion(bf16[416,1024]{1,0:T(8,128)(2,1)} %bitcast.108, f32[416,704]{1,0:T(8,128)} %copy-done.10, bf16[416,1024]{1,0:T(8,128)(2,1)S(1)} %bitcast.100, bf16[8,88,8,128]{3,2,1,0:T(8,128)(2,1)S(1)} %get-tuple-element.23), kind=kOutput, calls=%fused_computation.43 | convolution fusion | flops 1200156672 | bytes 7200768 | tf_op jit(solution)/shard_map/dot_general | solution.py:263
  186.4 6.4 %all-to-all-done.6 = bf16[4,104,1024]{2,1,0:T(8,128)(2,1)S(1)} async-done(((bf16[4,104,1024]{2,1,0:T(8,128)(2,1)}), bf16[4,104,1024]{2,1,0:T(8,128)(2,1)S(1)}, u32[]{:S(2)}, u32[]{:S(2)}) %all-to-all-start.6) | async-done | bytes 852000 | tf_op jit(solution)/shard_map/all_to_all | solution.py:207
  192.8 5.1 %fusion = bf16[88,8,8,128]{3,2,1,0:T(8,128)(2,1)S(1)} fusion(f32[1024,704]{0,1:T(8,128)} %fusion.53, bf16[416,1024]{1,0:T(8,128)(2,1)} %bitcast.111, f32[416,704]{1,0:T(8,128)} %copy-done.11, bf16[416,1024]{1,0:T(8,128)(2,1)S(1)} %bitcast.104, bf16[8,88,8,128]{3,2,1,0:T(8,128)(2,1)} %copy-done.1), kind=kOutput, calls=%fused_computation.4 | convolution fusion | flops 1201598464 | bytes 8642560 | tf_op jit(solution)/shard_map/dot_general | solution.py:263
  197.9 1.4 copy.63
  199.3 16.3 %all-to-all-start.7 = ((bf16[8,128,704]{1,2,0:T(8,128)(2,1)}), bf16[8,128,704]{1,2,0:T(8,128)(2,1)S(1)}, u32[]{:S(2)}, u32[]{:S(2)}) async-start(bf16[8,128,704]{1,2,0:T(8,128)(2,1)} %bitcast.102), calls=%async_computation.8 | async-start | bytes 2883584 | tf_op jit(solution)/shard_map/all_to_all | solution.py:269
  215.6 2.1 fusion.66
  217.8 1.0 fusion.1
  218.8 1.4 copy.62
  220.2 14.6 %all-to-all-done.7 = bf16[8,128,704]{1,2,0:T(8,128)(2,1)S(1)} async-done(((bf16[8,128,704]{1,2,0:T(8,128)(2,1)}), bf16[8,128,704]{1,2,0:T(8,128)(2,1)S(1)}, u32[]{:S(2)}, u32[]{:S(2)}) %all-to-all-start.7) | async-done | bytes 1441824 | tf_op jit(solution)/shard_map/all_to_all | solution.py:269
  234.8 5.1 %all-to-all-start.8 = ((bf16[8,128,704]{1,2,0:T(8,128)(2,1)}), bf16[8,128,704]{1,2,0:T(8,128)(2,1)}, u32[]{:S(2)}, u32[]{:S(2)}) async-start(bf16[8,128,704]{1,2,0:T(8,128)(2,1)} %bitcast.103), calls=%async_computation.9 | async-start | bytes 2883584 | tf_op jit(solution)/shard_map/all_to_all | solution.py:269
  239.9 0.9 convert_reduce_fusion.1
  240.9 18.4 %all-to-all-done.8 = bf16[8,128,704]{1,2,0:T(8,128)(2,1)} async-done(((bf16[8,128,704]{1,2,0:T(8,128)(2,1)}), bf16[8,128,704]{1,2,0:T(8,128)(2,1)}, u32[]{:S(2)}, u32[]{:S(2)}) %all-to-all-start.8) | async-done | bytes 1441824 | tf_op jit(solution)/shard_map/all_to_all | solution.py:269
  259.3 2.3 convert_reduce_fusion
  (27 shorter events, 0.5 us)
Async XLA Ops:
  7.2 78.6 %all-gather.3.cloned.1.call-start = ((), (), s32[]{:S(2)}) async-start(), calls=%async_computation.10 | async-start | bytes 4734976 | tf_op jit(solution)/shard_map/tok_gather/all_gather | solution.py:221
  8.9 152.4 %all-gather.5.cloned.1.call-start = ((), (), s32[]{:S(2)}) async-start(), calls=%async_computation.12 | async-start | bytes 4456448 | tf_op jit(solution)/shard_map/cot_gather/all_gather | solution.py:221
  13.3 76.5 %all-to-all-start.1 = ((bf16[8,704,384]{2,1,0:T(8,128)(2,1)}), bf16[8,704,384]{2,1,0:T(8,128)(2,1)}, u32[]{:S(2)}, u32[]{:S(2)}) async-start(bf16[8,704,384]{2,1,0:T(8,128)(2,1)} %broadcast_in_dim.12), calls=%async_computation.1 | async-start | bytes 8650752 | tf_op jit(solution)/shard_map/all_to_all | solution.py:229
  89.9 12.8 %all-to-all-start.3 = ((bf16[4,104,1024]{2,1,0:T(8,128)(2,1)}), bf16[4,104,1024]{2,1,0:T(8,128)(2,1)S(1)}, u32[]{:S(2)}, u32[]{:S(2)}) async-start(bf16[4,104,1024]{2,1,0:T(8,128)(2,1)} %get-tuple-element.18), calls=%async_computation.3 | async-start | bytes 1703936 | tf_op jit(solution)/shard_map/all_to_all | solution.py:207
  98.1 82.9 %copy-start.1 = (bf16[8,88,8,128]{3,2,1,0:T(8,128)(2,1)}, bf16[8,88,8,128]{3,2,1,0:T(8,128)(2,1)S(1)}, u32[]{:S(2)}) copy-start(bf16[8,88,8,128]{3,2,1,0:T(8,128)(2,1)S(1)} %get-tuple-element.23) | copy-start | bytes 4325380
  102.7 6.7 %copy-start.4 = (bf16[4,104,1024]{2,1,0:T(8,128)(2,1)}, bf16[4,104,1024]{2,1,0:T(8,128)(2,1)S(1)}, u32[]{:S(2)}) copy-start(bf16[4,104,1024]{2,1,0:T(8,128)(2,1)S(1)} %all-to-all-done.3) | copy-start | bytes 2555908
  102.7 14.2 %all-to-all-start = ((bf16[4,104,1024]{2,1,0:T(8,128)(2,1)}), bf16[4,104,1024]{2,1,0:T(8,128)(2,1)S(1)}, u32[]{:S(2)}, u32[]{:S(2)}) async-start(bf16[4,104,1024]{2,1,0:T(8,128)(2,1)} %get-tuple-element.15), calls=%async_computation | async-start | bytes 1703936 | tf_op jit(solution)/shard_map/all_to_all | solution.py:207
  107.0 2.5 copy-start.2
  109.4 1.1 copy-start.10
  110.5 0.8 copy-start.7
  116.9 6.0 %copy-start.5 = (bf16[4,104,1024]{2,1,0:T(8,128)(2,1)}, bf16[4,104,1024]{2,1,0:T(8,128)(2,1)S(1)}, u32[]{:S(2)}) copy-start(bf16[4,104,1024]{2,1,0:T(8,128)(2,1)S(1)} %all-to-all-done) | copy-start | bytes 2555908
  116.9 14.6 %all-to-all-start.4 = ((bf16[4,104,1024]{2,1,0:T(8,128)(2,1)}), bf16[4,104,1024]{2,1,0:T(8,128)(2,1)S(1)}, u32[]{:S(2)}, u32[]{:S(2)}) async-start(bf16[4,104,1024]{2,1,0:T(8,128)(2,1)} %bitcast.112), calls=%async_computation.4 | async-start | bytes 1703936 | tf_op jit(solution)/shard_map/all_to_all | solution.py:207
  120.4 2.5 copy-start.3
  122.9 1.1 copy-start.11
  124.0 0.8 copy-start.8
  131.5 0.9 copy-start.6
  132.4 14.8 %all-to-all-start.2 = ((bf16[4,104,1024]{2,1,0:T(8,128)(2,1)}), bf16[4,104,1024]{2,1,0:T(8,128)(2,1)S(1)}, u32[]{:S(2)}, u32[]{:S(2)}) async-start(bf16[4,104,1024]{2,1,0:T(8,128)(2,1)} %bitcast.12), calls=%async_computation.2 | async-start | bytes 1703936 | tf_op jit(solution)/shard_map/all_to_all | solution.py:207
  135.9 125.7 %reduce-scatter.2.cloned.1.call-start = ((), (), s32[]{:S(2)}) async-start(), calls=%async_computation.11 | async-start | bytes 4456448 | tf_op jit(solution)/shard_map/mixed_scatter/reduce_scatter | solution.py:254
  147.2 0.9 copy-start
  165.0 12.4 %all-to-all-start.5 = ((bf16[4,104,1024]{2,1,0:T(8,128)(2,1)}), bf16[4,104,1024]{2,1,0:T(8,128)(2,1)S(1)}, u32[]{:S(2)}, u32[]{:S(2)}) async-start(bf16[4,104,1024]{2,1,0:T(8,128)(2,1)} %pick_weighted.2), calls=%async_computation.6 | async-start | bytes 1703936 | tf_op jit(solution)/shard_map/all_to_all | solution.py:207
  177.5 15.3 %all-to-all-start.6 = ((bf16[4,104,1024]{2,1,0:T(8,128)(2,1)}), bf16[4,104,1024]{2,1,0:T(8,128)(2,1)S(1)}, u32[]{:S(2)}, u32[]{:S(2)}) async-start(bf16[4,104,1024]{2,1,0:T(8,128)(2,1)} %pick_weighted.3), calls=%async_computation.7 | async-start | bytes 1703936 | tf_op jit(solution)/shard_map/all_to_all | solution.py:207
  199.3 35.5 %all-to-all-start.7 = ((bf16[8,128,704]{1,2,0:T(8,128)(2,1)}), bf16[8,128,704]{1,2,0:T(8,128)(2,1)S(1)}, u32[]{:S(2)}, u32[]{:S(2)}) async-start(bf16[8,128,704]{1,2,0:T(8,128)(2,1)} %bitcast.102), calls=%async_computation.8 | async-start | bytes 2883584 | tf_op jit(solution)/shard_map/all_to_all | solution.py:269
  215.6 2.1 copy-start.9
  234.8 24.4 %all-to-all-start.8 = ((bf16[8,128,704]{1,2,0:T(8,128)(2,1)}), bf16[8,128,704]{1,2,0:T(8,128)(2,1)}, u32[]{:S(2)}, u32[]{:S(2)}) async-start(bf16[8,128,704]{1,2,0:T(8,128)(2,1)} %bitcast.103), calls=%async_computation.9 | async-start | bytes 2883584 | tf_op jit(solution)/shard_map/all_to_all | solution.py:269
Sparse Core Ops, SparseCore 0:
  10.6 75.0 all-gather.2
  87.8 73.5 all-gather.4
  164.8 76.5 reduce-scatter.1

commit v5 on v4

--- a/solution.py
+++ b/solution.py
@@ -203,6 +203,26 @@
     )(code_t, gate_t, rows, *((before,) if chained else ()))
 
 
+def split_body(core_ref, part_ref, kept_ref, sent_ref):
+    core = core_ref[0]
+    count, _, width = kept_ref.shape
+    for y in range(count):
+        kept_ref[y] = part_ref[:, pl.ds(pl.multiple_of((2 * y + core) * width, width), width)]
+        sent_ref[y] = part_ref[:, pl.ds(pl.multiple_of((2 * y + 1 - core) * width, width), width)]
+
+
+def split(core, part, count):
+    height, width = part.shape
+    shape = (count, height, width // (2 * count))
+    return pl.pallas_call(
+        split_body,
+        out_shape=[jax.ShapeDtypeStruct(shape, part.dtype)] * 2,
+        in_specs=[pl.BlockSpec(memory_space=pltpu.SMEM), pl.BlockSpec(memory_space=pltpu.VMEM)],
+        cost_estimate=pl.CostEstimate(flops=0, bytes_accessed=4 * height * width, transcendentals=0),
+        name="split",
+    )(core, part)
+
+
 def across_x(blocks):
     return lax.all_to_all(blocks, "ep", split_axis=0, concat_axis=0, axis_index_groups=XG, tiled=True)
 
@@ -231,6 +251,8 @@
         shards[:, :, n * share : (n + 1) * share].transpose(1, 0, 2).reshape(hidden_width, width)
         for n in range(3)
     )
+
+    all_tok, full_gate, full_up, full_down = tied((all_tok, full_gate, full_up, full_down))
 
     def forward(rows):
         gate_pre = lax.dot_general(rows, full_gate, last, preferred_element_type=jnp.float32)
@@ -254,23 +276,28 @@
         mixed_out = lax.psum_scatter(mixed, "ep", axis_index_groups=ZG, scatter_dimension=0, tiled=True)
 
     grads = [across_x(pick_weighted(*routes[b], all_cot, b)).reshape(NX * ROWS, width) for b in range(2)]
-    part_up = part_down = None
-    for b in range(2):
-        _, silu, hidden = outs[b]
-        down = lax.dot_general(grads[b], hidden, first, preferred_element_type=jnp.float32)
+    def summed(near, far, after=()):
+        part = (near + far).astype(jnp.bfloat16)
+        kept, sent = split((lax.axis_index("rep") % 2).reshape(1), part, n_rep // 2)
+        got = lax.ppermute(sent, "rep", [(r, r ^ 1) for r in range(n_rep)])
+        pair = (kept.astype(jnp.float32) + got.astype(jnp.float32)).astype(jnp.bfloat16)
+        sent_on, *after = tied((pair, *after))
+        groups = [list(range(c, n_rep, 2)) for c in range(2)]
+        pair = lax.all_to_all(sent_on, "rep", split_axis=0, concat_axis=0, axis_index_groups=groups, tiled=True)
+        return jnp.sum(pair.astype(jnp.float32), axis=0), sent_on, *after
+
+    def down(b):
+        return lax.dot_general(outs[b][2], grads[b], first, preferred_element_type=jnp.float32)
+
+    def up(b):
         hidden_grad = lax.dot_general(grads[b], full_down, last, preferred_element_type=jnp.float32)
-        up_grad = (hidden_grad * silu).astype(jnp.bfloat16)
-        up = lax.dot_general(picked[b], up_grad, first, preferred_element_type=jnp.float32)
-        part_down = down if b == 0 else part_down + down
-        part_up = up if b == 0 else part_up + up
-
-    def summed(part):
-        part = part.astype(jnp.bfloat16).reshape(n_rep, width // n_rep, hidden_width)
-        part = lax.all_to_all(part, "rep", split_axis=0, concat_axis=0, tiled=True)
-        return jnp.sum(part.astype(jnp.float32), axis=0)
-
-    grad_down = summed(part_down).T
-    grad_up = summed(part_up)
+        up_grad = (hidden_grad * outs[b][1]).astype(jnp.bfloat16)
+        return lax.dot_general(up_grad, picked[b], first, preferred_element_type=jnp.float32)
+
+    grad_down, sent_on = summed(down(0), down(1))
+    grads[1], _ = tied((grads[1], sent_on))
+    grad_up, _, grad_down = summed(up(0), up(1), (grad_down,))
+    grad_up = grad_up.T
     return mixed_out, grad_up[None], grad_down[None]
 
 

time: 269 us -> 271 us (level)
  waiting for transfers between devices: 125 us -> 91.2 us
  blocking collectives: 0 us -> 27.1 us
  matrix products: 23.8 us -> 32.2 us
  Pallas kernels: 31.8 us -> 36.9 us
  starting transfers between devices: 55.7 us -> 51.4 us
    all_gather x2, waiting for transfers between devices: 67.4 us -> 12.4 us  [along_z(): return lax.all_gather(rows, 'ep', axis_index_groups=ZG, axis=0, tiled=True)]
    all_to_all x1, waiting for transfers between devices: 0.01 us -> 49.5 us  [local(): lax.all_to_all(shards, 'rep', split_axis=0, concat_axis=0, tiled=True)]
    all_to_all x2 -> x0, waiting for transfers between devices: 33 us -> none  [summed(): part = lax.all_to_all(part, 'rep', split_axis=0, concat_axis=0, tiled=True)]
    all_to_all x0 -> x2, blocking collectives: none -> 27.1 us  [summed(): lax.all_to_all(sent_on, 'rep', split_axis=0, concat_axis=0, axis_index_gr...]
    all_to_all x2 -> x0, starting transfers between devices: 21.4 us -> none  [summed(): part = lax.all_to_all(part, 'rep', split_axis=0, concat_axis=0, tiled=True)]
    ppermute x0 -> x2, starting transfers between devices: none -> 16 us  [summed(): got = lax.ppermute(sent, 'rep', [(r, r ^ 1) for r in range(n_rep)])]
    pallas_call x0 -> x2, Pallas kernels: none -> 5.72 us  [split(): pl.pallas_call(split_body, out_shape=[jax.ShapeDtypeStruct(shape, part.dt...]
    dot_general x4, matrix products: 13.6 us -> 19.2 us  [the longest x2 11.4 us: up(): lax.dot_general(up_grad, picked[b], first, preferred_element_type=jnp.flo...]
  transfers between devices with their start and end apart: 12 -> 12, of which waited for: 9 -> 9; matrix products, arithmetic and copies ran while one was open for 14% -> 16% of each run, Pallas kernels for 11% -> 13%
where the time goes in v5:
time: 271 us; the launch traced here: 268 us
  waiting for transfers between devices  91.2 us (34%)
  starting transfers between devices  51.4 us (19%)
  Pallas kernels  36.9 us (14%)
  matrix products  32.2 us (12%)
  blocking collectives  27.1 us (10%)
  between operations  14 us (5%)
  local copies, waits for them, and re-layouts  10.5 us (4%)
  other arithmetic  4.56 us (2%)
    all_to_all x1, waiting for transfers between devices, local(): lax.all_to_all(shards, 'rep', split_axis=0, concat_axis=0, tiled=True)  49.5 us
    all_to_all x6, waiting for transfers between devices, across_x(): lax.all_to_all(blocks, 'ep', split_axis=0, concat_axis=0, axis_index_grou...  28.6 us
    all_to_all x2, blocking collectives, summed(): lax.all_to_all(sent_on, 'rep', split_axis=0, concat_axis=0, axis_index_gr...  27.1 us
    all_to_all x6, starting transfers between devices, across_x(): lax.all_to_all(blocks, 'ep', split_axis=0, concat_axis=0, axis_index_grou...  23.8 us
    ppermute x2, starting transfers between devices, summed(): got = lax.ppermute(sent, 'rep', [(r, r ^ 1) for r in range(n_rep)])  16 us
    pallas_call x2, Pallas kernels, mix(): pl.pallas_call(mix_body, out_shape=jax.ShapeDtypeStruct((NZ * TOK, width)...  13.9 us
    all_gather x2, waiting for transfers between devices, along_z(): return lax.all_gather(rows, 'ep', axis_index_groups=ZG, axis=0, tiled=True)  12.4 us
    dot_general x2, matrix products, up(): lax.dot_general(up_grad, picked[b], first, preferred_element_type=jnp.flo...  11.4 us
  transfers between devices with their start and end apart: 12, of which 9 were waited for; matrix products, arithmetic and copies ran while one was open for 16% of the time, Pallas kernels for 13%

profile of v5, /device:TPU:1, one launch (start us, length us, event | category | flops | bytes accessed | tf_op | source)
XLA Modules:
  0.0 267.8 jit_solution(15737013198302904993)
XLA Ops:
  7.2 1.7 pack.1
  8.9 1.2 pad_maximum_fusion
  10.1 2.4 broadcast_in_dim.12
  12.5 11.3 %all-to-all-start = ((bf16[8,704,384]{2,1,0:T(8,128)(2,1)}), bf16[8,704,384]{2,1,0:T(8,128)(2,1)}, u32[]{:S(2)}, u32[]{:S(2)}) async-start(bf16[8,704,384]{2,1,0:T(8,128)(2,1)} %broadcast_in_dim.12), calls=%async_computation | async-start | bytes 8650752 | tf_op jit(solution)/shard_map/all_to_all | solution.py:249
  24.6 49.5 %all-to-all-done = bf16[8,704,384]{2,1,0:T(8,128)(2,1)} async-done(((bf16[8,704,384]{2,1,0:T(8,128)(2,1)}), bf16[8,704,384]{2,1,0:T(8,128)(2,1)}, u32[]{:S(2)}, u32[]{:S(2)}) %all-to-all-start) | async-done | bytes 4325408 | tf_op jit(solution)/shard_map/all_to_all | solution.py:249
  74.0 2.5 slice_bitcast_fusion
  77.0 1.6 copy_bitcast_fusion
  78.5 7.3 %all-gather.3.cloned.1.call-done.all_ref = bf16[2176,1024]{1,0:T(8,128)(2,1)} async-done(((bf16[136,1024]{1,0:T(8,128)(2,1)}), bf16[2176,1024]{1,0:T(8,128)(2,1)}) %all-gather.3.cloned.1.call-update) | async-done | bytes 4456464 | tf_op jit(solution)/shard_map/tok_gather/all_gather | solution.py:241
  85.8 4.1 %pick.3 = (bf16[4,104,1024]{2,1,0:T(8,128)(2,1)}, s32[4,1024]{1,0:T(4,128)}, f32[4,1024]{1,0:T(4,128)}, f32[8,128,4]{2,1,0:T(8,128)}, f32[8,128,4]{2,1,0:T(8,128)}) custom-call(s32[1]{0:T(128)} %bitcast.place_ref, bf16[2176,1024]{1,0:T(8,128)(2,1)} %all-gather.3.cloned.1.call-done.all_ref), custom_call_target="tpu_custom_call" | custom-call | flops 872415232 | bytes 2949120 | tf_op jit(solution)/shard_map/pick/pallas_call | solution.py:116
  89.9 4.2 %all-to-all-start.3 = ((bf16[4,104,1024]{2,1,0:T(8,128)(2,1)}), bf16[4,104,1024]{2,1,0:T(8,128)(2,1)}, u32[]{:S(2)}, u32[]{:S(2)}) async-start(bf16[4,104,1024]{2,1,0:T(8,128)(2,1)} %get-tuple-element.33), calls=%async_computation.3 | async-start | bytes 1703936 | tf_op jit(solution)/shard_map/all_to_all | solution.py:227
  94.1 4.0 %pick.2 = (bf16[4,104,1024]{2,1,0:T(8,128)(2,1)}, s32[4,1024]{1,0:T(4,128)}, f32[4,1024]{1,0:T(4,128)}, f32[8,128,4]{2,1,0:T(8,128)}, f32[8,128,4]{2,1,0:T(8,128)}) custom-call(s32[1]{0:T(128)} %bitcast.place_ref, bf16[2176,1024]{1,0:T(8,128)(2,1)} %all-gather.3.cloned.1.call-done.all_ref), custom_call_target="tpu_custom_call" | custom-call | flops 872415232 | bytes 2949120 | tf_op jit(solution)/shard_map/pick/pallas_call | solution.py:116
  98.2 4.7 %all-to-all-done.3 = bf16[4,104,1024]{2,1,0:T(8,128)(2,1)} async-done(((bf16[4,104,1024]{2,1,0:T(8,128)(2,1)}), bf16[4,104,1024]{2,1,0:T(8,128)(2,1)}, u32[]{:S(2)}, u32[]{:S(2)}) %all-to-all-start.3) | async-done | bytes 852000 | tf_op jit(solution)/shard_map/all_to_all | solution.py:227
  102.9 4.2 %all-to-all-start.1 = ((bf16[4,104,1024]{2,1,0:T(8,128)(2,1)}), bf16[4,104,1024]{2,1,0:T(8,128)(2,1)}, u32[]{:S(2)}, u32[]{:S(2)}) async-start(bf16[4,104,1024]{2,1,0:T(8,128)(2,1)} %get-tuple-element.27), calls=%async_computation.1 | async-start | bytes 1703936 | tf_op jit(solution)/shard_map/all_to_all | solution.py:227
  107.1 2.1 fusion.8
  109.2 2.6 fusion.1
  111.8 0.9 copy-done.6
  112.7 1.8 convolution_convert_fusion
  114.5 2.4 all-to-all-done.1
  116.9 4.2 %all-to-all-start.4 = ((bf16[4,104,1024]{2,1,0:T(8,128)(2,1)}), bf16[4,104,1024]{2,1,0:T(8,128)(2,1)}, u32[]{:S(2)}, u32[]{:S(2)}) async-start(bf16[4,104,1024]{2,1,0:T(8,128)(2,1)} %bitcast.66), calls=%async_computation.4 | async-start | bytes 1703936 | tf_op jit(solution)/shard_map/all_to_all | solution.py:227
  121.1 2.1 fusion.7
  123.3 2.6 fusion
  125.9 1.7 convolution_convert_fusion.1
  127.7 4.5 %all-to-all-done.4.rows_ref = bf16[4,104,1024]{2,1,0:T(8,128)(2,1)} async-done(((bf16[4,104,1024]{2,1,0:T(8,128)(2,1)}), bf16[4,104,1024]{2,1,0:T(8,128)(2,1)}, u32[]{:S(2)}, u32[]{:S(2)}) %all-to-all-start.4) | async-done | bytes 852000 | tf_op jit(solution)/shard_map/all_to_all | solution.py:227
  132.1 3.5 %all-to-all-start.2 = ((bf16[4,104,1024]{2,1,0:T(8,128)(2,1)}), bf16[4,104,1024]{2,1,0:T(8,128)(2,1)S(1)}, u32[]{:S(2)}, u32[]{:S(2)}) async-start(bf16[4,104,1024]{2,1,0:T(8,128)(2,1)} %bitcast.65), calls=%async_computation.2 | async-start | bytes 1703936 | tf_op jit(solution)/shard_map/all_to_all | solution.py:227
  135.9 6.9 %mix.2.refs_0_ = bf16[2048,1024]{1,0:T(8,128)(2,1)} custom-call(f32[8,128,4]{2,1,0:T(8,128)} %get-tuple-element.31.code_ref, f32[8,128,4]{2,1,0:T(8,128)} %get-tuple-element.32.gate_ref, bf16[4,104,1024]{2,1,0:T(8,128)(2,1)} %all-to-all-done.4.rows_ref), custom_call_target="tpu_custom_call" | custom-call | flops 2147483648 | bytes 2949120 | tf_op jit(solution)/shard_map/mix/pallas_call | solution.py:185
  142.8 5.6 %all-to-all-done.2.rows_ref = bf16[4,104,1024]{2,1,0:T(8,128)(2,1)S(1)} async-done(((bf16[4,104,1024]{2,1,0:T(8,128)(2,1)}), bf16[4,104,1024]{2,1,0:T(8,128)(2,1)S(1)}, u32[]{:S(2)}, u32[]{:S(2)}) %all-to-all-start.2) | async-done | bytes 852000 | tf_op jit(solution)/shard_map/all_to_all | solution.py:227
  148.4 0.9 copy-done
  149.3 7.0 %mix.3 = bf16[2048,1024]{1,0:T(8,128)(2,1)} custom-call(f32[8,128,4]{2,1,0:T(8,128)} %get-tuple-element.25.code_ref, f32[8,128,4]{2,1,0:T(8,128)} %get-tuple-element.26.gate_ref, bf16[4,104,1024]{2,1,0:T(8,128)(2,1)} %copy-done, bf16[2048,1024]{1,0:T(8,128)(2,1)} %mix.2.refs_0_), custom_call_target="tpu_custom_call", output_to_operand_aliasing={{}: (3, {})} | custom-call | flops 2147483648 | bytes 2949120 | tf_op jit(solution)/shard_map/mix/pallas_call | solution.py:185
  156.4 5.1 %all-gather.5.cloned.1.call-done.all_ref = bf16[2048,1024]{1,0:T(8,128)(2,1)} async-done(((bf16[128,1024]{1,0:T(8,128)(2,1)}), bf16[2048,1024]{1,0:T(8,128)(2,1)}) %all-gather.5.cloned.1.call-update) | async-done | bytes 4194320 | tf_op jit(solution)/shard_map/cot_gather/all_gather | solution.py:241
  161.5 3.7 %pick_weighted.2 = bf16[4,104,1024]{2,1,0:T(8,128)(2,1)} custom-call(s32[4,1024]{1,0:T(4,128)} %get-tuple-element.34.code_ref, f32[4,1024]{1,0:T(4,128)} %get-tuple-element.35.gate_ref, bf16[2048,1024]{1,0:T(8,128)(2,1)} %all-gather.5.cloned.1.call-done.all_ref), custom_call_target="tpu_custom_call" | custom-call | flops 872415232 | bytes 2949120 | tf_op jit(solution)/shard_map/pick_weighted/pallas_call | solution.py:143
  165.2 4.2 %all-to-all-start.5 = ((bf16[4,104,1024]{2,1,0:T(8,128)(2,1)}), bf16[4,104,1024]{2,1,0:T(8,128)(2,1)S(1)}, u32[]{:S(2)}, u32[]{:S(2)}) async-start(bf16[4,104,1024]{2,1,0:T(8,128)(2,1)} %pick_weighted.2), calls=%async_computation.6 | async-start | bytes 1703936 | tf_op jit(solution)/shard_map/all_to_all | solution.py:227
  169.4 3.7 %pick_weighted.3 = bf16[4,104,1024]{2,1,0:T(8,128)(2,1)} custom-call(s32[4,1024]{1,0:T(4,128)} %get-tuple-element.36.code_ref, f32[4,1024]{1,0:T(4,128)} %get-tuple-element.37.gate_ref, bf16[2048,1024]{1,0:T(8,128)(2,1)} %all-gather.5.cloned.1.call-done.all_ref), custom_call_target="tpu_custom_call" | custom-call | flops 872415232 | bytes 2949120 | tf_op jit(solution)/shard_map/pick_weighted/pallas_call | solution.py:143
  173.1 5.0 %all-to-all-done.5 = bf16[4,104,1024]{2,1,0:T(8,128)(2,1)S(1)} async-done(((bf16[4,104,1024]{2,1,0:T(8,128)(2,1)}), bf16[4,104,1024]{2,1,0:T(8,128)(2,1)S(1)}, u32[]{:S(2)}, u32[]{:S(2)}) %all-to-all-start.5) | async-done | bytes 852000 | tf_op jit(solution)/shard_map/all_to_all | solution.py:227
  178.1 0.9 copy-done.3
  179.0 3.5 %all-to-all-start.6 = ((bf16[4,104,1024]{2,1,0:T(8,128)(2,1)}), bf16[4,104,1024]{2,1,0:T(8,128)(2,1)S(1)}, u32[]{:S(2)}, u32[]{:S(2)}) async-start(bf16[4,104,1024]{2,1,0:T(8,128)(2,1)} %pick_weighted.3), calls=%async_computation.7 | async-start | bytes 1703936 | tf_op jit(solution)/shard_map/all_to_all | solution.py:227
  182.5 3.9 %fusion.9 = f32[704,1024]{1,0:T(8,128)} fusion(bf16[416,704]{1,0:T(8,128)(2,1)} %copy-done.6, bf16[416,1024]{1,0:T(8,128)(2,1)} %bitcast.63), kind=kOutput, calls=%fused_computation.30 | convolution fusion | flops 599785472 | bytes 4321280 | tf_op jit(solution)/shard_map/dot_general | solution.py:290
  186.4 6.4 %all-to-all-done.6 = bf16[4,104,1024]{2,1,0:T(8,128)(2,1)S(1)} async-done(((bf16[4,104,1024]{2,1,0:T(8,128)(2,1)}), bf16[4,104,1024]{2,1,0:T(8,128)(2,1)S(1)}, u32[]{:S(2)}, u32[]{:S(2)}) %all-to-all-start.6) | async-done | bytes 852000 | tf_op jit(solution)/shard_map/all_to_all | solution.py:227
  192.8 3.9 %add_convert_fusion.1.part_ref = bf16[704,1024]{1,0:T(8,128)(2,1)} fusion(f32[704,1024]{1,0:T(8,128)} %fusion.9, bf16[416,704]{1,0:T(8,128)(2,1)S(1)} %fusion, bf16[416,1024]{1,0:T(8,128)(2,1)S(1)} %bitcast.59), kind=kOutput, calls=%fused_computation.1 | convolution fusion | flops 601227264 | bytes 5763072 | tf_op jit(solution)/shard_map/dot_general | solution.py:290
  196.7 2.9 %split.2 = (bf16[4,704,128]{2,1,0:T(8,128)(2,1)}, bf16[4,704,128]{2,1,0:T(8,128)(2,1)}) custom-call(s32[1]{0:T(128)} %bitcast.15.core_ref, bf16[704,1024]{1,0:T(8,128)(2,1)} %add_convert_fusion.1.part_ref), custom_call_target="tpu_custom_call" | custom-call | bytes 2883584 | tf_op jit(solution)/shard_map/split/pallas_call | solution.py:217
  199.5 14.0 %collective-permute-start = (bf16[4,704,128]{2,1,0:T(8,128)(2,1)}, bf16[4,704,128]{2,1,0:T(8,128)(2,1)S(1)}, u32[]{:S(2)}, u32[]{:S(2)}) collective-permute-start(bf16[4,704,128]{2,1,0:T(8,128)(2,1)} %get-tuple-element.39), channel_id=1, source_target_pairs={{0,1},{1,0},{2,3},{3,2},{4,5},{5,4},{6,7},{7,6},{8,9},{9,8},{10,11... | collective-permute-start | bytes 2162696 | tf_op jit(solution)/shard_map/ppermute | solution.py:282
  213.5 5.6 %fusion.4 = f32[704,1024]{1,0:T(8,128)} fusion(bf16[416,1024]{1,0:T(8,128)(2,1)} %bitcast.13, bf16[416,1024]{1,0:T(8,128)(2,1)} %bitcast.64, bf16[704,1024]{1,0:T(8,128)(2,1)S(1)} %get-tuple-element.30, f32[416,704]{1,0:T(8,128)} %copy-done.7), kind=kOutput, calls=%fused_computation.24 | convolution fusion | flops 1201328128 | bytes 7200768 | tf_op jit(solution)/shard_map/dot_general | solution.py:295
  219.1 0.9 copy-done.5
  220.0 1.5 add_convert_fusion.3
  221.5 5.8 %add_convert_fusion.part_ref = bf16[704,1024]{1,0:T(8,128)(2,1)} fusion(f32[704,1024]{1,0:T(8,128)} %fusion.4, bf16[416,1024]{1,0:T(8,128)(2,1)} %bitcast.11, bf16[416,1024]{1,0:T(8,128)(2,1)S(1)} %bitcast.60, bf16[704,1024]{1,0:T(8,128)(2,1)S(1)} %get-tuple-element.30, f32[416,704]{1,0:T(8,128)} %copy-done.8), kind=kOutput, calls=%fused_computation | convolution fusion | flops 1202769920 | bytes 8642560 | tf_op jit(solution)/shard_map/dot_general | solution.py:295
  227.4 2.9 %split.3 = (bf16[4,704,128]{2,1,0:T(8,128)(2,1)}, bf16[4,704,128]{2,1,0:T(8,128)(2,1)}) custom-call(s32[1]{0:T(128)} %bitcast.15.core_ref, bf16[704,1024]{1,0:T(8,128)(2,1)} %add_convert_fusion.part_ref), custom_call_target="tpu_custom_call" | custom-call | bytes 2883584 | tf_op jit(solution)/shard_map/split/pallas_call | solution.py:217
  230.2 2.1 collective-permute-start.1
  232.3 14.7 %all_to_all.45 = bf16[4,704,128]{2,1,0:T(8,128)(2,1)S(1)} all-to-all(bf16[4,704,128]{2,1,0:T(8,128)(2,1)S(1)} %add_convert_fusion.3), channel_id=1, replica_groups={{0,2,4,6},{1,3,5,7},{8,10,12,14},{9,11,13,15},{16,18,20,22},{17,19,21,2..., dimensions={0} | all-to-all | bytes 1441792 | tf_op jit(solution)/shard_map/all_to_all | solution.py:286
  248.0 12.4 %all_to_all.46 = bf16[4,704,128]{2,1,0:T(8,128)(2,1)S(1)} all-to-all(bf16[4,704,128]{2,1,0:T(8,128)(2,1)S(1)} %add_convert_fusion.2), channel_id=1, replica_groups={{0,2,4,6},{1,3,5,7},{8,10,12,14},{9,11,13,15},{16,18,20,22},{17,19,21,2..., dimensions={0} | all-to-all | bytes 1441792 | tf_op jit(solution)/shard_map/all_to_all | solution.py:286
  (27 shorter events, 3.3 us)
Async XLA Ops:
  7.2 78.6 %all-gather.3.cloned.1.call-start = ((), (), s32[]{:S(2)}) async-start(), calls=%async_computation.10 | async-start | bytes 4734976 | tf_op jit(solution)/shard_map/tok_gather/all_gather | solution.py:241
  12.5 61.5 %all-to-all-start = ((bf16[8,704,384]{2,1,0:T(8,128)(2,1)}), bf16[8,704,384]{2,1,0:T(8,128)(2,1)}, u32[]{:S(2)}, u32[]{:S(2)}) async-start(bf16[8,704,384]{2,1,0:T(8,128)(2,1)} %broadcast_in_dim.12), calls=%async_computation | async-start | bytes 8650752 | tf_op jit(solution)/shard_map/all_to_all | solution.py:249
  23.8 137.7 %all-gather.5.cloned.1.call-start = ((), (), s32[]{:S(2)}) async-start(), calls=%async_computation.12 | async-start | bytes 4456448 | tf_op jit(solution)/shard_map/cot_gather/all_gather | solution.py:241
  89.9 13.0 %all-to-all-start.3 = ((bf16[4,104,1024]{2,1,0:T(8,128)(2,1)}), bf16[4,104,1024]{2,1,0:T(8,128)(2,1)}, u32[]{:S(2)}, u32[]{:S(2)}) async-start(bf16[4,104,1024]{2,1,0:T(8,128)(2,1)} %get-tuple-element.33), calls=%async_computation.3 | async-start | bytes 1703936 | tf_op jit(solution)/shard_map/all_to_all | solution.py:227
  102.9 14.1 %all-to-all-start.1 = ((bf16[4,104,1024]{2,1,0:T(8,128)(2,1)}), bf16[4,104,1024]{2,1,0:T(8,128)(2,1)}, u32[]{:S(2)}, u32[]{:S(2)}) async-start(bf16[4,104,1024]{2,1,0:T(8,128)(2,1)} %get-tuple-element.27), calls=%async_computation.1 | async-start | bytes 1703936 | tf_op jit(solution)/shard_map/all_to_all | solution.py:227
  107.1 2.1 copy-start.1
  109.2 2.6 copy-start.7
  111.8 0.9 copy-start.6
  116.9 15.2 %all-to-all-start.4 = ((bf16[4,104,1024]{2,1,0:T(8,128)(2,1)}), bf16[4,104,1024]{2,1,0:T(8,128)(2,1)}, u32[]{:S(2)}, u32[]{:S(2)}) async-start(bf16[4,104,1024]{2,1,0:T(8,128)(2,1)} %bitcast.66), calls=%async_computation.4 | async-start | bytes 1703936 | tf_op jit(solution)/shard_map/all_to_all | solution.py:227
  121.1 2.2 copy-start.2
  123.3 2.6 copy-start.8
  132.1 16.3 %all-to-all-start.2 = ((bf16[4,104,1024]{2,1,0:T(8,128)(2,1)}), bf16[4,104,1024]{2,1,0:T(8,128)(2,1)S(1)}, u32[]{:S(2)}, u32[]{:S(2)}) async-start(bf16[4,104,1024]{2,1,0:T(8,128)(2,1)} %bitcast.65), calls=%async_computation.2 | async-start | bytes 1703936 | tf_op jit(solution)/shard_map/all_to_all | solution.py:227
  135.6 125.7 %reduce-scatter.2.cloned.1.call-start = ((), (), s32[]{:S(2)}) async-start(), calls=%async_computation.11 | async-start | bytes 4456448 | tf_op jit(solution)/shard_map/mixed_scatter/reduce_scatter | solution.py:276
  148.4 0.9 copy-start
  165.2 12.9 %all-to-all-start.5 = ((bf16[4,104,1024]{2,1,0:T(8,128)(2,1)}), bf16[4,104,1024]{2,1,0:T(8,128)(2,1)S(1)}, u32[]{:S(2)}, u32[]{:S(2)}) async-start(bf16[4,104,1024]{2,1,0:T(8,128)(2,1)} %pick_weighted.2), calls=%async_computation.6 | async-start | bytes 1703936 | tf_op jit(solution)/shard_map/all_to_all | solution.py:227
  178.1 0.9 copy-start.3
  179.0 13.8 %all-to-all-start.6 = ((bf16[4,104,1024]{2,1,0:T(8,128)(2,1)}), bf16[4,104,1024]{2,1,0:T(8,128)(2,1)S(1)}, u32[]{:S(2)}, u32[]{:S(2)}) async-start(bf16[4,104,1024]{2,1,0:T(8,128)(2,1)} %pick_weighted.3), calls=%async_computation.7 | async-start | bytes 1703936 | tf_op jit(solution)/shard_map/all_to_all | solution.py:227
  199.5 19.6 %collective-permute-start = (bf16[4,704,128]{2,1,0:T(8,128)(2,1)}, bf16[4,704,128]{2,1,0:T(8,128)(2,1)S(1)}, u32[]{:S(2)}, u32[]{:S(2)}) collective-permute-start(bf16[4,704,128]{2,1,0:T(8,128)(2,1)} %get-tuple-element.39), channel_id=1, source_target_pairs={{0,1},{1,0},{2,3},{3,2},{4,5},{5,4},{6,7},{7,6},{8,9},{9,8},{10,11... | collective-permute-start | bytes 2162696 | tf_op jit(solution)/shard_map/ppermute | solution.py:282
  219.1 0.9 copy-start.5
  230.2 17.6 %copy-start.4 = (bf16[4,704,128]{2,1,0:T(8,128)(2,1)S(1)}, bf16[4,704,128]{2,1,0:T(8,128)(2,1)}, u32[]{:S(2)}) copy-start(bf16[4,704,128]{2,1,0:T(8,128)(2,1)} %get-tuple-element.41) | copy-start | bytes 2162692
  230.2 17.6 %collective-permute-start.1 = (bf16[4,704,128]{2,1,0:T(8,128)(2,1)}, bf16[4,704,128]{2,1,0:T(8,128)(2,1)S(1)}, u32[]{:S(2)}, u32[]{:S(2)}) collective-permute-start(bf16[4,704,128]{2,1,0:T(8,128)(2,1)} %get-tuple-element.42), channel_id=1, source_target_pairs={{0,1},{1,0},{2,3},{3,2},{4,5},{5,4},{6,7},{7,6},{8,9},{9,8},{10,11... | collective-permute-start | bytes 2162696 | tf_op jit(solution)/shard_map/ppermute | solution.py:282
Sparse Core Ops, SparseCore 0:
  10.6 75.1 all-gather.2
  87.9 73.5 all-gather.4
  164.9 77.1 reduce-scatter.1
